TPU v7x, 256 devices: a whole 4x4x8 slice. The times are simulated.
256 devices in a mesh: enc: 32 (over z, x), tp: 8 (over y, core).
Axes of the slice: x: 4, y: 4, z: 8, core: 2. Of those that a mesh axis runs over, the one named last changes fastest.
Arguments:
- grad_rows: bfloat16 [20480, 8192], P('enc', 'tp'), may hold values from -6 to 6
- features: bfloat16 [20480, 1280], P('enc'), may hold values from -6 to 6
- block_in: bfloat16 [20480, 1280], P('enc', 'tp'), may hold values from -6 to 6
- patch_counts: int32 [32, 5], replicated, may hold values from 32 to 128, as said below
- owner: int32 [32, 5], replicated, may hold values from 0 to 31, as said below
- ln1_gain: float32 [1280], replicated, may hold values from 0.5 to 1.5
- w_qkv: bfloat16 [1280, 16, 240], P(None, 'tp')
- w_out: bfloat16 [1280, 1280], P('tp'), may hold values from -0.15625 to 0.15625
- w_proj: bfloat16 [1280, 8192], P(None, 'tp'), may hold values from -0.15625 to 0.15625
Outputs:
- grad_input: bfloat16 [20480, 1280], P('enc', 'tp')
- grad_proj: float32 [1280, 8192], P('enc', 'tp')
- grad_qkv: float32 [1280, 16, 240], P('enc', 'tp')
- grad_out: float32 [1280, 1280], P('tp', 'enc')
- grad_ln1: float32 [1280], P('enc')
Inputs may be any that keep to these rules, and one draw needn't show every extreme that they name: `patch_counts`: some image has exactly 128 live rows and some exactly 32. `owner`: each encoder device receives exactly 5 images, never two from the same block.
All inputs are finite; a program needn't handle non-finite values.
Results may differ from a plain program's by a relative error of at most 0.033.
Values may be sent and summed in bfloat16 or wider, within the bound.
No kernel may reach another device: no remote copies, remote signals or barrier semaphores. Data moves between devices by JAX's collectives and lax.ppermute only.
A program may use at most 64 MiB of HBM per device.

v0:
```python
import jax
import jax.numpy as jnp
from jax import lax
from jax.experimental import pallas as pl
from jax.experimental.pallas import tpu as pltpu
from jax.sharding import Mesh
from jax.sharding import PartitionSpec as P


TILE = 128
IMG = 5
ROWS = IMG * TILE
WIDTH = 1280
HEAD = 80
LANE = 128
PEERS = 32
ENC = ("z", "x")
TP = ("y", "c")
EPSILON = 1e-05
SCALING = 1.0 / HEAD**0.5
BF = jnp.bfloat16
F32 = jnp.float32
SWAP = ((0, 1), (1, 0))


def exchanged(blocks, axis):
    return lax.all_to_all(blocks, axis, split_axis=0, concat_axis=0, tiled=True)


def shifted(values, axis, by):
    pairs = tuple((i, (i + by) % 4) for i in range(4))
    return lax.ppermute(values, axis, pairs)


def swapped(values):
    return lax.ppermute(values, "c", SWAP)


def dot(left, right, dim_left, dim_right):
    return lax.dot_general(
        left, right, (((dim_left,), (dim_right,)), ((), ())), preferred_element_type=F32
    )


def smem():
    return pl.BlockSpec(memory_space=pltpu.SMEM)


def normalize(values):
    centred = values - jnp.mean(values, axis=-1, keepdims=True)
    variance = jnp.mean(centred * centred, axis=-1, keepdims=True)
    inverse = lax.rsqrt(variance + EPSILON)
    return (centred * inverse, inverse)


def shifted_sum(pieces, lanes):
    total = None
    for at, piece in enumerate(pieces):
        wide = jnp.concatenate(
            [piece, jnp.zeros((piece.shape[0], lanes - LANE), piece.dtype)], axis=1
        )
        if at:
            wide = pltpu.roll(wide, HEAD * at, 1)
        total = wide if total is None else total + wide
    return total


def spread_kernel(place_ref, counts_ref, arrived_ref, out_ref):
    first_row = place_ref[0] * 16
    for image in range(IMG):
        rows = arrived_ref[0, image].astype(F32)
        for peer in range(1, 4):
            rows = rows + arrived_ref[peer, image].astype(F32)
        line = first_row + lax.broadcasted_iota(jnp.int32, rows.shape, 0)
        rows = jnp.where(line < counts_ref[image], rows, 0.0).astype(BF)
        for half in range(2):
            for group in range(10):
                out_ref[half * 10 + group, image] = rows[
                    half * 8 : half * 8 + 8, group * LANE : (group + 1) * LANE
                ]
    out_ref[20:32] = jnp.zeros((12, IMG, 8, LANE), BF)


def spread(place, counts, arrived):
    return pl.pallas_call(
        spread_kernel,
        out_shape=jax.ShapeDtypeStruct((PEERS, IMG, 8, LANE), BF),
        in_specs=[smem(), smem(), pl.BlockSpec(memory_space=pltpu.VMEM)],
        out_specs=pl.BlockSpec(memory_space=pltpu.VMEM),
        name="spread",
    )(place, counts, arrived)


def forward_kernel(index_ref, pieces_ref, out_ref):
    def step(at, carry):
        out_ref[at] = pieces_ref[index_ref[at]]
        return carry

    lax.fori_loop(0, PEERS * IMG, step, 0, unroll=8)


def forwarded(index, pieces):
    flat = pieces.reshape(PEERS * IMG, 8, LANE)
    return pl.pallas_call(
        forward_kernel,
        out_shape=jax.ShapeDtypeStruct(flat.shape, BF),
        in_specs=[smem(), pl.BlockSpec(memory_space=pltpu.VMEM)],
        out_specs=pl.BlockSpec(memory_space=pltpu.VMEM),
        name="forwarded",
    )(index, flat).reshape(pieces.shape)


def collect_kernel(pieces_ref, rows_ref, copies_ref):
    for image in range(IMG):
        for half in range(2):
            for group in range(10):
                piece = pieces_ref[half * 10 + group, image]
                at = (slice(half * 8, half * 8 + 8), slice(group * LANE, (group + 1) * LANE))
                rows_ref[image, at[0], at[1]] = piece
                for peer in range(4):
                    copies_ref[peer, image, at[0], at[1]] = piece


def collected(pieces):
    return pl.pallas_call(
        collect_kernel,
        out_shape=(
            jax.ShapeDtypeStruct((IMG, 16, WIDTH), BF),
            jax.ShapeDtypeStruct((4, IMG, 16, WIDTH), BF),
        ),
        in_specs=[pl.BlockSpec(memory_space=pltpu.VMEM)],
        out_specs=(pl.BlockSpec(memory_space=pltpu.VMEM),) * 2,
        name="collected",
    )(pieces)


def attention_kernel(
    words_ref,
    counts_ref,
    own_ref,
    other_ref,
    gain_ref,
    w_ref,
    normed_in_ref,
    normed_ref,
    rows_ref,
    packed_ref,
    prob_ref,
    mixed_ref,
    scratch,
):
    first = words_ref[0] == 0
    shares = []
    for near in range(4):
        at = lax.rem(words_ref[2] + 4 - near, 4)
        own, other = own_ref[at], other_ref[at]
        shares += [jnp.where(first, own, other), jnp.where(first, other, own)]
    values = jnp.concatenate(shares, axis=0).astype(F32).T
    scratch[...] = values
    rows_ref[0] = scratch[pl.ds(pl.multiple_of(words_ref[1] * 16, 16), 16), :].astype(BF)
    normed, _ = normalize(values)
    normed_ref[...] = normed.astype(BF)
    normed_in = (normed * gain_ref[...]).astype(BF)
    normed_in_ref[...] = normed_in
    packed = dot(normed_in, w_ref[...], 1, 1).astype(BF)
    packed_ref[...] = packed
    count = counts_ref[pl.program_id(0)]
    live_row = lax.broadcasted_iota(jnp.int32, (TILE, TILE), 0) < count
    live_col = lax.broadcasted_iota(jnp.int32, (TILE, TILE), 1) < count
    same_kind = (live_row & live_col) | (~live_row & ~live_col)
    mixed = []
    for head in range(2):
        query, key, value = (
            packed[:, (head * 3 + i) * LANE : (head * 3 + i + 1) * LANE] for i in range(3)
        )
        scores = jnp.where(same_kind, dot(query, key, 1, 1) * SCALING, -1e30)
        exp_terms = jnp.exp(scores - jnp.max(scores, axis=-1, keepdims=True))
        probability = exp_terms / jnp.sum(exp_terms, axis=-1, keepdims=True)
        prob_ref[0, head] = probability
        mixed.append(dot(probability.astype(BF), value, 1, 0))
    mixed_ref[...] = shifted_sum(mixed, 256)[:, :160].astype(BF)


def attention(words, counts, own, other, gain, w_pad):
    share = pl.BlockSpec((4, 160, TILE), lambda i: (0, 0, i))
    rows = pl.BlockSpec((TILE, WIDTH), lambda i: (i, 0))
    return pl.pallas_call(
        attention_kernel,
        grid=(IMG,),
        out_shape=(
            jax.ShapeDtypeStruct((ROWS, WIDTH), BF),
            jax.ShapeDtypeStruct((ROWS, WIDTH), BF),
            jax.ShapeDtypeStruct((IMG, 16, WIDTH), BF),
            jax.ShapeDtypeStruct((ROWS, 6 * LANE), BF),
            jax.ShapeDtypeStruct((IMG, 2, TILE, TILE), F32),
            jax.ShapeDtypeStruct((ROWS, 2 * HEAD), BF),
        ),
        in_specs=[
            smem(),
            smem(),
            share,
            share,
            pl.BlockSpec((1, WIDTH), lambda i: (0, 0)),
            pl.BlockSpec((6 * LANE, WIDTH), lambda i: (0, 0)),
        ],
        out_specs=(
            rows,
            rows,
            pl.BlockSpec((1, 16, WIDTH), lambda i: (i, 0, 0)),
            pl.BlockSpec((TILE, 6 * LANE), lambda i: (i, 0)),
            pl.BlockSpec((1, 2, TILE, TILE), lambda i: (i, 0, 0, 0)),
            pl.BlockSpec((TILE, 2 * HEAD), lambda i: (i, 0)),
        ),
        scratch_shapes=[pltpu.VMEM((TILE, WIDTH), F32)],
        cost_estimate=pl.CostEstimate(
            flops=10_000_000_000, bytes_accessed=10_000_000, transcendentals=0
        ),
        name="attention",
    )(words, counts, own, other, gain, w_pad)


def backward_kernel(
    words_ref,
    own_ref,
    other_ref,
    wout_ref,
    w_ref,
    packed_ref,
    prob_ref,
    normed_ref,
    upstream_ref,
    packed_grad_ref,
    in_own_ref,
    in_other_ref,
    gain_term,
):
    step = pl.program_id(0)

    @pl.when(step == 0)
    def _():
        gain_term[...] = jnp.zeros_like(gain_term)

    @pl.when(step < IMG)
    def _():
        first = words_ref[0] == 0
        own = own_ref[...].reshape(64, WIDTH)
        other = other_ref[...].reshape(64, WIDTH)
        upstream = jnp.concatenate(
            [jnp.where(first, own, other), jnp.where(first, other, own)], axis=0
        )
        upstream_ref[...] = upstream
        mixed_grads = dot(upstream, wout_ref[...], 1, 1).astype(BF)
        pieces = []
        for head in range(2):
            query, key, value = (
                packed_ref[:, (head * 3 + i) * LANE : (head * 3 + i + 1) * LANE]
                for i in range(3)
            )
            probability = prob_ref[0, head]
            mixed_grad = mixed_grads[:, head * LANE : (head + 1) * LANE]
            prob_grad = dot(mixed_grad, value, 1, 1)
            inner = jnp.sum(probability * prob_grad, axis=-1, keepdims=True)
            score_grad = (probability * (prob_grad - inner) * SCALING).astype(BF)
            pieces.append(dot(score_grad, key, 1, 0))
            pieces.append(dot(score_grad, query, 0, 0))
            pieces.append(dot(probability.astype(BF), mixed_grad, 0, 0))
        packed_grad_ref[...] = shifted_sum(pieces, 512)[:, :480].astype(BF)
        wide = jnp.concatenate([piece.astype(BF) for piece in pieces], axis=1)
        in_part = dot(wide, w_ref[...], 1, 0).astype(BF)
        gain_term[...] += jnp.sum(
            in_part.astype(F32) * normed_ref[...].astype(F32), axis=0, keepdims=True
        )
        low, high = in_part[:64], in_part[64:]
        in_own_ref[...] = jnp.where(first, low, high).reshape(4, 1, 16, WIDTH)
        in_other_ref[...] = jnp.where(first, high, low).reshape(4, 1, 16, WIDTH)

    @pl.when(step == IMG)
    def _():
        row = lax.broadcasted_iota(jnp.int32, (16, WIDTH), 0)
        plane = jnp.where(row == 0, gain_term[...], 0.0).astype(BF)
        for peer in range(4):
            in_own_ref[peer, 0] = plane
            in_other_ref[peer, 0] = plane


def backward(words, own, other, wout_pad, w_pad, packed, prob, normed):
    def image(i):
        return jnp.minimum(i, IMG - 1)

    quarter = pl.BlockSpec((4, 1, 16, WIDTH), lambda i: (0, image(i), 0, 0))
    plane = pl.BlockSpec((4, 1, 16, WIDTH), lambda i: (0, i, 0, 0))
    rows = pl.BlockSpec((TILE, WIDTH), lambda i: (image(i), 0))
    return pl.pallas_call(
        backward_kernel,
        grid=(IMG + 1,),
        out_shape=(
            jax.ShapeDtypeStruct((ROWS, WIDTH), BF),
            jax.ShapeDtypeStruct((ROWS, 6 * HEAD), BF),
            jax.ShapeDtypeStruct((4, IMG + 1, 16, WIDTH), BF),
            jax.ShapeDtypeStruct((4, IMG + 1, 16, WIDTH), BF),
        ),
        in_specs=[
            smem(),
            quarter,
            quarter,
            pl.BlockSpec((2 * LANE, WIDTH), lambda i: (0, 0)),
            pl.BlockSpec((6 * LANE, WIDTH), lambda i: (0, 0)),
            pl.BlockSpec((TILE, 6 * LANE), lambda i: (image(i), 0)),
            pl.BlockSpec((1, 2, TILE, TILE), lambda i: (image(i), 0, 0, 0)),
            rows,
        ],
        out_specs=(
            rows,
            pl.BlockSpec((TILE, 6 * HEAD), lambda i: (image(i), 0)),
            plane,
            plane,
        ),
        scratch_shapes=[pltpu.VMEM((1, WIDTH), F32)],
        cost_estimate=pl.CostEstimate(
            flops=10_000_000_000, bytes_accessed=10_000_000, transcendentals=0
        ),
        name="backward",
    )(words, own, other, wout_pad, w_pad, packed, prob, normed)


def weights_kernel(normed_ref, upstream_ref, packed_grad_ref, mixed_ref, out_ref):
    qkv = dot(normed_ref[...], packed_grad_ref[...], 0, 0)
    out = dot(upstream_ref[...], mixed_ref[...], 0, 0)
    out_ref[...] = jnp.concatenate([qkv, out], axis=1).astype(BF)


def weight_terms(normed, upstream, packed_grad, mixed):
    return pl.pallas_call(
        weights_kernel,
        grid=(2,),
        out_shape=jax.ShapeDtypeStruct((WIDTH, 640), BF),
        in_specs=[
            pl.BlockSpec((ROWS, 640), lambda i: (0, i)),
            pl.BlockSpec((ROWS, 640), lambda i: (0, i)),
            pl.BlockSpec((ROWS, 6 * HEAD), lambda i: (0, 0)),
            pl.BlockSpec((ROWS, 2 * HEAD), lambda i: (0, 0)),
        ],
        out_specs=pl.BlockSpec((640, 640), lambda i: (i, 0)),
        cost_estimate=pl.CostEstimate(
            flops=4_000_000_000, bytes_accessed=6_000_000, transcendentals=0
        ),
        name="weight_terms",
    )(normed, upstream, packed_grad, mixed)


def norm_back_kernel(arrived_ref, block_ref, upstream_ref, gain_ref, out_ref, term_ref):
    gain = gain_ref[...]
    results = []
    for image in range(IMG + 1):
        incoming = arrived_ref[0, image].astype(F32)
        for peer in range(1, 4):
            incoming = incoming + arrived_ref[peer, image].astype(F32)
        if image == IMG:
            term_ref[...] = incoming[:8]
            continue
        normed, inverse = normalize(block_ref[image].astype(F32))
        scaled = incoming * gain
        inner = jnp.mean(scaled * normed, axis=-1, keepdims=True)
        outgoing = inverse * (scaled - jnp.mean(scaled, axis=-1, keepdims=True) - normed * inner)
        results.append(upstream_ref[image].astype(F32) + outgoing)
    grads = jnp.concatenate(results, axis=0)
    for share in range(8):
        start = share * 160 // LANE * LANE
        offset = share * 160 - start
        lanes = min(256 if offset + 160 <= 256 else 384, WIDTH - start)
        window = grads[:, start : start + lanes]
        if offset:
            window = pltpu.roll(window, lanes - offset, 1)
        out_ref[share] = window[:, :160].astype(BF)


def norm_back(arrived, block_rows, upstream_rows, gain):
    return pl.pallas_call(
        norm_back_kernel,
        out_shape=(
            jax.ShapeDtypeStruct((8, 80, 160), BF),
            jax.ShapeDtypeStruct((8, WIDTH), F32),
        ),
        in_specs=[pl.BlockSpec(memory_space=pltpu.VMEM)] * 4,
        out_specs=(pl.BlockSpec(memory_space=pltpu.VMEM),) * 2,
        name="norm_back",
    )(arrived, block_rows, upstream_rows, gain)


def summed(blocks):
    return blocks.astype(F32).sum(axis=0)


def after(value, *earlier):
    return lax.optimization_barrier((value, *earlier))[0]


def near_sum(term, columns):
    blocks = term.reshape(8, 4, -1, columns)
    here = lax.axis_index("x")

    def rows_of(at):
        return lax.dynamic_index_in_dim(blocks, lax.rem(here + at, 4), 1, keepdims=False)

    got = [shifted(rows_of(at), "x", at) for at in (2, 1, 3)]
    own = rows_of(0)
    total = own.astype(F32)
    for rows in got:
        total = total + rows.astype(F32)
    return total.astype(BF)


def shards(grad_rows, features, block_in, patch_counts, owner, ln1_gain, w_qkv, w_out, w_proj):
    device = lax.axis_index(ENC)
    core = lax.axis_index("c")
    place = core * 4 + lax.axis_index("y")
    words = jnp.stack([core, place, lax.axis_index("y")]).astype(jnp.int32)
    place_word = place.reshape(1).astype(jnp.int32)
    gain = ln1_gain.reshape(1, WIDTH)
    columns = grad_rows.shape[1]

    own_counts = lax.dynamic_index_in_dim(patch_counts, device, 0, keepdims=False)
    images = jnp.arange(PEERS * IMG, dtype=jnp.int32)
    block_of = images // IMG
    owners = owner.reshape(-1)
    ahead = (owners[:, None] == owners[None, :]) & (block_of[None, :] < block_of[:, None])
    target = owners * IMG + jnp.sum(ahead.astype(jnp.int32), axis=1)
    hits = target[None, :] == images[:, None]
    source_of = jnp.sum(jnp.where(hits, images[None, :], 0), axis=1)
    all_counts = jnp.sum(jnp.where(hits, patch_counts.reshape(1, -1), 0), axis=1)
    arrived_counts = lax.dynamic_slice_in_dim(all_counts, device * IMG, IMG, 0)

    by_place = grad_rows.reshape(IMG, 2, 4, 16, -1).transpose(1, 2, 0, 3, 4)
    by_place = by_place.reshape(2, ROWS // 2, -1)
    for_other = lax.dynamic_index_in_dim(by_place, 1 - core, 0, keepdims=False)
    for_own = lax.dynamic_index_in_dim(by_place, core, 0, keepdims=False)
    part_other = dot(for_other, w_proj, 1, 1).astype(BF)
    from_other = swapped(part_other)
    part_own = dot(for_own, w_proj, 1, 1)
    pair = (part_own + from_other.astype(F32)).astype(BF)
    features = after(features, pair)
    arrived = exchanged(pair.reshape(4, 80, WIDTH), "y").reshape(4, IMG, 16, WIDTH)

    line = jnp.arange(TILE, dtype=jnp.int32)
    live_own = (line[None, :] < own_counts[:, None]).reshape(-1)
    kept_rows = jnp.where(live_own[:, None], features, jnp.zeros_like(features))
    proj_term = dot(kept_rows, grad_rows, 0, 0).astype(BF)
    arrived = after(arrived, proj_term)
    pieces = spread(place_word, own_counts, arrived)
    proj_near = near_sum(proj_term, columns)

    share = after(block_in.T, arrived)
    block_own = jnp.stack([share] + [shifted(share, "y", at) for at in (1, 2, 3)])
    block_other = swapped(block_own)

    w_pad = jnp.pad(w_qkv.transpose(1, 2, 0).reshape(6, HEAD, WIDTH), ((0, 0), (0, 48), (0, 0)))
    w_pad = w_pad.reshape(6 * LANE, WIDTH)
    wout_pad = jnp.pad(w_out.reshape(2, HEAD, WIDTH), ((0, 0), (0, 48), (0, 0)))
    wout_pad = wout_pad.reshape(2 * LANE, WIDTH)
    normed_in, normed, block_rows, packed, prob, mixed = attention(
        words, arrived_counts, block_own, block_other, gain, w_pad
    )

    passing = exchanged(pieces, ENC)
    passing = forwarded(source_of, passing)
    landed = after(exchanged(passing, ENC), proj_near, prob)
    upstream_rows, copies = collected(landed)
    half_own = exchanged(copies.reshape(4, 80, WIDTH), "y").reshape(4, IMG, 16, WIDTH)
    half_other = swapped(half_own)

    proj_far = exchanged(after(proj_near, half_own), "z")

    upstream, packed_grad, in_own, in_other = backward(
        words, half_own, half_other, wout_pad, w_pad, packed, prob, normed
    )
    in_got = swapped(in_other)
    terms = weight_terms(normed_in, upstream, packed_grad, mixed)
    in_pair = (in_own.astype(F32) + in_got.astype(F32)).astype(BF)
    in_pair, proj_far = lax.optimization_barrier((in_pair, proj_far))
    grad_proj = summed(proj_far)
    in_arrived = exchanged(in_pair.reshape(4, 96, WIDTH), "y").reshape(4, IMG + 1, 16, WIDTH)
    term_near = near_sum(terms, 640)
    shares, gain_term = norm_back(in_arrived, block_rows, upstream_rows, gain)
    shares = exchanged(shares, TP)
    grad_input = shares.reshape(4, 2, IMG, 16, 160).transpose(2, 1, 0, 3, 4)
    grad_input = grad_input.reshape(ROWS, 160)
    gain_near = near_sum(gain_term[0].astype(BF).reshape(PEERS * 40, 1), 1)
    last = jnp.concatenate([term_near, jnp.pad(gain_near, ((0, 0), (0, 0), (0, 127)))], axis=2)
    last = summed(exchanged(last, "z"))
    grad_qkv = last[:, :480].reshape(40, 2, 240)
    grad_out = last[:, 480:640].T
    grad_ln1 = last[:, 640]
    return (grad_input, grad_proj, grad_qkv, grad_out, grad_ln1)


def solution(mesh):
    torus = Mesh(mesh.devices.reshape(8, 4, 4, 2), ("z", "x", "y", "c"))

    return jax.shard_map(
        shards,
        mesh=torus,
        in_specs=(
            P(ENC, TP),
            P(ENC, None),
            P(ENC, TP),
            P(),
            P(),
            P(),
            P(None, TP, None),
            P(TP, None),
            P(None, TP),
        ),
        out_specs=(P(ENC, TP), P(ENC, TP), P(ENC, TP, None), P(TP, ENC), P(ENC)),
        check_vma=False,
    )
```

profile of v0, /device:TPU:8, one launch (start us, length us, event | category | flops | bytes accessed | tf_op | source)
XLA Modules:
  0.0 232.9 jit_solution(7781892592706270783)
XLA Ops:
  3.4 3.0 %convolution_convert_fusion.1 = bf16[320,1280]{1,0:T(8,128)(2,1)} fusion(bf16[1280,1024]{1,0:T(8,128)(2,1)S(1)} %copy-done, bf16[2,320,1024]{2,1,0:T(8,128)(2,1)} %bitcast.88, s32[]{:T(128)S(6)} %select_n.65), kind=kOutput, calls=%fused_computation.1 | convolution fusion | flops 839270400 | bytes 4096004 | tf_op jit(solution)/shard_map/dot_general | solution.py:40
  8.9 3.1 %add_convert_fusion.1 = bf16[320,1280]{1,0:T(8,128)(2,1)} fusion(bf16[320,1280]{1,0:T(8,128)(2,1)S(1)} %collective-permute-done, bf16[1280,1024]{1,0:T(8,128)(2,1)S(1)} %copy-done, bf16[2,320,1024]{2,1,0:T(8,128)(2,1)} %bitcast.89, s32[]{:T(128)S(6)} %select_n.64), kind=kOutput, calls=%fused_computation.4 | convolution fusion | flops 840089600 | bytes 4915204 | tf_op jit(solution)/shard_map/dot_general | solution.py:40
  12.0 5.6 %all-to-all-start = ((bf16[4,80,1280]{2,1,0:T(8,128)(2,1)}), bf16[4,80,1280]{2,1,0:T(8,128)(2,1)S(1)}, u32[]{:S(2)}, u32[]{:S(2)}) async-start(bf16[4,80,1280]{2,1,0:T(8,128)(2,1)} %bitcast.96), calls=%async_computation | async-start | bytes 1638400 | tf_op jit(solution)/shard_map/all_to_all | solution.py:27
  17.7 5.7 %convolution_convert_fusion = bf16[1280,1024]{1,0:T(8,128)(2,1)} fusion(bf16[640,1024]{1,0:T(8,128)(2,1)} %param.9, bf16[640,1280]{1,0:T(8,128)(2,1)} %param.10, pred[640]{0:T(1024)(128)(4,1)S(1)} %fusion.22), kind=kOutput, calls=%fused_computation | convolution fusion | flops 1679851520 | bytes 5571200 | tf_op jit(solution)/shard_map/dot_general | solution.py:40
  23.4 6.0 %all-to-all-done = bf16[4,80,1280]{2,1,0:T(8,128)(2,1)S(1)} async-done(((bf16[4,80,1280]{2,1,0:T(8,128)(2,1)}), bf16[4,80,1280]{2,1,0:T(8,128)(2,1)S(1)}, u32[]{:S(2)}, u32[]{:S(2)}) %all-to-all-start) | async-done | bytes 819232 | tf_op jit(solution)/shard_map/all_to_all | solution.py:27
  34.5 2.9 %dynamic-slice_bitcast_fusion.2 = (bf16[8,40,1024]{2,1,0:T(8,128)(2,1)}, bf16[8,40,1024]{2,1,0:T(8,128)(2,1)}, bf16[8,40,1024]{2,1,0:T(8,128)(2,1)}) fusion(bf16[8,4,40,1024]{3,2,1,0:T(8,128)(2,1)} %bitcast.81, s32[]{:T(128)S(6)} %select_n.68, s32[]{:T(128)S(6)} %select_n.70, s32[]{:T(128)S(6)} %select_n.69), kind=kLoop, calls=%fused_computation.25 | loop fusion | bytes 3932172 | tf_op jit(solution)/shard_map/jit(dynamic_index_in_dim)/squeeze | solution.py:403
  46.6 10.0 %all-to-all-start.1 = ((bf16[32,5,8,128]{3,2,1,0:T(8,128)(2,1)}), bf16[32,5,8,128]{3,2,1,0:T(8,128)(2,1)S(1)}, u32[]{:S(2)}, u32[]{:S(2)}) async-start(bf16[32,5,8,128]{3,2,1,0:T(8,128)(2,1)} %spread.1), calls=%async_computation.1 | async-start | bytes 655360 | tf_op jit(solution)/shard_map/all_to_all | solution.py:27
  61.3 9.2 %collective-permute-done.3 = bf16[8,40,1024]{2,1,0:T(8,128)(2,1)} collective-permute-done((bf16[8,40,1024]{2,1,0:T(8,128)(2,1)}, bf16[8,40,1024]{2,1,0:T(8,128)(2,1)}, u32[]{:S(2)}, u32[]{:S(2)}) %collective-permute-start.3) | collective-permute-done | bytes 655392 | tf_op jit(solution)/shard_map/ppermute | solution.py:32
  71.7 3.0 %fusion.4 = bf16[8,40,1024]{2,1,0:T(8,128)(2,1)} fusion(bf16[8,40,1024]{2,1,0:T(8,128)(2,1)} %collective-permute-done.3, bf16[8,40,1024]{2,1,0:T(8,128)(2,1)} %collective-permute-done.2, bf16[8,40,1024]{2,1,0:T(8,128)(2,1)} %collective-permute-done.1, bf16[8,4,40,1024]{3,2,1,0:T(8,128)(2,1)} %bitcast.82, s32[]{:T(128)S(6)} %select_n.67), kind=kLoop, calls=%fused_computation.9 | loop fusion | flops 2621440 | bytes 3276804 | tf_op jit(solution)/shard_map/convert_element_type | solution.py:410
  77.4 10.2 %all-to-all-start.2 = ((bf16[32,5,8,128]{3,2,1,0:T(8,128)(2,1)}), bf16[32,5,8,128]{3,2,1,0:T(8,128)(2,1)S(1)}, u32[]{:S(2)}, u32[]{:S(2)}) async-start(bf16[32,5,8,128]{3,2,1,0:T(8,128)(2,1)} %bitcast.91), calls=%async_computation.2 | async-start | bytes 655360 | tf_op jit(solution)/shard_map/all_to_all | solution.py:27
  87.7 11.5 %attention.1 = (bf16[640,1280]{1,0:T(8,128)(2,1)}, bf16[640,1280]{1,0:T(8,128)(2,1)}, bf16[5,16,1280]{2,1,0:T(8,128)(2,1)}, bf16[640,768]{1,0:T(8,128)(2,1)}, f3...) custom-call(s32[3]{0:T(128)} %pad_add_fusion.words_ref, s32[5]{0:T(128)} %dynamic_slice.60.counts_ref, ...), custom_call_target="tpu_custom_call" | custom-call | flops 10000000000 | bytes 10000000 | tf_op jit(solution)/shard_map/attention/pallas_call | solution.py:187
  104.5 14.3 %all_to_all.40 = bf16[4,80,1280]{2,1,0:T(8,128)(2,1)S(1)} all-to-all(bf16[4,80,1280]{2,1,0:T(8,128)(2,1)} %bitcast.97), channel_id=1, replica_groups=mesh['z'=8,'x'=4,'y'=4,'c'=2] {'y'}, dimensions={0} | all-to-all | bytes 1638400 | tf_op jit(solution)/shard_map/all_to_all | solution.py:27
  122.0 12.0 %backward.1 = (bf16[640,1280]{1,0:T(8,128)(2,1)}, bf16[640,480]{1,0:T(8,128)(2,1)}, bf16[4,6,16,1280]{3,2,1,0:T(8,128)(2,1)}, bf16[4,6,16,1280]{3,2,1,0:T(8,128)(2,1)}) custom-call(s32[3]{0:T(128)} %pad_add_fusion.words_ref, bf16[4,5,16,1280]{3,2,1,0:T(8,128)(2,1)} %bitcast.95, bf16[4,5,16,1280]{3,2,1,0:T(8,128)(2,1)} %copy-done.10, ...), custom_call_target="tpu_custom_call" | custom-call | flops 10000000000 | bytes 10000000 | tf_op jit(solution)/shard_map/backward/pallas_call | solution.py:293
  134.1 5.6 %all-to-all-start.4 = ((bf16[8,40,1024]{2,1,0:T(8,128)(2,1)}), bf16[8,40,1024]{2,1,0:T(8,128)(2,1)S(1)}, u32[]{:S(2)}, u32[]{:S(2)}) async-start(bf16[8,40,1024]{2,1,0:T(8,128)(2,1)} %fusion.4), calls=%async_computation.4 | async-start | bytes 1310720 | tf_op jit(solution)/shard_map/all_to_all | solution.py:27
  142.4 18.2 %all-to-all-done.4 = bf16[8,40,1024]{2,1,0:T(8,128)(2,1)S(1)} async-done(((bf16[8,40,1024]{2,1,0:T(8,128)(2,1)}), bf16[8,40,1024]{2,1,0:T(8,128)(2,1)S(1)}, u32[]{:S(2)}, u32[]{:S(2)}) %all-to-all-start.4) | async-done | bytes 655392 | tf_op jit(solution)/shard_map/all_to_all | solution.py:27
  160.6 5.7 %all-to-all-start.5 = ((bf16[4,96,1280]{2,1,0:T(8,128)(2,1)}), bf16[4,96,1280]{2,1,0:T(8,128)(2,1)}, u32[]{:S(2)}, u32[]{:S(2)}) async-start(bf16[4,96,1280]{2,1,0:T(8,128)(2,1)} %bitcast.79), calls=%async_computation.5 | async-start | bytes 1966080 | tf_op jit(solution)/shard_map/all_to_all | solution.py:27
  166.2 4.6 %weight_terms.1 = bf16[1280,640]{1,0:T(8,128)(2,1)} custom-call(bf16[640,1280]{1,0:T(8,128)(2,1)} %get-tuple-element.42.normed_ref, bf16[640,1280]{1,0:T(8,128)(2,1)} %get-tuple-element.43.upstream_ref, bf16[640,480]{1,0:T(8,128)(2,1)} %get-tuple-element.44.packed_grad_ref, bf16[640,160]{1,0:T(8,128)(2,1)} %get-tuple-element.45.mixed_ref), custom_call_target="tpu_custom_call" | custom-call | flops 4000000000 | bytes 6000000 | tf_op jit(solution)/shard_map/weight_terms/pallas_call | solution.py:333
  173.1 3.0 %collective-permute-start.10 = (bf16[8,40,640]{2,1,0:T(8,128)(2,1)}, bf16[8,40,640]{2,1,0:T(8,128)(2,1)}, u32[]{:S(2)}, u32[]{:S(2)}) collective-permute-start(bf16[8,40,640]{2,1,0:T(8,128)(2,1)} %get-tuple-element.67), channel_id=1, source_target_pairs={{0,16},{8,24},{16,0},{24,8},{1,17},{9,25},{17,1},{25,9},{2,18},{10... | collective-permute-start | bytes 1228808 | tf_op jit(solution)/shard_map/ppermute | solution.py:32
  183.3 2.7 %collective-permute-start.15 = (bf16[8,40,1]{1,0,2:T(8,128)(2,1)S(1)}, bf16[8,40,1]{1,0,2:T(8,128)(2,1)S(1)}, u32[]{:S(2)}, u32[]{:S(2)}) collective-permute-start(bf16[8,40,1]{1,0,2:T(8,128)(2,1)S(1)} %bitcast.106), channel_id=1, source_target_pairs={{0,24},{8,0},{16,8},{24,16},{1,25},{9,1},{17,9},{25,17},{2,26},{10... | collective-permute-start | bytes 1928 | tf_op jit(solution)/shard_map/ppermute | solution.py:32
  188.8 6.1 %collective-permute-done.12 = bf16[8,40,640]{2,1,0:T(8,128)(2,1)} collective-permute-done((bf16[8,40,640]{2,1,0:T(8,128)(2,1)}, bf16[8,40,640]{2,1,0:T(8,128)(2,1)}, u32[]{:S(2)}, u32[]{:S(2)}) %collective-permute-start.12) | collective-permute-done | bytes 409632 | tf_op jit(solution)/shard_map/ppermute | solution.py:32
  197.3 4.8 %all-to-all-start.6 = ((bf16[8,80,160]{2,1,0:T(8,128)(2,1)}), bf16[8,80,160]{2,1,0:T(8,128)(2,1)}, u32[]{:S(2)}, u32[]{:S(2)}) async-start(bf16[8,80,160]{2,1,0:T(8,128)(2,1)} %get-tuple-element.40), calls=%async_computation.6 | async-start | bytes 655360 | tf_op jit(solution)/shard_map/all_to_all | solution.py:27
  204.1 4.8 %all-to-all-done.6 = bf16[8,80,160]{2,1,0:T(8,128)(2,1)} async-done(((bf16[8,80,160]{2,1,0:T(8,128)(2,1)}), bf16[8,80,160]{2,1,0:T(8,128)(2,1)}, u32[]{:S(2)}, u32[]{:S(2)}) %all-to-all-start.6) | async-done | bytes 204832 | tf_op jit(solution)/shard_map/all_to_all | solution.py:27
  208.9 4.1 %all-to-all-start.7 = ((bf16[8,40,768]{2,1,0:T(8,128)(2,1)}), bf16[8,40,768]{2,1,0:T(8,128)(2,1)}, u32[]{:S(2)}, u32[]{:S(2)}) async-start(bf16[8,40,768]{2,1,0:T(8,128)(2,1)} %fusion.17), calls=%async_computation.7 | async-start | bytes 983040 | tf_op jit(solution)/shard_map/all_to_all | solution.py:27
  215.7 14.0 %all-to-all-done.7 = bf16[8,40,768]{2,1,0:T(8,128)(2,1)} async-done(((bf16[8,40,768]{2,1,0:T(8,128)(2,1)}), bf16[8,40,768]{2,1,0:T(8,128)(2,1)}, u32[]{:S(2)}, u32[]{:S(2)}) %all-to-all-start.7) | async-done | bytes 491552 | tf_op jit(solution)/shard_map/all_to_all | solution.py:27
  (94 shorter events, 61.9 us)
Async XLA Ops:
  6.4 2.5 %collective-permute-start = (bf16[320,1280]{1,0:T(8,128)(2,1)}, bf16[320,1280]{1,0:T(8,128)(2,1)S(1)}, u32[]{:S(2)}, u32[]{:S(2)}) collective-permute-start(bf16[320,1280]{1,0:T(8,128)(2,1)} %convolution_convert_fusion.1), channel_id=1, source_target_pairs={{0,1},{1,0},{2,3},{3,2},{4,5},{5,4},{6,7},{7,6},{8,9},{9,8},{10,11... | collective-permute-start | bytes 2457608 | tf_op jit(solution)/shard_map/ppermute | solution.py:36
  12.0 17.4 %all-to-all-start = ((bf16[4,80,1280]{2,1,0:T(8,128)(2,1)}), bf16[4,80,1280]{2,1,0:T(8,128)(2,1)S(1)}, u32[]{:S(2)}, u32[]{:S(2)}) async-start(bf16[4,80,1280]{2,1,0:T(8,128)(2,1)} %bitcast.96), calls=%async_computation | async-start | bytes 1638400 | tf_op jit(solution)/shard_map/all_to_all | solution.py:27
  17.7 16.5 %copy-start.8 = (s32[32,5]{0,1:T(8,128)S(1)}, s32[32,5]{0,1:T(8,128)}, u32[]{:S(2)}) copy-start(s32[32,5]{0,1:T(8,128)} %param.13) | copy-start | bytes 1924
  29.4 11.2 %collective-permute-start.6 = (bf16[160,640]{1,0:T(8,128)(2,1)}, bf16[160,640]{1,0:T(8,128)(2,1)}, u32[]{:S(2)}, u32[]{:S(2)}) collective-permute-start(bf16[160,640]{1,0:T(8,128)(2,1)} %bitcast.100), channel_id=1, source_target_pairs={{0,6},{2,0},{4,2},{6,4},{1,7},{3,1},{5,3},{7,5},{8,14},{10,8},{12,... | collective-permute-start | bytes 614408 | tf_op jit(solution)/shard_map/ppermute | solution.py:32
  30.8 10.7 %collective-permute-start.5 = (bf16[160,640]{1,0:T(8,128)(2,1)}, bf16[160,640]{1,0:T(8,128)(2,1)}, u32[]{:S(2)}, u32[]{:S(2)}) collective-permute-start(bf16[160,640]{1,0:T(8,128)(2,1)} %bitcast.101), channel_id=1, source_target_pairs={{0,4},{2,6},{4,0},{6,2},{1,5},{3,7},{5,1},{7,3},{8,12},{10,14},{12... | collective-permute-start | bytes 614408 | tf_op jit(solution)/shard_map/ppermute | solution.py:32
  30.8 11.3 %collective-permute-start.4 = (bf16[160,640]{1,0:T(8,128)(2,1)}, bf16[160,640]{1,0:T(8,128)(2,1)}, u32[]{:S(2)}, u32[]{:S(2)}) collective-permute-start(bf16[160,640]{1,0:T(8,128)(2,1)} %bitcast.102), channel_id=1, source_target_pairs={{0,2},{2,4},{4,6},{6,0},{1,3},{3,5},{5,7},{7,1},{8,10},{10,12},{12... | collective-permute-start | bytes 614408 | tf_op jit(solution)/shard_map/ppermute | solution.py:32
  37.4 23.9 %collective-permute-start.1 = (bf16[8,40,1024]{2,1,0:T(8,128)(2,1)}, bf16[8,40,1024]{2,1,0:T(8,128)(2,1)}, u32[]{:S(2)}, u32[]{:S(2)}) collective-permute-start(bf16[8,40,1024]{2,1,0:T(8,128)(2,1)} %get-tuple-element.64), channel_id=1, source_target_pairs={{0,16},{8,24},{16,0},{24,8},{1,17},{9,25},{17,1},{25,9},{2,18},{10... | collective-permute-start | bytes 1966088 | tf_op jit(solution)/shard_map/ppermute | solution.py:32
  39.5 31.1 %collective-permute-start.3 = (bf16[8,40,1024]{2,1,0:T(8,128)(2,1)}, bf16[8,40,1024]{2,1,0:T(8,128)(2,1)}, u32[]{:S(2)}, u32[]{:S(2)}) collective-permute-start(bf16[8,40,1024]{2,1,0:T(8,128)(2,1)} %get-tuple-element.65), channel_id=1, source_target_pairs={{0,24},{8,0},{16,8},{24,16},{1,25},{9,1},{17,9},{25,17},{2,26},{10... | collective-permute-start | bytes 1966088 | tf_op jit(solution)/shard_map/ppermute | solution.py:32
  40.6 31.0 %collective-permute-start.2 = (bf16[8,40,1024]{2,1,0:T(8,128)(2,1)}, bf16[8,40,1024]{2,1,0:T(8,128)(2,1)}, u32[]{:S(2)}, u32[]{:S(2)}) collective-permute-start(bf16[8,40,1024]{2,1,0:T(8,128)(2,1)} %get-tuple-element.66), channel_id=1, source_target_pairs={{0,8},{8,16},{16,24},{24,0},{1,9},{9,17},{17,25},{25,1},{2,10},{10... | collective-permute-start | bytes 1966088 | tf_op jit(solution)/shard_map/ppermute | solution.py:32
  44.3 43.3 %collective-permute-start.7 = (bf16[4,160,640]{2,1,0:T(8,128)(2,1)}, bf16[4,160,640]{2,1,0:T(8,128)(2,1)}, u32[]{:S(2)}, u32[]{:S(2)}) collective-permute-start(bf16[4,160,640]{2,1,0:T(8,128)(2,1)} %pad_maximum_fusion.own_ref), channel_id=1, source_target_pairs={{0,1},{1,0},{2,3},{3,2},{4,5},{5,4},{6,7},{7,6},{8,9},{9,8},{10,11... | collective-permute-start | bytes 2457608 | tf_op jit(solution)/shard_map/ppermute | solution.py:36
  46.6 28.1 %all-to-all-start.1 = ((bf16[32,5,8,128]{3,2,1,0:T(8,128)(2,1)}), bf16[32,5,8,128]{3,2,1,0:T(8,128)(2,1)S(1)}, u32[]{:S(2)}, u32[]{:S(2)}) async-start(bf16[32,5,8,128]{3,2,1,0:T(8,128)(2,1)} %spread.1), calls=%async_computation.1 | async-start | bytes 655360 | tf_op jit(solution)/shard_map/all_to_all | solution.py:27
  77.4 24.2 %all-to-all-start.2 = ((bf16[32,5,8,128]{3,2,1,0:T(8,128)(2,1)}), bf16[32,5,8,128]{3,2,1,0:T(8,128)(2,1)S(1)}, u32[]{:S(2)}, u32[]{:S(2)}) async-start(bf16[32,5,8,128]{3,2,1,0:T(8,128)(2,1)} %bitcast.91), calls=%async_computation.2 | async-start | bytes 655360 | tf_op jit(solution)/shard_map/all_to_all | solution.py:27
  118.8 2.3 %collective-permute-start.8 = (bf16[4,5,16,1280]{3,2,1,0:T(8,128)(2,1)S(1)}, bf16[4,5,16,1280]{3,2,1,0:T(8,128)(2,1)S(1)}, u32[]{:S(2)}, u32[]{:S(2)}) collective-permute-start(bf16[4,5,16,1280]{3,2,1,0:T(8,128)(2,1)S(1)} %bitcast.94), channel_id=1, source_target_pairs={{0,1},{1,0},{2,3},{3,2},{4,5},{5,4},{6,7},{7,6},{8,9},{9,8},{10,11... | collective-permute-start | bytes 2457608 | tf_op jit(solution)/shard_map/ppermute | solution.py:36
  134.0 5.8 %collective-permute-start.9 = (bf16[4,6,16,1280]{3,2,1,0:T(8,128)(2,1)}, bf16[4,6,16,1280]{3,2,1,0:T(8,128)(2,1)}, u32[]{:S(2)}, u32[]{:S(2)}) collective-permute-start(bf16[4,6,16,1280]{3,2,1,0:T(8,128)(2,1)} %get-tuple-element.35), channel_id=1, source_target_pairs={{0,1},{1,0},{2,3},{3,2},{4,5},{5,4},{6,7},{7,6},{8,9},{9,8},{10,11... | collective-permute-start | bytes 2949128 | tf_op jit(solution)/shard_map/ppermute | solution.py:36
  134.1 26.4 %all-to-all-start.4 = ((bf16[8,40,1024]{2,1,0:T(8,128)(2,1)}), bf16[8,40,1024]{2,1,0:T(8,128)(2,1)S(1)}, u32[]{:S(2)}, u32[]{:S(2)}) async-start(bf16[8,40,1024]{2,1,0:T(8,128)(2,1)} %fusion.4), calls=%async_computation.4 | async-start | bytes 1310720 | tf_op jit(solution)/shard_map/all_to_all | solution.py:27
  160.6 19.2 %all-to-all-start.5 = ((bf16[4,96,1280]{2,1,0:T(8,128)(2,1)}), bf16[4,96,1280]{2,1,0:T(8,128)(2,1)}, u32[]{:S(2)}, u32[]{:S(2)}) async-start(bf16[4,96,1280]{2,1,0:T(8,128)(2,1)} %bitcast.79), calls=%async_computation.5 | async-start | bytes 1966080 | tf_op jit(solution)/shard_map/all_to_all | solution.py:27
  173.1 14.2 %collective-permute-start.10 = (bf16[8,40,640]{2,1,0:T(8,128)(2,1)}, bf16[8,40,640]{2,1,0:T(8,128)(2,1)}, u32[]{:S(2)}, u32[]{:S(2)}) collective-permute-start(bf16[8,40,640]{2,1,0:T(8,128)(2,1)} %get-tuple-element.67), channel_id=1, source_target_pairs={{0,16},{8,24},{16,0},{24,8},{1,17},{9,25},{17,1},{25,9},{2,18},{10... | collective-permute-start | bytes 1228808 | tf_op jit(solution)/shard_map/ppermute | solution.py:32
  176.1 18.8 %collective-permute-start.12 = (bf16[8,40,640]{2,1,0:T(8,128)(2,1)}, bf16[8,40,640]{2,1,0:T(8,128)(2,1)}, u32[]{:S(2)}, u32[]{:S(2)}) collective-permute-start(bf16[8,40,640]{2,1,0:T(8,128)(2,1)} %get-tuple-element.68), channel_id=1, source_target_pairs={{0,24},{8,0},{16,8},{24,16},{1,25},{9,1},{17,9},{25,17},{2,26},{10... | collective-permute-start | bytes 1228808 | tf_op jit(solution)/shard_map/ppermute | solution.py:32
  177.3 17.7 %collective-permute-start.11 = (bf16[8,40,640]{2,1,0:T(8,128)(2,1)}, bf16[8,40,640]{2,1,0:T(8,128)(2,1)}, u32[]{:S(2)}, u32[]{:S(2)}) collective-permute-start(bf16[8,40,640]{2,1,0:T(8,128)(2,1)} %get-tuple-element.69), channel_id=1, source_target_pairs={{0,8},{8,16},{16,24},{24,0},{1,9},{9,17},{17,25},{25,1},{2,10},{10... | collective-permute-start | bytes 1228808 | tf_op jit(solution)/shard_map/ppermute | solution.py:32
  183.3 18.8 %collective-permute-start.15 = (bf16[8,40,1]{1,0,2:T(8,128)(2,1)S(1)}, bf16[8,40,1]{1,0,2:T(8,128)(2,1)S(1)}, u32[]{:S(2)}, u32[]{:S(2)}) collective-permute-start(bf16[8,40,1]{1,0,2:T(8,128)(2,1)S(1)} %bitcast.106), channel_id=1, source_target_pairs={{0,24},{8,0},{16,8},{24,16},{1,25},{9,1},{17,9},{25,17},{2,26},{10... | collective-permute-start | bytes 1928 | tf_op jit(solution)/shard_map/ppermute | solution.py:32
  186.0 16.1 %collective-permute-start.13 = (bf16[8,40,1]{1,0,2:T(8,128)(2,1)S(1)}, bf16[8,40,1]{1,0,2:T(8,128)(2,1)S(1)}, u32[]{:S(2)}, u32[]{:S(2)}) collective-permute-start(bf16[8,40,1]{1,0,2:T(8,128)(2,1)S(1)} %bitcast.105), channel_id=1, source_target_pairs={{0,16},{8,24},{16,0},{24,8},{1,17},{9,25},{17,1},{25,9},{2,18},{10... | collective-permute-start | bytes 1928 | tf_op jit(solution)/shard_map/ppermute | solution.py:32
  187.3 14.8 %collective-permute-start.14 = (bf16[8,40,1]{1,0,2:T(8,128)(2,1)S(1)}, bf16[8,40,1]{1,0,2:T(8,128)(2,1)S(1)}, u32[]{:S(2)}, u32[]{:S(2)}) collective-permute-start(bf16[8,40,1]{1,0,2:T(8,128)(2,1)S(1)} %bitcast.104), channel_id=1, source_target_pairs={{0,8},{8,16},{16,24},{24,0},{1,9},{9,17},{17,25},{25,1},{2,10},{10... | collective-permute-start | bytes 1928 | tf_op jit(solution)/shard_map/ppermute | solution.py:32
  197.3 11.7 %all-to-all-start.6 = ((bf16[8,80,160]{2,1,0:T(8,128)(2,1)}), bf16[8,80,160]{2,1,0:T(8,128)(2,1)}, u32[]{:S(2)}, u32[]{:S(2)}) async-start(bf16[8,80,160]{2,1,0:T(8,128)(2,1)} %get-tuple-element.40), calls=%async_computation.6 | async-start | bytes 655360 | tf_op jit(solution)/shard_map/all_to_all | solution.py:27
  208.9 20.8 %all-to-all-start.7 = ((bf16[8,40,768]{2,1,0:T(8,128)(2,1)}), bf16[8,40,768]{2,1,0:T(8,128)(2,1)}, u32[]{:S(2)}, u32[]{:S(2)}) async-start(bf16[8,40,768]{2,1,0:T(8,128)(2,1)} %fusion.17), calls=%async_computation.7 | async-start | bytes 983040 | tf_op jit(solution)/shard_map/all_to_all | solution.py:27
  (10 other events, 54.0 us)
where the time goes:
time: 235 us; the launch traced here: 233 us
  waiting for transfers between devices  67.3 us (29%)
  starting transfers between devices  64.4 us (27%)
  Pallas kernels  36.8 us (16%)
  local copies, waits for them, and re-layouts  22.1 us (9%)
  other arithmetic  15.5 us (7%)
  blocking collectives  14.3 us (6%)
  matrix products  11.8 us (5%)
    all_to_all x7, waiting for transfers between devices, exchanged(): return lax.all_to_all(blocks, axis, split_axis=0, concat_axis=0, tiled=True)  47.2 us
    all_to_all x7, starting transfers between devices, exchanged(): return lax.all_to_all(blocks, axis, split_axis=0, concat_axis=0, tiled=True)  46 us
    ppermute x12, starting transfers between devices, shifted(): return lax.ppermute(values, axis, pairs)  18.2 us
    ppermute x12, waiting for transfers between devices, shifted(): return lax.ppermute(values, axis, pairs)  17.6 us
    all_to_all x1, blocking collectives, exchanged(): return lax.all_to_all(blocks, axis, split_axis=0, concat_axis=0, tiled=True)  14.3 us
    pallas_call x1, Pallas kernels, backward(): pl.pallas_call(backward_kernel, grid=(IMG + 1,), out_shape=(jax.ShapeDtyp...  12 us
    dot_general x3, matrix products, dot(): lax.dot_general(left, right, (((dim_left,), (dim_right,)), ((), ())), pre...  11.8 us
    pallas_call x1, Pallas kernels, attention(): pl.pallas_call(attention_kernel, grid=(IMG,), out_shape=(jax.ShapeDtypeSt...  11.5 us
  transfers between devices with their start and end apart: 23, of which 13 were waited for; matrix products, arithmetic and copies ran while one was open for 15% of the time, Pallas kernels for 10%

commit v1 on v0

--- a/solution.py
+++ b/solution.py
@@ -463,7 +463,7 @@
 
     passing = exchanged(pieces, ENC)
     passing = forwarded(source_of, passing)
-    landed = after(exchanged(passing, ENC), proj_near, prob)
+    landed = after(exchanged(passing, ENC), prob)
     upstream_rows, copies = collected(landed)
     half_own = exchanged(copies.reshape(4, 80, WIDTH), "y").reshape(4, IMG, 16, WIDTH)
     half_other = swapped(half_own)
@@ -484,12 +484,28 @@
     shares = exchanged(shares, TP)
     grad_input = shares.reshape(4, 2, IMG, 16, 160).transpose(2, 1, 0, 3, 4)
     grad_input = grad_input.reshape(ROWS, 160)
-    gain_near = near_sum(gain_term[0].astype(BF).reshape(PEERS * 40, 1), 1)
-    last = jnp.concatenate([term_near, jnp.pad(gain_near, ((0, 0), (0, 0), (0, 127)))], axis=2)
-    last = summed(exchanged(last, "z"))
+    last = summed(exchanged(term_near, "z"))
+    gain_rows = gain_term[0].astype(BF).reshape(8, 4, 40).transpose(1, 0, 2)
+    gain_rows = gain_rows.reshape(4, 1, 320)
+    here = lax.axis_index("x")
+
+    def gain_of(at):
+        return lax.dynamic_index_in_dim(gain_rows, lax.rem(here + at, 4), 0, keepdims=False)
+
+    gain_sum = gain_of(0).astype(F32)
+    for at in (2, 1, 3):
+        gain_sum = gain_sum + shifted(gain_of(at), "x", at).astype(F32)
+    gain_sum = gain_sum.reshape(8, 40)
+    far = lax.axis_index("z")
+    for reach in (4, 2, 1):
+        upper = (far // reach) % 2 == 1
+        low, high = gain_sum[:reach], gain_sum[reach:]
+        sent = jnp.where(upper, low, high).astype(BF)
+        got = lax.ppermute(sent, "z", tuple((i, i ^ reach) for i in range(8)))
+        gain_sum = jnp.where(upper, high, low) + got.astype(F32)
     grad_qkv = last[:, :480].reshape(40, 2, 240)
-    grad_out = last[:, 480:640].T
-    grad_ln1 = last[:, 640]
+    grad_out = last[:, 480:].T
+    grad_ln1 = gain_sum.reshape(40)
     return (grad_input, grad_proj, grad_qkv, grad_out, grad_ln1)
 
 

time: 235 us -> 256 us (1.089)
  waiting for transfers between devices: 67.3 us -> 94.2 us
  local copies, waits for them, and re-layouts: 22.1 us -> 18.5 us
    ppermute x12, waiting for transfers between devices: 17.6 us -> 39.6 us  [shifted(): return lax.ppermute(values, axis, pairs)]
    ppermute x0 -> x3, waiting for transfers between devices: none -> 9.52 us  [shards(): got = lax.ppermute(sent, 'z', tuple(((i, i ^ reach) for i in range(8))))]
    all_to_all x7, starting transfers between devices: 46 us -> 40.9 us  [exchanged(): return lax.all_to_all(blocks, axis, split_axis=0, concat_axis=0, tiled=True)]
    all_to_all x7, waiting for transfers between devices: 47.2 us -> 42.7 us  [exchanged(): return lax.all_to_all(blocks, axis, split_axis=0, concat_axis=0, tiled=True)]
    convert_element_type x3 -> x2, other arithmetic: 5.36 us -> 4.97 us  [near_sum(): return total.astype(BF)]
  transfers between devices with their start and end apart: 23 -> 26, of which waited for: 13 -> 16; matrix products, arithmetic and copies ran while one was open for 15% -> 12% of each run, Pallas kernels for 10% -> 14%
where the time goes in v1:
time: 256 us; the launch traced here: 253 us
  waiting for transfers between devices  94.2 us (37%)
  starting transfers between devices  62.9 us (25%)
  Pallas kernels  36.7 us (14%)
  local copies, waits for them, and re-layouts  18.5 us (7%)
  other arithmetic  14 us (5%)
  blocking collectives  14 us (5%)
  matrix products  11.7 us (5%)
    all_to_all x7, waiting for transfers between devices, exchanged(): return lax.all_to_all(blocks, axis, split_axis=0, concat_axis=0, tiled=True)  42.7 us
    all_to_all x7, starting transfers between devices, exchanged(): return lax.all_to_all(blocks, axis, split_axis=0, concat_axis=0, tiled=True)  40.9 us
    ppermute x12, waiting for transfers between devices, shifted(): return lax.ppermute(values, axis, pairs)  39.6 us
    ppermute x12, starting transfers between devices, shifted(): return lax.ppermute(values, axis, pairs)  20.4 us
    all_to_all x1, blocking collectives, exchanged(): return lax.all_to_all(blocks, axis, split_axis=0, concat_axis=0, tiled=True)  14 us
    pallas_call x1, Pallas kernels, backward(): pl.pallas_call(backward_kernel, grid=(IMG + 1,), out_shape=(jax.ShapeDtyp...  11.9 us
    dot_general x3, matrix products, dot(): lax.dot_general(left, right, (((dim_left,), (dim_right,)), ((), ())), pre...  11.7 us
    pallas_call x1, Pallas kernels, attention(): pl.pallas_call(attention_kernel, grid=(IMG,), out_shape=(jax.ShapeDtypeSt...  11.4 us
  transfers between devices with their start and end apart: 26, of which 16 were waited for; matrix products, arithmetic and copies ran while one was open for 12% of the time, Pallas kernels for 14%

profile of v1, /device:TPU:8, one launch (start us, length us, event | category | flops | bytes accessed | tf_op | source)
XLA Modules:
  0.0 253.0 jit_solution(12926983737908727708)
XLA Ops:
  8.9 3.0 %add_convert_fusion.1 = bf16[320,1280]{1,0:T(8,128)(2,1)} fusion(bf16[320,1280]{1,0:T(8,128)(2,1)S(1)} %collective-permute-done, bf16[1280,1024]{1,0:T(8,128)(2,1)S(1)} %copy-done, bf16[2,320,1024]{2,1,0:T(8,128)(2,1)} %bitcast.97, s32[]{:T(128)S(6)} %select_n.127), kind=kOutput, calls=%fused_computation.4 | convolution fusion | flops 840089600 | bytes 4915204 | tf_op jit(solution)/shard_map/dot_general | solution.py:40
  12.0 5.6 %all-to-all-start = ((bf16[4,80,1280]{2,1,0:T(8,128)(2,1)}), bf16[4,80,1280]{2,1,0:T(8,128)(2,1)S(1)}, u32[]{:S(2)}, u32[]{:S(2)}) async-start(bf16[4,80,1280]{2,1,0:T(8,128)(2,1)} %bitcast.105), calls=%async_computation | async-start | bytes 1638400 | tf_op jit(solution)/shard_map/all_to_all | solution.py:27
  17.7 5.6 %convolution_convert_fusion = bf16[1280,1024]{1,0:T(8,128)(2,1)} fusion(bf16[640,1024]{1,0:T(8,128)(2,1)} %param.9, bf16[640,1280]{1,0:T(8,128)(2,1)} %param.10, pred[640]{0:T(1024)(128)(4,1)S(1)} %fusion.17), kind=kOutput, calls=%fused_computation | convolution fusion | flops 1679851520 | bytes 5571200 | tf_op jit(solution)/shard_map/dot_general | solution.py:40
  23.3 6.0 %all-to-all-done = bf16[4,80,1280]{2,1,0:T(8,128)(2,1)S(1)} async-done(((bf16[4,80,1280]{2,1,0:T(8,128)(2,1)}), bf16[4,80,1280]{2,1,0:T(8,128)(2,1)S(1)}, u32[]{:S(2)}, u32[]{:S(2)}) %all-to-all-start) | async-done | bytes 819232 | tf_op jit(solution)/shard_map/all_to_all | solution.py:27
  29.4 3.5 %collective-permute-start.2 = (bf16[160,640]{1,0:T(8,128)(2,1)}, bf16[160,640]{1,0:T(8,128)(2,1)S(1)}, u32[]{:S(2)}, u32[]{:S(2)}) collective-permute-start(bf16[160,640]{1,0:T(8,128)(2,1)} %bitcast.110), channel_id=1, source_target_pairs={{0,4},{2,6},{4,0},{6,2},{1,5},{3,7},{5,1},{7,3},{8,12},{10,14},{12... | collective-permute-start | bytes 614408 | tf_op jit(solution)/shard_map/ppermute | solution.py:32
  33.5 4.1 %collective-permute-done.1 = bf16[160,640]{1,0:T(8,128)(2,1)S(1)} collective-permute-done((bf16[160,640]{1,0:T(8,128)(2,1)}, bf16[160,640]{1,0:T(8,128)(2,1)S(1)}, u32[]{:S(2)}, u32[]{:S(2)}) %collective-permute-start.1) | collective-permute-done | bytes 204832 | tf_op jit(solution)/shard_map/ppermute | solution.py:32
  46.8 10.0 %all-to-all-start.1 = ((bf16[32,5,8,128]{3,2,1,0:T(8,128)(2,1)}), bf16[32,5,8,128]{3,2,1,0:T(8,128)(2,1)S(1)}, u32[]{:S(2)}, u32[]{:S(2)}) async-start(bf16[32,5,8,128]{3,2,1,0:T(8,128)(2,1)} %spread.1), calls=%async_computation.1 | async-start | bytes 655360 | tf_op jit(solution)/shard_map/all_to_all | solution.py:27
  61.8 9.9 %all-to-all-done.1 = bf16[32,5,8,128]{3,2,1,0:T(8,128)(2,1)S(1)} async-done(((bf16[32,5,8,128]{3,2,1,0:T(8,128)(2,1)}), bf16[32,5,8,128]{3,2,1,0:T(8,128)(2,1)S(1)}, u32[]{:S(2)}, u32[]{:S(2)}) %all-to-all-start.1) | async-done | bytes 327712 | tf_op jit(solution)/shard_map/all_to_all | solution.py:27
  74.4 4.0 %all-to-all-start.2 = ((bf16[32,5,8,128]{3,2,1,0:T(8,128)(2,1)}), bf16[32,5,8,128]{3,2,1,0:T(8,128)(2,1)S(1)}, u32[]{:S(2)}, u32[]{:S(2)}) async-start(bf16[32,5,8,128]{3,2,1,0:T(8,128)(2,1)} %bitcast.99), calls=%async_computation.2 | async-start | bytes 655360 | tf_op jit(solution)/shard_map/all_to_all | solution.py:27
  78.5 11.4 %attention.1 = (bf16[640,1280]{1,0:T(8,128)(2,1)}, bf16[640,1280]{1,0:T(8,128)(2,1)}, bf16[5,16,1280]{2,1,0:T(8,128)(2,1)}, bf16[640,768]{1,0:T(8,128)(2,1)}, f3...) custom-call(s32[3]{0:T(128)} %pad_add_fusion.words_ref, s32[5]{0:T(128)} %dynamic_slice.56.counts_ref, ...), custom_call_target="tpu_custom_call" | custom-call | flops 10000000000 | bytes 10000000 | tf_op jit(solution)/shard_map/attention/pallas_call | solution.py:187
  94.7 14.0 %all_to_all.40 = bf16[4,80,1280]{2,1,0:T(8,128)(2,1)S(1)} all-to-all(bf16[4,80,1280]{2,1,0:T(8,128)(2,1)} %bitcast.106), channel_id=1, replica_groups=mesh['z'=8,'x'=4,'y'=4,'c'=2] {'y'}, dimensions={0} | all-to-all | bytes 1638400 | tf_op jit(solution)/shard_map/all_to_all | solution.py:27
  119.8 11.9 %backward.1 = (bf16[640,1280]{1,0:T(8,128)(2,1)}, bf16[640,480]{1,0:T(8,128)(2,1)}, bf16[4,6,16,1280]{3,2,1,0:T(8,128)(2,1)}, bf16[4,6,16,1280]{3,2,1,0:T(8,128)(2,1)}) custom-call(s32[3]{0:T(128)} %pad_add_fusion.words_ref, bf16[4,5,16,1280]{3,2,1,0:T(8,128)(2,1)} %bitcast.104, bf16[4,5,16,1280]{3,2,1,0:T(8,128)(2,1)} %collective-permute-done.5.other_ref, ...), custom_call_target="tpu_custom_call" | custom-call | flops 10000000000 | bytes 10000000 | tf_op jit(solution)/shard_map/backward/pallas_call | solution.py:293
  133.2 13.3 %collective-permute-done.8 = bf16[8,40,1024]{2,1,0:T(8,128)(2,1)} collective-permute-done((bf16[8,40,1024]{2,1,0:T(8,128)(2,1)}, bf16[8,40,1024]{2,1,0:T(8,128)(2,1)}, u32[]{:S(2)}, u32[]{:S(2)}) %collective-permute-start.8) | collective-permute-done | bytes 655392 | tf_op jit(solution)/shard_map/ppermute | solution.py:32
  149.4 6.6 %all-to-all-start.4 = ((bf16[8,40,1024]{2,1,0:T(8,128)(2,1)}), bf16[8,40,1024]{2,1,0:T(8,128)(2,1)S(1)}, u32[]{:S(2)}, u32[]{:S(2)}) async-start(bf16[8,40,1024]{2,1,0:T(8,128)(2,1)} %fusion.4), calls=%async_computation.4 | async-start | bytes 1310720 | tf_op jit(solution)/shard_map/all_to_all | solution.py:27
  156.1 4.7 %weight_terms.1 = bf16[1280,640]{1,0:T(8,128)(2,1)} custom-call(bf16[640,1280]{1,0:T(8,128)(2,1)} %get-tuple-element.42.normed_ref, bf16[640,1280]{1,0:T(8,128)(2,1)} %get-tuple-element.43.upstream_ref, bf16[640,480]{1,0:T(8,128)(2,1)} %get-tuple-element.44.packed_grad_ref, bf16[640,160]{1,0:T(8,128)(2,1)} %get-tuple-element.45.mixed_ref), custom_call_target="tpu_custom_call" | custom-call | flops 4000000000 | bytes 6000000 | tf_op jit(solution)/shard_map/weight_terms/pallas_call | solution.py:333
  163.4 13.1 %all-to-all-done.4 = bf16[8,40,1024]{2,1,0:T(8,128)(2,1)S(1)} async-done(((bf16[8,40,1024]{2,1,0:T(8,128)(2,1)}), bf16[8,40,1024]{2,1,0:T(8,128)(2,1)S(1)}, u32[]{:S(2)}, u32[]{:S(2)}) %all-to-all-start.4) | async-done | bytes 655392 | tf_op jit(solution)/shard_map/all_to_all | solution.py:27
  176.5 5.6 %all-to-all-start.5 = ((bf16[4,96,1280]{2,1,0:T(8,128)(2,1)}), bf16[4,96,1280]{2,1,0:T(8,128)(2,1)}, u32[]{:S(2)}, u32[]{:S(2)}) async-start(bf16[4,96,1280]{2,1,0:T(8,128)(2,1)} %bitcast.87), calls=%async_computation.5 | async-start | bytes 1966080 | tf_op jit(solution)/shard_map/all_to_all | solution.py:27
  188.3 9.2 %collective-permute-done.10 = bf16[8,40,640]{2,1,0:T(8,128)(2,1)S(1)} collective-permute-done((bf16[8,40,640]{2,1,0:T(8,128)(2,1)S(1)}, bf16[8,40,640]{2,1,0:T(8,128)(2,1)S(1)}, u32[]{:S(2)}, u32[]{:S(2)}) %collective-permute-start.10) | collective-permute-done | bytes 409632 | tf_op jit(solution)/shard_map/ppermute | solution.py:32
  197.5 7.5 %collective-permute-done.11 = bf16[8,40,640]{2,1,0:T(8,128)(2,1)S(1)} collective-permute-done((bf16[8,40,640]{2,1,0:T(8,128)(2,1)S(1)}, bf16[8,40,640]{2,1,0:T(8,128)(2,1)S(1)}, u32[]{:S(2)}, u32[]{:S(2)}) %collective-permute-start.11) | collective-permute-done | bytes 409632 | tf_op jit(solution)/shard_map/ppermute | solution.py:32
  207.0 4.1 %all-to-all-start.7 = ((bf16[8,40,640]{2,1,0:T(8,128)(2,1)}), bf16[8,40,640]{2,1,0:T(8,128)(2,1)}, u32[]{:S(2)}, u32[]{:S(2)}) async-start(bf16[8,40,640]{2,1,0:T(8,128)(2,1)} %fusion.7), calls=%async_computation.7 | async-start | bytes 819200 | tf_op jit(solution)/shard_map/all_to_all | solution.py:27
  220.9 5.7 %all-to-all-done.7 = bf16[8,40,640]{2,1,0:T(8,128)(2,1)} async-done(((bf16[8,40,640]{2,1,0:T(8,128)(2,1)}), bf16[8,40,640]{2,1,0:T(8,128)(2,1)}, u32[]{:S(2)}, u32[]{:S(2)}) %all-to-all-start.7) | async-done | bytes 409632 | tf_op jit(solution)/shard_map/all_to_all | solution.py:27
  228.8 6.5 %collective-permute-done.16 = bf16[4,40]{1,0:T(4,128)(2,1)S(1)} collective-permute-done((bf16[4,40]{1,0:T(4,128)(2,1)S(1)}, bf16[4,40]{1,0:T(4,128)(2,1)S(1)}, u32[]{:S(2)}, u32[]{:S(2)}) %collective-permute-start.16) | collective-permute-done | bytes 352 | tf_op jit(solution)/shard_map/ppermute | solution.py:504
  240.6 4.8 %all-to-all-start.6 = ((bf16[8,80,160]{2,1,0:T(8,128)(2,1)}), bf16[8,80,160]{2,1,0:T(8,128)(2,1)S(1)}, u32[]{:S(2)}, u32[]{:S(2)}) async-start(bf16[8,80,160]{2,1,0:T(8,128)(2,1)} %get-tuple-element.40), calls=%async_computation.6 | async-start | bytes 655360 | tf_op jit(solution)/shard_map/all_to_all | solution.py:27
  245.9 6.2 %all-to-all-done.6 = bf16[8,80,160]{2,1,0:T(8,128)(2,1)S(1)} async-done(((bf16[8,80,160]{2,1,0:T(8,128)(2,1)}), bf16[8,80,160]{2,1,0:T(8,128)(2,1)S(1)}, u32[]{:S(2)}, u32[]{:S(2)}) %all-to-all-start.6) | async-done | bytes 204832 | tf_op jit(solution)/shard_map/all_to_all | solution.py:27
  (101 shorter events, 75.5 us)
Async XLA Ops:
  12.0 17.4 %all-to-all-start = ((bf16[4,80,1280]{2,1,0:T(8,128)(2,1)}), bf16[4,80,1280]{2,1,0:T(8,128)(2,1)S(1)}, u32[]{:S(2)}, u32[]{:S(2)}) async-start(bf16[4,80,1280]{2,1,0:T(8,128)(2,1)} %bitcast.105), calls=%async_computation | async-start | bytes 1638400 | tf_op jit(solution)/shard_map/all_to_all | solution.py:27
  29.4 8.2 %collective-permute-start.1 = (bf16[160,640]{1,0:T(8,128)(2,1)}, bf16[160,640]{1,0:T(8,128)(2,1)S(1)}, u32[]{:S(2)}, u32[]{:S(2)}) collective-permute-start(bf16[160,640]{1,0:T(8,128)(2,1)} %bitcast.109), channel_id=1, source_target_pairs={{0,2},{2,4},{4,6},{6,0},{1,3},{3,5},{5,7},{7,1},{8,10},{10,12},{12... | collective-permute-start | bytes 614408 | tf_op jit(solution)/shard_map/ppermute | solution.py:32
  29.4 9.7 %collective-permute-start.2 = (bf16[160,640]{1,0:T(8,128)(2,1)}, bf16[160,640]{1,0:T(8,128)(2,1)S(1)}, u32[]{:S(2)}, u32[]{:S(2)}) collective-permute-start(bf16[160,640]{1,0:T(8,128)(2,1)} %bitcast.110), channel_id=1, source_target_pairs={{0,4},{2,6},{4,0},{6,2},{1,5},{3,7},{5,1},{7,3},{8,12},{10,14},{12... | collective-permute-start | bytes 614408 | tf_op jit(solution)/shard_map/ppermute | solution.py:32
  32.9 8.9 %collective-permute-start.3 = (bf16[160,640]{1,0:T(8,128)(2,1)}, bf16[160,640]{1,0:T(8,128)(2,1)S(1)}, u32[]{:S(2)}, u32[]{:S(2)}) collective-permute-start(bf16[160,640]{1,0:T(8,128)(2,1)} %bitcast.111), channel_id=1, source_target_pairs={{0,6},{2,0},{4,2},{6,4},{1,7},{3,1},{5,3},{7,5},{8,14},{10,8},{12,... | collective-permute-start | bytes 614408 | tf_op jit(solution)/shard_map/ppermute | solution.py:32
  43.8 34.7 %collective-permute-start.4 = (bf16[4,160,640]{2,1,0:T(8,128)(2,1)}, bf16[4,160,640]{2,1,0:T(8,128)(2,1)}, u32[]{:S(2)}, u32[]{:S(2)}) collective-permute-start(bf16[4,160,640]{2,1,0:T(8,128)(2,1)} %pad_maximum_fusion.own_ref), channel_id=1, source_target_pairs={{0,1},{1,0},{2,3},{3,2},{4,5},{5,4},{6,7},{7,6},{8,9},{9,8},{10,11... | collective-permute-start | bytes 2457608 | tf_op jit(solution)/shard_map/ppermute | solution.py:36
  46.8 24.9 %all-to-all-start.1 = ((bf16[32,5,8,128]{3,2,1,0:T(8,128)(2,1)}), bf16[32,5,8,128]{3,2,1,0:T(8,128)(2,1)S(1)}, u32[]{:S(2)}, u32[]{:S(2)}) async-start(bf16[32,5,8,128]{3,2,1,0:T(8,128)(2,1)} %spread.1), calls=%async_computation.1 | async-start | bytes 655360 | tf_op jit(solution)/shard_map/all_to_all | solution.py:27
  74.4 17.3 %all-to-all-start.2 = ((bf16[32,5,8,128]{3,2,1,0:T(8,128)(2,1)}), bf16[32,5,8,128]{3,2,1,0:T(8,128)(2,1)S(1)}, u32[]{:S(2)}, u32[]{:S(2)}) async-start(bf16[32,5,8,128]{3,2,1,0:T(8,128)(2,1)} %bitcast.99), calls=%async_computation.2 | async-start | bytes 655360 | tf_op jit(solution)/shard_map/all_to_all | solution.py:27
  108.7 11.1 %collective-permute-start.5 = (bf16[4,5,16,1280]{3,2,1,0:T(8,128)(2,1)S(1)}, bf16[4,5,16,1280]{3,2,1,0:T(8,128)(2,1)}, u32[]{:S(2)}, u32[]{:S(2)}) collective-permute-start(bf16[4,5,16,1280]{3,2,1,0:T(8,128)(2,1)S(1)} %bitcast.103), channel_id=1, source_target_pairs={{0,1},{1,0},{2,3},{3,2},{4,5},{5,4},{6,7},{7,6},{8,9},{9,8},{10,11... | collective-permute-start | bytes 2457608 | tf_op jit(solution)/shard_map/ppermute | solution.py:36
  113.7 19.5 %collective-permute-start.7 = (bf16[8,40,1024]{2,1,0:T(8,128)(2,1)}, bf16[8,40,1024]{2,1,0:T(8,128)(2,1)}, u32[]{:S(2)}, u32[]{:S(2)}) collective-permute-start(bf16[8,40,1024]{2,1,0:T(8,128)(2,1)} %get-tuple-element.64), channel_id=1, source_target_pairs={{0,16},{8,24},{16,0},{24,8},{1,17},{9,25},{17,1},{25,9},{2,18},{10... | collective-permute-start | bytes 1966088 | tf_op jit(solution)/shard_map/ppermute | solution.py:32
  116.6 29.8 %collective-permute-start.8 = (bf16[8,40,1024]{2,1,0:T(8,128)(2,1)}, bf16[8,40,1024]{2,1,0:T(8,128)(2,1)}, u32[]{:S(2)}, u32[]{:S(2)}) collective-permute-start(bf16[8,40,1024]{2,1,0:T(8,128)(2,1)} %get-tuple-element.66), channel_id=1, source_target_pairs={{0,8},{8,16},{16,24},{24,0},{1,9},{9,17},{17,25},{25,1},{2,10},{10... | collective-permute-start | bytes 1966088 | tf_op jit(solution)/shard_map/ppermute | solution.py:32
  117.2 29.3 %collective-permute-start.9 = (bf16[8,40,1024]{2,1,0:T(8,128)(2,1)}, bf16[8,40,1024]{2,1,0:T(8,128)(2,1)}, u32[]{:S(2)}, u32[]{:S(2)}) collective-permute-start(bf16[8,40,1024]{2,1,0:T(8,128)(2,1)} %get-tuple-element.65), channel_id=1, source_target_pairs={{0,24},{8,0},{16,8},{24,16},{1,25},{9,1},{17,9},{25,17},{2,26},{10... | collective-permute-start | bytes 1966088 | tf_op jit(solution)/shard_map/ppermute | solution.py:32
  131.7 29.0 %collective-permute-start.6 = (bf16[4,6,16,1280]{3,2,1,0:T(8,128)(2,1)}, bf16[4,6,16,1280]{3,2,1,0:T(8,128)(2,1)}, u32[]{:S(2)}, u32[]{:S(2)}) collective-permute-start(bf16[4,6,16,1280]{3,2,1,0:T(8,128)(2,1)} %get-tuple-element.35), channel_id=1, source_target_pairs={{0,1},{1,0},{2,3},{3,2},{4,5},{5,4},{6,7},{7,6},{8,9},{9,8},{10,11... | collective-permute-start | bytes 2949128 | tf_op jit(solution)/shard_map/ppermute | solution.py:36
  149.4 27.1 %all-to-all-start.4 = ((bf16[8,40,1024]{2,1,0:T(8,128)(2,1)}), bf16[8,40,1024]{2,1,0:T(8,128)(2,1)S(1)}, u32[]{:S(2)}, u32[]{:S(2)}) async-start(bf16[8,40,1024]{2,1,0:T(8,128)(2,1)} %fusion.4), calls=%async_computation.4 | async-start | bytes 1310720 | tf_op jit(solution)/shard_map/all_to_all | solution.py:27
  176.5 30.5 %all-to-all-start.5 = ((bf16[4,96,1280]{2,1,0:T(8,128)(2,1)}), bf16[4,96,1280]{2,1,0:T(8,128)(2,1)}, u32[]{:S(2)}, u32[]{:S(2)}) async-start(bf16[4,96,1280]{2,1,0:T(8,128)(2,1)} %bitcast.87), calls=%async_computation.5 | async-start | bytes 1966080 | tf_op jit(solution)/shard_map/all_to_all | solution.py:27
  183.5 14.0 %collective-permute-start.10 = (bf16[8,40,640]{2,1,0:T(8,128)(2,1)S(1)}, bf16[8,40,640]{2,1,0:T(8,128)(2,1)S(1)}, u32[]{:S(2)}, u32[]{:S(2)}) collective-permute-start(bf16[8,40,640]{2,1,0:T(8,128)(2,1)S(1)} %get-tuple-element.67), channel_id=1, source_target_pairs={{0,16},{8,24},{16,0},{24,8},{1,17},{9,25},{17,1},{25,9},{2,18},{10... | collective-permute-start | bytes 1228808 | tf_op jit(solution)/shard_map/ppermute | solution.py:32
  185.0 19.9 %collective-permute-start.11 = (bf16[8,40,640]{2,1,0:T(8,128)(2,1)S(1)}, bf16[8,40,640]{2,1,0:T(8,128)(2,1)S(1)}, u32[]{:S(2)}, u32[]{:S(2)}) collective-permute-start(bf16[8,40,640]{2,1,0:T(8,128)(2,1)S(1)} %get-tuple-element.69), channel_id=1, source_target_pairs={{0,8},{8,16},{16,24},{24,0},{1,9},{9,17},{17,25},{25,1},{2,10},{10... | collective-permute-start | bytes 1228808 | tf_op jit(solution)/shard_map/ppermute | solution.py:32
  187.1 17.9 %collective-permute-start.12 = (bf16[8,40,640]{2,1,0:T(8,128)(2,1)S(1)}, bf16[8,40,640]{2,1,0:T(8,128)(2,1)S(1)}, u32[]{:S(2)}, u32[]{:S(2)}) collective-permute-start(bf16[8,40,640]{2,1,0:T(8,128)(2,1)S(1)} %get-tuple-element.68), channel_id=1, source_target_pairs={{0,24},{8,0},{16,8},{24,16},{1,25},{9,1},{17,9},{25,17},{2,26},{10... | collective-permute-start | bytes 1228808 | tf_op jit(solution)/shard_map/ppermute | solution.py:32
  207.0 19.6 %all-to-all-start.7 = ((bf16[8,40,640]{2,1,0:T(8,128)(2,1)}), bf16[8,40,640]{2,1,0:T(8,128)(2,1)}, u32[]{:S(2)}, u32[]{:S(2)}) async-start(bf16[8,40,640]{2,1,0:T(8,128)(2,1)} %fusion.7), calls=%async_computation.7 | async-start | bytes 819200 | tf_op jit(solution)/shard_map/all_to_all | solution.py:27
  215.5 12.1 %collective-permute-start.13 = (bf16[1,320]{1,0:T(2,128)(2,1)S(1)}, bf16[1,320]{1,0:T(2,128)(2,1)S(1)}, u32[]{:S(2)}, u32[]{:S(2)}) collective-permute-start(bf16[1,320]{1,0:T(2,128)(2,1)S(1)} %get-tuple-element.70), channel_id=1, source_target_pairs={{0,16},{8,24},{16,0},{24,8},{1,17},{9,25},{17,1},{25,9},{2,18},{10... | collective-permute-start | bytes 1928 | tf_op jit(solution)/shard_map/ppermute | solution.py:32
  217.7 10.0 %collective-permute-start.14 = (bf16[1,320]{1,0:T(2,128)(2,1)S(1)}, bf16[1,320]{1,0:T(2,128)(2,1)S(1)}, u32[]{:S(2)}, u32[]{:S(2)}) collective-permute-start(bf16[1,320]{1,0:T(2,128)(2,1)S(1)} %get-tuple-element.72), channel_id=1, source_target_pairs={{0,8},{8,16},{16,24},{24,0},{1,9},{9,17},{17,25},{25,1},{2,10},{10... | collective-permute-start | bytes 1928 | tf_op jit(solution)/shard_map/ppermute | solution.py:32
  219.1 8.6 %collective-permute-start.15 = (bf16[1,320]{1,0:T(2,128)(2,1)S(1)}, bf16[1,320]{1,0:T(2,128)(2,1)S(1)}, u32[]{:S(2)}, u32[]{:S(2)}) collective-permute-start(bf16[1,320]{1,0:T(2,128)(2,1)S(1)} %get-tuple-element.71), channel_id=1, source_target_pairs={{0,24},{8,0},{16,8},{24,16},{1,25},{9,1},{17,9},{25,17},{2,26},{10... | collective-permute-start | bytes 1928 | tf_op jit(solution)/shard_map/ppermute | solution.py:32
  227.9 7.5 %collective-permute-start.16 = (bf16[4,40]{1,0:T(4,128)(2,1)S(1)}, bf16[4,40]{1,0:T(4,128)(2,1)S(1)}, u32[]{:S(2)}, u32[]{:S(2)}) collective-permute-start(bf16[4,40]{1,0:T(4,128)(2,1)S(1)} %convert_element_type.148), channel_id=1, source_target_pairs={{0,128},{32,160},{64,192},{96,224},{128,0},{160,32},{192,64},{224,... | collective-permute-start | bytes 968 | tf_op jit(solution)/shard_map/ppermute | solution.py:504
  239.9 5.5 %collective-permute-start.18 = (bf16[1,40]{1,0:T(2,128)(2,1)S(1)}, bf16[1,40]{1,0:T(2,128)(2,1)S(1)}, u32[]{:S(2)}, u32[]{:S(2)}) collective-permute-start(bf16[1,40]{1,0:T(2,128)(2,1)S(1)} %fusion.33), channel_id=1, source_target_pairs={{0,32},{32,0},{64,96},{96,64},{128,160},{160,128},{192,224},{224,1... | collective-permute-start | bytes 248 | tf_op jit(solution)/shard_map/ppermute | solution.py:504
  240.6 11.6 %all-to-all-start.6 = ((bf16[8,80,160]{2,1,0:T(8,128)(2,1)}), bf16[8,80,160]{2,1,0:T(8,128)(2,1)S(1)}, u32[]{:S(2)}, u32[]{:S(2)}) async-start(bf16[8,80,160]{2,1,0:T(8,128)(2,1)} %get-tuple-element.40), calls=%async_computation.6 | async-start | bytes 655360 | tf_op jit(solution)/shard_map/all_to_all | solution.py:27
  (11 other events, 87.2 us)

commit v2 on v1

--- a/solution.py
+++ b/solution.py
@@ -23,6 +23,12 @@
 SWAP = ((0, 1), (1, 0))
 
 
+def padded_heads(padded_ref, heads_ref):
+    for at in range(heads_ref.shape[0] // HEAD):
+        padded_ref[at * LANE : at * LANE + HEAD] = heads_ref[at * HEAD : (at + 1) * HEAD]
+        padded_ref[at * LANE + HEAD : (at + 1) * LANE] = jnp.zeros((LANE - HEAD, WIDTH), BF)
+
+
 def exchanged(blocks, axis):
     return lax.all_to_all(blocks, axis, split_axis=0, concat_axis=0, tiled=True)
 
@@ -148,7 +154,12 @@
     prob_ref,
     mixed_ref,
     scratch,
+    w_pad,
 ):
+    @pl.when(pl.program_id(0) == 0)
+    def _():
+        padded_heads(w_pad, w_ref)
+
     first = words_ref[0] == 0
     shares = []
     for near in range(4):
@@ -162,7 +173,7 @@
     normed_ref[...] = normed.astype(BF)
     normed_in = (normed * gain_ref[...]).astype(BF)
     normed_in_ref[...] = normed_in
-    packed = dot(normed_in, w_ref[...], 1, 1).astype(BF)
+    packed = dot(normed_in, w_pad[...], 1, 1).astype(BF)
     packed_ref[...] = packed
     count = counts_ref[pl.program_id(0)]
     live_row = lax.broadcasted_iota(jnp.int32, (TILE, TILE), 0) < count
@@ -181,7 +192,7 @@
     mixed_ref[...] = shifted_sum(mixed, 256)[:, :160].astype(BF)
 
 
-def attention(words, counts, own, other, gain, w_pad):
+def attention(words, counts, own, other, gain, w_heads):
     share = pl.BlockSpec((4, 160, TILE), lambda i: (0, 0, i))
     rows = pl.BlockSpec((TILE, WIDTH), lambda i: (i, 0))
     return pl.pallas_call(
@@ -201,7 +212,7 @@
             share,
             share,
             pl.BlockSpec((1, WIDTH), lambda i: (0, 0)),
-            pl.BlockSpec((6 * LANE, WIDTH), lambda i: (0, 0)),
+            pl.BlockSpec((6 * HEAD, WIDTH), lambda i: (0, 0)),
         ],
         out_specs=(
             rows,
@@ -211,12 +222,12 @@
             pl.BlockSpec((1, 2, TILE, TILE), lambda i: (i, 0, 0, 0)),
             pl.BlockSpec((TILE, 2 * HEAD), lambda i: (i, 0)),
         ),
-        scratch_shapes=[pltpu.VMEM((TILE, WIDTH), F32)],
+        scratch_shapes=[pltpu.VMEM((TILE, WIDTH), F32), pltpu.VMEM((6 * LANE, WIDTH), BF)],
         cost_estimate=pl.CostEstimate(
             flops=10_000_000_000, bytes_accessed=10_000_000, transcendentals=0
         ),
         name="attention",
-    )(words, counts, own, other, gain, w_pad)
+    )(words, counts, own, other, gain, w_heads)
 
 
 def backward_kernel(
@@ -233,12 +244,16 @@
     in_own_ref,
     in_other_ref,
     gain_term,
+    w_pad,
+    wout_pad,
 ):
     step = pl.program_id(0)
 
     @pl.when(step == 0)
     def _():
         gain_term[...] = jnp.zeros_like(gain_term)
+        padded_heads(wout_pad, wout_ref)
+        padded_heads(w_pad, w_ref)
 
     @pl.when(step < IMG)
     def _():
@@ -249,7 +264,7 @@
             [jnp.where(first, own, other), jnp.where(first, other, own)], axis=0
         )
         upstream_ref[...] = upstream
-        mixed_grads = dot(upstream, wout_ref[...], 1, 1).astype(BF)
+        mixed_grads = dot(upstream, wout_pad[...], 1, 1).astype(BF)
         pieces = []
         for head in range(2):
             query, key, value = (
@@ -266,7 +281,7 @@
             pieces.append(dot(probability.astype(BF), mixed_grad, 0, 0))
         packed_grad_ref[...] = shifted_sum(pieces, 512)[:, :480].astype(BF)
         wide = jnp.concatenate([piece.astype(BF) for piece in pieces], axis=1)
-        in_part = dot(wide, w_ref[...], 1, 0).astype(BF)
+        in_part = dot(wide, w_pad[...], 1, 0).astype(BF)
         gain_term[...] += jnp.sum(
             in_part.astype(F32) * normed_ref[...].astype(F32), axis=0, keepdims=True
         )
@@ -283,7 +298,7 @@
             in_other_ref[peer, 0] = plane
 
 
-def backward(words, own, other, wout_pad, w_pad, packed, prob, normed):
+def backward(words, own, other, w_out, w_heads, packed, prob, normed):
     def image(i):
         return jnp.minimum(i, IMG - 1)
 
@@ -303,8 +318,8 @@
             smem(),
             quarter,
             quarter,
-            pl.BlockSpec((2 * LANE, WIDTH), lambda i: (0, 0)),
-            pl.BlockSpec((6 * LANE, WIDTH), lambda i: (0, 0)),
+            pl.BlockSpec((2 * HEAD, WIDTH), lambda i: (0, 0)),
+            pl.BlockSpec((6 * HEAD, WIDTH), lambda i: (0, 0)),
             pl.BlockSpec((TILE, 6 * LANE), lambda i: (image(i), 0)),
             pl.BlockSpec((1, 2, TILE, TILE), lambda i: (image(i), 0, 0, 0)),
             rows,
@@ -315,37 +330,52 @@
             plane,
             plane,
         ),
-        scratch_shapes=[pltpu.VMEM((1, WIDTH), F32)],
+        scratch_shapes=[
+            pltpu.VMEM((1, WIDTH), F32),
+            pltpu.VMEM((6 * LANE, WIDTH), BF),
+            pltpu.VMEM((2 * LANE, WIDTH), BF),
+        ],
         cost_estimate=pl.CostEstimate(
             flops=10_000_000_000, bytes_accessed=10_000_000, transcendentals=0
         ),
         name="backward",
-    )(words, own, other, wout_pad, w_pad, packed, prob, normed)
-
-
-def weights_kernel(normed_ref, upstream_ref, packed_grad_ref, mixed_ref, out_ref):
+    )(words, own, other, w_out, w_heads, packed, prob, normed)
+
+
+def weights_kernel(
+    words_ref, normed_ref, upstream_ref, packed_grad_ref, mixed_ref, *out_refs_and_scratch
+):
+    *out_refs, scratch = out_refs_and_scratch
     qkv = dot(normed_ref[...], packed_grad_ref[...], 0, 0)
     out = dot(upstream_ref[...], mixed_ref[...], 0, 0)
-    out_ref[...] = jnp.concatenate([qkv, out], axis=1).astype(BF)
-
-
-def weight_terms(normed, upstream, packed_grad, mixed):
+    term = jnp.concatenate([qkv, out], axis=1)
+    for at in range(16):
+        scratch[at] = term[at * 40 : (at + 1) * 40].astype(BF)
+    for by, out_ref in enumerate(out_refs):
+        near = lax.rem(words_ref[3] + by, 4)
+        for far in range(4):
+            out_ref[far] = scratch[far * 4 + near]
+
+
+def weight_terms(words, normed, upstream, packed_grad, mixed):
     return pl.pallas_call(
         weights_kernel,
         grid=(2,),
-        out_shape=jax.ShapeDtypeStruct((WIDTH, 640), BF),
+        out_shape=(jax.ShapeDtypeStruct((8, 40, 640), BF),) * 4,
         in_specs=[
+            smem(),
             pl.BlockSpec((ROWS, 640), lambda i: (0, i)),
             pl.BlockSpec((ROWS, 640), lambda i: (0, i)),
             pl.BlockSpec((ROWS, 6 * HEAD), lambda i: (0, 0)),
             pl.BlockSpec((ROWS, 2 * HEAD), lambda i: (0, 0)),
         ],
-        out_specs=pl.BlockSpec((640, 640), lambda i: (i, 0)),
+        out_specs=(pl.BlockSpec((4, 40, 640), lambda i: (i, 0, 0)),) * 4,
+        scratch_shapes=[pltpu.VMEM((16, 40, 640), BF)],
         cost_estimate=pl.CostEstimate(
             flops=4_000_000_000, bytes_accessed=6_000_000, transcendentals=0
         ),
         name="weight_terms",
-    )(normed, upstream, packed_grad, mixed)
+    )(words, normed, upstream, packed_grad, mixed)
 
 
 def norm_back_kernel(arrived_ref, block_ref, upstream_ref, gain_ref, out_ref, term_ref):
@@ -395,16 +425,18 @@
     return lax.optimization_barrier((value, *earlier))[0]
 
 
-def near_sum(term, columns):
+def rows_along(term, columns):
     blocks = term.reshape(8, 4, -1, columns)
     here = lax.axis_index("x")
-
-    def rows_of(at):
-        return lax.dynamic_index_in_dim(blocks, lax.rem(here + at, 4), 1, keepdims=False)
-
-    got = [shifted(rows_of(at), "x", at) for at in (2, 1, 3)]
-    own = rows_of(0)
-    total = own.astype(F32)
+    return [
+        lax.dynamic_index_in_dim(blocks, lax.rem(here + at, 4), 1, keepdims=False)
+        for at in range(4)
+    ]
+
+
+def near_sum(parts):
+    got = [shifted(parts[at], "x", at) for at in (2, 1, 3)]
+    total = parts[0].astype(F32)
     for rows in got:
         total = total + rows.astype(F32)
     return total.astype(BF)
@@ -414,7 +446,7 @@
     device = lax.axis_index(ENC)
     core = lax.axis_index("c")
     place = core * 4 + lax.axis_index("y")
-    words = jnp.stack([core, place, lax.axis_index("y")]).astype(jnp.int32)
+    words = jnp.stack([core, place, lax.axis_index("y"), lax.axis_index("x")]).astype(jnp.int32)
     place_word = place.reshape(1).astype(jnp.int32)
     gain = ln1_gain.reshape(1, WIDTH)
     columns = grad_rows.shape[1]
@@ -447,23 +479,21 @@
     proj_term = dot(kept_rows, grad_rows, 0, 0).astype(BF)
     arrived = after(arrived, proj_term)
     pieces = spread(place_word, own_counts, arrived)
-    proj_near = near_sum(proj_term, columns)
+    proj_near = near_sum(rows_along(proj_term, columns))
 
     share = after(block_in.T, arrived)
-    block_own = jnp.stack([share] + [shifted(share, "y", at) for at in (1, 2, 3)])
+    shares = [share] + [shifted(share, "y", at) for at in (1, 2, 3)]
+    block_own = jnp.stack(shares)
     block_other = swapped(block_own)
 
-    w_pad = jnp.pad(w_qkv.transpose(1, 2, 0).reshape(6, HEAD, WIDTH), ((0, 0), (0, 48), (0, 0)))
-    w_pad = w_pad.reshape(6 * LANE, WIDTH)
-    wout_pad = jnp.pad(w_out.reshape(2, HEAD, WIDTH), ((0, 0), (0, 48), (0, 0)))
-    wout_pad = wout_pad.reshape(2 * LANE, WIDTH)
+    w_heads = w_qkv.transpose(1, 2, 0).reshape(6 * HEAD, WIDTH)
     normed_in, normed, block_rows, packed, prob, mixed = attention(
-        words, arrived_counts, block_own, block_other, gain, w_pad
+        words, arrived_counts, block_own, block_other, gain, w_heads
     )
 
     passing = exchanged(pieces, ENC)
     passing = forwarded(source_of, passing)
-    landed = after(exchanged(passing, ENC), prob)
+    landed = exchanged(passing, ENC)
     upstream_rows, copies = collected(landed)
     half_own = exchanged(copies.reshape(4, 80, WIDTH), "y").reshape(4, IMG, 16, WIDTH)
     half_other = swapped(half_own)
@@ -471,15 +501,15 @@
     proj_far = exchanged(after(proj_near, half_own), "z")
 
     upstream, packed_grad, in_own, in_other = backward(
-        words, half_own, half_other, wout_pad, w_pad, packed, prob, normed
+        words, half_own, half_other, w_out, w_heads, packed, prob, normed
     )
     in_got = swapped(in_other)
-    terms = weight_terms(normed_in, upstream, packed_grad, mixed)
+    terms = weight_terms(words, normed_in, upstream, packed_grad, mixed)
     in_pair = (in_own.astype(F32) + in_got.astype(F32)).astype(BF)
     in_pair, proj_far = lax.optimization_barrier((in_pair, proj_far))
     grad_proj = summed(proj_far)
     in_arrived = exchanged(in_pair.reshape(4, 96, WIDTH), "y").reshape(4, IMG + 1, 16, WIDTH)
-    term_near = near_sum(terms, 640)
+    term_near = near_sum(terms)
     shares, gain_term = norm_back(in_arrived, block_rows, upstream_rows, gain)
     shares = exchanged(shares, TP)
     grad_input = shares.reshape(4, 2, IMG, 16, 160).transpose(2, 1, 0, 3, 4)

time: 256 us -> 233 us (0.910)
  blocking collectives: 14 us -> 0 us
  waiting for transfers between devices: 94.2 us -> 85.8 us
  starting transfers between devices: 62.9 us -> 68.6 us
  local copies, waits for them, and re-layouts: 18.5 us -> 13.2 us
    ppermute x12, waiting for transfers between devices: 39.6 us -> 24.5 us  [shifted(): return lax.ppermute(values, axis, pairs)]
    all_to_all x1 -> x0, blocking collectives: 14 us -> none  [exchanged(): return lax.all_to_all(blocks, axis, split_axis=0, concat_axis=0, tiled=True)]
    all_to_all x7 -> x8, waiting for transfers between devices: 42.7 us -> 49.4 us  [exchanged(): return lax.all_to_all(blocks, axis, split_axis=0, concat_axis=0, tiled=True)]
    pad x2 -> x0, local copies, waits for them, and re-layouts: 4.89 us -> none  [the longest x1 2.73 us: shards(): jnp.pad(w_qkv.transpose(1, 2, 0).reshape(6, HEAD, WIDTH), ((0, 0), (0, 48...]
    all_to_all x7 -> x8, starting transfers between devices: 40.9 us -> 45.3 us  [exchanged(): return lax.all_to_all(blocks, axis, split_axis=0, concat_axis=0, tiled=True)]
  transfers between devices with their start and end apart: 26 -> 27, of which waited for: 16 -> 17; matrix products, arithmetic and copies ran while one was open for 12% -> 11% of each run, Pallas kernels for 14% -> 14%
where the time goes in v2:
time: 233 us; the launch traced here: 230 us
  waiting for transfers between devices  85.8 us (37%)
  starting transfers between devices  68.6 us (29%)
  Pallas kernels  37 us (16%)
  local copies, waits for them, and re-layouts  13.2 us (6%)
  other arithmetic  12.9 us (6%)
  matrix products  11.7 us (5%)
    all_to_all x8, waiting for transfers between devices, exchanged(): return lax.all_to_all(blocks, axis, split_axis=0, concat_axis=0, tiled=True)  49.4 us
    all_to_all x8, starting transfers between devices, exchanged(): return lax.all_to_all(blocks, axis, split_axis=0, concat_axis=0, tiled=True)  45.3 us
    ppermute x12, waiting for transfers between devices, shifted(): return lax.ppermute(values, axis, pairs)  24.5 us
    ppermute x12, starting transfers between devices, shifted(): return lax.ppermute(values, axis, pairs)  21.4 us
    pallas_call x1, Pallas kernels, backward(): pl.pallas_call(backward_kernel, grid=(IMG + 1,), out_shape=(jax.ShapeDtyp...  11.8 us
    dot_general x3, matrix products, dot(): lax.dot_general(left, right, (((dim_left,), (dim_right,)), ((), ())), pre...  11.7 us
    pallas_call x1, Pallas kernels, attention(): pl.pallas_call(attention_kernel, grid=(IMG,), out_shape=(jax.ShapeDtypeSt...  11.7 us
    ppermute x3, waiting for transfers between devices, shards(): got = lax.ppermute(sent, 'z', tuple(((i, i ^ reach) for i in range(8))))  9.53 us
  transfers between devices with their start and end apart: 27, of which 17 were waited for; matrix products, arithmetic and copies ran while one was open for 11% of the time, Pallas kernels for 14%

profile of v2, /device:TPU:8, one launch (start us, length us, event | category | flops | bytes accessed | tf_op | source)
XLA Modules:
  0.0 230.1 jit_solution(5568343683253762537)
XLA Ops:
  3.4 3.0 %convolution_convert_fusion.1 = bf16[320,1280]{1,0:T(8,128)(2,1)} fusion(bf16[1280,1024]{1,0:T(8,128)(2,1)S(1)} %copy-done, bf16[2,320,1024]{2,1,0:T(8,128)(2,1)} %bitcast.80, s32[]{:T(128)S(6)} %select_n.123), kind=kOutput, calls=%fused_computation.1 | convolution fusion | flops 839270400 | bytes 4096004 | tf_op jit(solution)/shard_map/dot_general | solution.py:46
  8.9 3.0 %add_convert_fusion.1 = bf16[320,1280]{1,0:T(8,128)(2,1)} fusion(bf16[320,1280]{1,0:T(8,128)(2,1)S(1)} %collective-permute-done, bf16[1280,1024]{1,0:T(8,128)(2,1)S(1)} %copy-done, bf16[2,320,1024]{2,1,0:T(8,128)(2,1)} %bitcast.81, s32[]{:T(128)S(6)} %select_n.122), kind=kOutput, calls=%fused_computation.4 | convolution fusion | flops 840089600 | bytes 4915204 | tf_op jit(solution)/shard_map/dot_general | solution.py:46
  12.0 5.6 %all-to-all-start = ((bf16[4,80,1280]{2,1,0:T(8,128)(2,1)}), bf16[4,80,1280]{2,1,0:T(8,128)(2,1)S(1)}, u32[]{:S(2)}, u32[]{:S(2)}) async-start(bf16[4,80,1280]{2,1,0:T(8,128)(2,1)} %bitcast.89), calls=%async_computation | async-start | bytes 1638400 | tf_op jit(solution)/shard_map/all_to_all | solution.py:33
  17.7 5.6 %convolution_convert_fusion = bf16[1280,1024]{1,0:T(8,128)(2,1)} fusion(bf16[640,1024]{1,0:T(8,128)(2,1)} %param.9, bf16[640,1280]{1,0:T(8,128)(2,1)} %param.10, pred[640]{0:T(1024)(128)(4,1)S(1)} %fusion.14), kind=kOutput, calls=%fused_computation | convolution fusion | flops 1679851520 | bytes 5571200 | tf_op jit(solution)/shard_map/dot_general | solution.py:46
  23.3 6.0 %all-to-all-done = bf16[4,80,1280]{2,1,0:T(8,128)(2,1)S(1)} async-done(((bf16[4,80,1280]{2,1,0:T(8,128)(2,1)}), bf16[4,80,1280]{2,1,0:T(8,128)(2,1)S(1)}, u32[]{:S(2)}, u32[]{:S(2)}) %all-to-all-start) | async-done | bytes 819232 | tf_op jit(solution)/shard_map/all_to_all | solution.py:33
  32.3 10.5 %all-to-all-start.1 = ((bf16[32,5,8,128]{3,2,1,0:T(8,128)(2,1)}), bf16[32,5,8,128]{3,2,1,0:T(8,128)(2,1)S(1)}, u32[]{:S(2)}, u32[]{:S(2)}) async-start(bf16[32,5,8,128]{3,2,1,0:T(8,128)(2,1)} %spread.1), calls=%async_computation.1 | async-start | bytes 655360 | tf_op jit(solution)/shard_map/all_to_all | solution.py:33
  44.1 12.1 %all-to-all-done.1 = bf16[32,5,8,128]{3,2,1,0:T(8,128)(2,1)S(1)} async-done(((bf16[32,5,8,128]{3,2,1,0:T(8,128)(2,1)}), bf16[32,5,8,128]{3,2,1,0:T(8,128)(2,1)S(1)}, u32[]{:S(2)}, u32[]{:S(2)}) %all-to-all-start.1) | async-done | bytes 327712 | tf_op jit(solution)/shard_map/all_to_all | solution.py:33
  59.0 3.9 %all-to-all-start.2 = ((bf16[32,5,8,128]{3,2,1,0:T(8,128)(2,1)}), bf16[32,5,8,128]{3,2,1,0:T(8,128)(2,1)S(1)}, u32[]{:S(2)}, u32[]{:S(2)}) async-start(bf16[32,5,8,128]{3,2,1,0:T(8,128)(2,1)} %bitcast.82), calls=%async_computation.2 | async-start | bytes 655360 | tf_op jit(solution)/shard_map/all_to_all | solution.py:33
  63.0 3.5 %collective-permute-start.3 = (bf16[160,640]{1,0:T(8,128)(2,1)S(1)}, bf16[160,640]{1,0:T(8,128)(2,1)S(1)}, u32[]{:S(2)}, u32[]{:S(2)}) collective-permute-start(bf16[160,640]{1,0:T(8,128)(2,1)S(1)} %bitcast.91), channel_id=1, source_target_pairs={{0,4},{2,6},{4,0},{6,2},{1,5},{3,7},{5,1},{7,3},{8,12},{10,14},{12... | collective-permute-start | bytes 614408 | tf_op jit(solution)/shard_map/ppermute | solution.py:38
  67.0 3.6 %collective-permute-done.2 = bf16[160,640]{1,0:T(8,128)(2,1)S(1)} collective-permute-done((bf16[160,640]{1,0:T(8,128)(2,1)S(1)}, bf16[160,640]{1,0:T(8,128)(2,1)S(1)}, u32[]{:S(2)}, u32[]{:S(2)}) %collective-permute-start.2) | collective-permute-done | bytes 204832 | tf_op jit(solution)/shard_map/ppermute | solution.py:38
  79.0 4.9 %all-to-all-start.3 = ((bf16[4,80,1280]{2,1,0:T(8,128)(2,1)}), bf16[4,80,1280]{2,1,0:T(8,128)(2,1)S(1)}, u32[]{:S(2)}, u32[]{:S(2)}) async-start(bf16[4,80,1280]{2,1,0:T(8,128)(2,1)} %bitcast.88), calls=%async_computation.3 | async-start | bytes 1638400 | tf_op jit(solution)/shard_map/all_to_all | solution.py:33
  95.6 11.7 %attention.1 = (bf16[640,1280]{1,0:T(8,128)(2,1)}, bf16[640,1280]{1,0:T(8,128)(2,1)}, bf16[5,16,1280]{2,1,0:T(8,128)(2,1)}, bf16[640,768]{1,0:T(8,128)(2,1)}, f3...) custom-call(s32[4]{0:T(128)} %pad_add_fusion.words_ref, s32[5]{0:T(128)} %dynamic_slice.43.counts_ref, ...), custom_call_target="tpu_custom_call" | custom-call | flops 10000000000 | bytes 10000000 | tf_op jit(solution)/shard_map/attention/pallas_call | solution.py:198
  107.3 11.8 %backward.1 = (bf16[640,1280]{1,0:T(8,128)(2,1)}, bf16[640,480]{1,0:T(8,128)(2,1)}, bf16[4,6,16,1280]{3,2,1,0:T(8,128)(2,1)}, bf16[4,6,16,1280]{3,2,1,0:T(8,128)(2,1)}) custom-call(s32[4]{0:T(128)} %pad_add_fusion.words_ref, bf16[4,5,16,1280]{3,2,1,0:T(8,128)(2,1)} %bitcast.87, bf16[4,5,16,1280]{3,2,1,0:T(8,128)(2,1)} %collective-permute-done.1.other_ref, ...), custom_call_target="tpu_custom_call" | custom-call | flops 10000000000 | bytes 10000000 | tf_op jit(solution)/shard_map/backward/pallas_call | solution.py:308
  123.9 6.7 %all-to-all-start.4 = ((bf16[8,40,1024]{2,1,0:T(8,128)(2,1)}), bf16[8,40,1024]{2,1,0:T(8,128)(2,1)S(1)}, u32[]{:S(2)}, u32[]{:S(2)}) async-start(bf16[8,40,1024]{2,1,0:T(8,128)(2,1)} %fusion.4), calls=%async_computation.4 | async-start | bytes 1310720 | tf_op jit(solution)/shard_map/all_to_all | solution.py:33
  133.2 17.8 %all-to-all-done.4 = bf16[8,40,1024]{2,1,0:T(8,128)(2,1)S(1)} async-done(((bf16[8,40,1024]{2,1,0:T(8,128)(2,1)}), bf16[8,40,1024]{2,1,0:T(8,128)(2,1)S(1)}, u32[]{:S(2)}, u32[]{:S(2)}) %all-to-all-start.4) | async-done | bytes 655392 | tf_op jit(solution)/shard_map/all_to_all | solution.py:33
  151.0 4.8 %all-to-all-start.5 = ((bf16[4,96,1280]{2,1,0:T(8,128)(2,1)}), bf16[4,96,1280]{2,1,0:T(8,128)(2,1)}, u32[]{:S(2)}, u32[]{:S(2)}) async-start(bf16[4,96,1280]{2,1,0:T(8,128)(2,1)} %bitcast.75), calls=%async_computation.5 | async-start | bytes 1966080 | tf_op jit(solution)/shard_map/all_to_all | solution.py:33
  155.8 4.9 %weight_terms.1 = (bf16[8,40,640]{2,1,0:T(8,128)(2,1)}, bf16[8,40,640]{2,1,0:T(8,128)(2,1)}, bf16[8,40,640]{2,1,0:T(8,128)(2,1)}, bf16[8,40,640]{2,1,0:T(8,128)(2,1)}) custom-call(s32[4]{0:T(128)} %pad_add_fusion.words_ref, bf16[640,1280]{1,0:T(8,128)(2,1)} %get-tuple-element.44.normed_ref, bf16[640,1280]{1,0:T(8,128)(2,1)} %get-tuple-element.45.upstream_ref, ...), custom_call_target="tpu_custom_call" | custom-call | flops 4000000000 | bytes 6000000 | tf_op jit(solution)/shard_map/weight_terms/pallas_call | solution.py:361
  166.5 8.3 %collective-permute-done.10 = bf16[8,40,640]{2,1,0:T(8,128)(2,1)S(1)} collective-permute-done((bf16[8,40,640]{2,1,0:T(8,128)(2,1)}, bf16[8,40,640]{2,1,0:T(8,128)(2,1)S(1)}, u32[]{:S(2)}, u32[]{:S(2)}) %collective-permute-start.10) | collective-permute-done | bytes 409632 | tf_op jit(solution)/shard_map/ppermute | solution.py:38
  174.8 7.2 %collective-permute-done.11 = bf16[8,40,640]{2,1,0:T(8,128)(2,1)S(1)} collective-permute-done((bf16[8,40,640]{2,1,0:T(8,128)(2,1)}, bf16[8,40,640]{2,1,0:T(8,128)(2,1)S(1)}, u32[]{:S(2)}, u32[]{:S(2)}) %collective-permute-start.11) | collective-permute-done | bytes 409632 | tf_op jit(solution)/shard_map/ppermute | solution.py:38
  184.0 4.1 %all-to-all-start.7 = ((bf16[8,40,640]{2,1,0:T(8,128)(2,1)}), bf16[8,40,640]{2,1,0:T(8,128)(2,1)}, u32[]{:S(2)}, u32[]{:S(2)}) async-start(bf16[8,40,640]{2,1,0:T(8,128)(2,1)} %add_convert_fusion.2), calls=%async_computation.7 | async-start | bytes 819200 | tf_op jit(solution)/shard_map/all_to_all | solution.py:33
  197.9 5.7 %all-to-all-done.7 = bf16[8,40,640]{2,1,0:T(8,128)(2,1)} async-done(((bf16[8,40,640]{2,1,0:T(8,128)(2,1)}), bf16[8,40,640]{2,1,0:T(8,128)(2,1)}, u32[]{:S(2)}, u32[]{:S(2)}) %all-to-all-start.7) | async-done | bytes 409632 | tf_op jit(solution)/shard_map/all_to_all | solution.py:33
  205.9 6.5 %collective-permute-done.16 = bf16[4,40]{1,0:T(4,128)(2,1)S(1)} collective-permute-done((bf16[4,40]{1,0:T(4,128)(2,1)S(1)}, bf16[4,40]{1,0:T(4,128)(2,1)S(1)}, u32[]{:S(2)}, u32[]{:S(2)}) %collective-permute-start.16) | collective-permute-done | bytes 352 | tf_op jit(solution)/shard_map/ppermute | solution.py:534
  217.6 4.8 %all-to-all-start.6 = ((bf16[8,80,160]{2,1,0:T(8,128)(2,1)}), bf16[8,80,160]{2,1,0:T(8,128)(2,1)S(1)}, u32[]{:S(2)}, u32[]{:S(2)}) async-start(bf16[8,80,160]{2,1,0:T(8,128)(2,1)} %get-tuple-element.42), calls=%async_computation.6 | async-start | bytes 655360 | tf_op jit(solution)/shard_map/all_to_all | solution.py:33
  223.0 6.2 %all-to-all-done.6 = bf16[8,80,160]{2,1,0:T(8,128)(2,1)S(1)} async-done(((bf16[8,80,160]{2,1,0:T(8,128)(2,1)}), bf16[8,80,160]{2,1,0:T(8,128)(2,1)S(1)}, u32[]{:S(2)}, u32[]{:S(2)}) %all-to-all-start.6) | async-done | bytes 204832 | tf_op jit(solution)/shard_map/all_to_all | solution.py:33
  (101 shorter events, 66.9 us)
Async XLA Ops:
  12.0 17.4 %all-to-all-start = ((bf16[4,80,1280]{2,1,0:T(8,128)(2,1)}), bf16[4,80,1280]{2,1,0:T(8,128)(2,1)S(1)}, u32[]{:S(2)}, u32[]{:S(2)}) async-start(bf16[4,80,1280]{2,1,0:T(8,128)(2,1)} %bitcast.89), calls=%async_computation | async-start | bytes 1638400 | tf_op jit(solution)/shard_map/all_to_all | solution.py:33
  32.3 23.9 %all-to-all-start.1 = ((bf16[32,5,8,128]{3,2,1,0:T(8,128)(2,1)}), bf16[32,5,8,128]{3,2,1,0:T(8,128)(2,1)S(1)}, u32[]{:S(2)}, u32[]{:S(2)}) async-start(bf16[32,5,8,128]{3,2,1,0:T(8,128)(2,1)} %spread.1), calls=%async_computation.1 | async-start | bytes 655360 | tf_op jit(solution)/shard_map/all_to_all | solution.py:33
  59.0 17.2 %all-to-all-start.2 = ((bf16[32,5,8,128]{3,2,1,0:T(8,128)(2,1)}), bf16[32,5,8,128]{3,2,1,0:T(8,128)(2,1)S(1)}, u32[]{:S(2)}, u32[]{:S(2)}) async-start(bf16[32,5,8,128]{3,2,1,0:T(8,128)(2,1)} %bitcast.82), calls=%async_computation.2 | async-start | bytes 655360 | tf_op jit(solution)/shard_map/all_to_all | solution.py:33
  62.9 7.8 %collective-permute-start.2 = (bf16[160,640]{1,0:T(8,128)(2,1)S(1)}, bf16[160,640]{1,0:T(8,128)(2,1)S(1)}, u32[]{:S(2)}, u32[]{:S(2)}) collective-permute-start(bf16[160,640]{1,0:T(8,128)(2,1)S(1)} %bitcast.90), channel_id=1, source_target_pairs={{0,2},{2,4},{4,6},{6,0},{1,3},{3,5},{5,7},{7,1},{8,10},{10,12},{12... | collective-permute-start | bytes 614408 | tf_op jit(solution)/shard_map/ppermute | solution.py:38
  63.0 9.3 %collective-permute-start.3 = (bf16[160,640]{1,0:T(8,128)(2,1)S(1)}, bf16[160,640]{1,0:T(8,128)(2,1)S(1)}, u32[]{:S(2)}, u32[]{:S(2)}) collective-permute-start(bf16[160,640]{1,0:T(8,128)(2,1)S(1)} %bitcast.91), channel_id=1, source_target_pairs={{0,4},{2,6},{4,0},{6,2},{1,5},{3,7},{5,1},{7,3},{8,12},{10,14},{12... | collective-permute-start | bytes 614408 | tf_op jit(solution)/shard_map/ppermute | solution.py:38
  66.5 7.9 %collective-permute-start.4 = (bf16[160,640]{1,0:T(8,128)(2,1)S(1)}, bf16[160,640]{1,0:T(8,128)(2,1)S(1)}, u32[]{:S(2)}, u32[]{:S(2)}) collective-permute-start(bf16[160,640]{1,0:T(8,128)(2,1)S(1)} %bitcast.92), channel_id=1, source_target_pairs={{0,6},{2,0},{4,2},{6,4},{1,7},{3,1},{5,3},{7,5},{8,14},{10,8},{12,... | collective-permute-start | bytes 614408 | tf_op jit(solution)/shard_map/ppermute | solution.py:38
  75.5 20.1 %collective-permute-start.5 = (bf16[4,160,640]{2,1,0:T(8,128)(2,1)}, bf16[4,160,640]{2,1,0:T(8,128)(2,1)}, u32[]{:S(2)}, u32[]{:S(2)}) collective-permute-start(bf16[4,160,640]{2,1,0:T(8,128)(2,1)} %pad_maximum_fusion.own_ref), channel_id=1, source_target_pairs={{0,1},{1,0},{2,3},{3,2},{4,5},{5,4},{6,7},{7,6},{8,9},{9,8},{10,11... | collective-permute-start | bytes 2457608 | tf_op jit(solution)/shard_map/ppermute | solution.py:42
  79.0 16.6 %all-to-all-start.3 = ((bf16[4,80,1280]{2,1,0:T(8,128)(2,1)}), bf16[4,80,1280]{2,1,0:T(8,128)(2,1)S(1)}, u32[]{:S(2)}, u32[]{:S(2)}) async-start(bf16[4,80,1280]{2,1,0:T(8,128)(2,1)} %bitcast.88), calls=%async_computation.3 | async-start | bytes 1638400 | tf_op jit(solution)/shard_map/all_to_all | solution.py:33
  88.5 30.9 %collective-permute-start.7 = (bf16[8,40,1024]{2,1,0:T(8,128)(2,1)}, bf16[8,40,1024]{2,1,0:T(8,128)(2,1)}, u32[]{:S(2)}, u32[]{:S(2)}) collective-permute-start(bf16[8,40,1024]{2,1,0:T(8,128)(2,1)} %get-tuple-element.70), channel_id=1, source_target_pairs={{0,16},{8,24},{16,0},{24,8},{1,17},{9,25},{17,1},{25,9},{2,18},{10... | collective-permute-start | bytes 1966088 | tf_op jit(solution)/shard_map/ppermute | solution.py:38
  91.4 29.5 %collective-permute-start.8 = (bf16[8,40,1024]{2,1,0:T(8,128)(2,1)}, bf16[8,40,1024]{2,1,0:T(8,128)(2,1)}, u32[]{:S(2)}, u32[]{:S(2)}) collective-permute-start(bf16[8,40,1024]{2,1,0:T(8,128)(2,1)} %get-tuple-element.72), channel_id=1, source_target_pairs={{0,8},{8,16},{16,24},{24,0},{1,9},{9,17},{17,25},{25,1},{2,10},{10... | collective-permute-start | bytes 1966088 | tf_op jit(solution)/shard_map/ppermute | solution.py:38
  91.9 29.0 %collective-permute-start.9 = (bf16[8,40,1024]{2,1,0:T(8,128)(2,1)}, bf16[8,40,1024]{2,1,0:T(8,128)(2,1)}, u32[]{:S(2)}, u32[]{:S(2)}) collective-permute-start(bf16[8,40,1024]{2,1,0:T(8,128)(2,1)} %get-tuple-element.71), channel_id=1, source_target_pairs={{0,24},{8,0},{16,8},{24,16},{1,25},{9,1},{17,9},{25,17},{2,26},{10... | collective-permute-start | bytes 1966088 | tf_op jit(solution)/shard_map/ppermute | solution.py:38
  95.6 11.7 %collective-permute-start.1 = (bf16[4,5,16,1280]{3,2,1,0:T(8,128)(2,1)S(1)}, bf16[4,5,16,1280]{3,2,1,0:T(8,128)(2,1)}, u32[]{:S(2)}, u32[]{:S(2)}) collective-permute-start(bf16[4,5,16,1280]{3,2,1,0:T(8,128)(2,1)S(1)} %bitcast.86), channel_id=1, source_target_pairs={{0,1},{1,0},{2,3},{3,2},{4,5},{5,4},{6,7},{7,6},{8,9},{9,8},{10,11... | collective-permute-start | bytes 2457608 | tf_op jit(solution)/shard_map/ppermute | solution.py:42
  119.1 11.5 %collective-permute-start.6 = (bf16[4,6,16,1280]{3,2,1,0:T(8,128)(2,1)}, bf16[4,6,16,1280]{3,2,1,0:T(8,128)(2,1)}, u32[]{:S(2)}, u32[]{:S(2)}) collective-permute-start(bf16[4,6,16,1280]{3,2,1,0:T(8,128)(2,1)} %get-tuple-element.37), channel_id=1, source_target_pairs={{0,1},{1,0},{2,3},{3,2},{4,5},{5,4},{6,7},{7,6},{8,9},{9,8},{10,11... | collective-permute-start | bytes 2949128 | tf_op jit(solution)/shard_map/ppermute | solution.py:42
  123.9 27.1 %all-to-all-start.4 = ((bf16[8,40,1024]{2,1,0:T(8,128)(2,1)}), bf16[8,40,1024]{2,1,0:T(8,128)(2,1)S(1)}, u32[]{:S(2)}, u32[]{:S(2)}) async-start(bf16[8,40,1024]{2,1,0:T(8,128)(2,1)} %fusion.4), calls=%async_computation.4 | async-start | bytes 1310720 | tf_op jit(solution)/shard_map/all_to_all | solution.py:33
  151.0 33.0 %all-to-all-start.5 = ((bf16[4,96,1280]{2,1,0:T(8,128)(2,1)}), bf16[4,96,1280]{2,1,0:T(8,128)(2,1)}, u32[]{:S(2)}, u32[]{:S(2)}) async-start(bf16[4,96,1280]{2,1,0:T(8,128)(2,1)} %bitcast.75), calls=%async_computation.5 | async-start | bytes 1966080 | tf_op jit(solution)/shard_map/all_to_all | solution.py:33
  160.7 14.1 %collective-permute-start.10 = (bf16[8,40,640]{2,1,0:T(8,128)(2,1)}, bf16[8,40,640]{2,1,0:T(8,128)(2,1)S(1)}, u32[]{:S(2)}, u32[]{:S(2)}) collective-permute-start(bf16[8,40,640]{2,1,0:T(8,128)(2,1)} %get-tuple-element.49), channel_id=1, source_target_pairs={{0,16},{8,24},{16,0},{24,8},{1,17},{9,25},{17,1},{25,9},{2,18},{10... | collective-permute-start | bytes 1228808 | tf_op jit(solution)/shard_map/ppermute | solution.py:38
  163.3 18.8 %collective-permute-start.11 = (bf16[8,40,640]{2,1,0:T(8,128)(2,1)}, bf16[8,40,640]{2,1,0:T(8,128)(2,1)S(1)}, u32[]{:S(2)}, u32[]{:S(2)}) collective-permute-start(bf16[8,40,640]{2,1,0:T(8,128)(2,1)} %get-tuple-element.50), channel_id=1, source_target_pairs={{0,8},{8,16},{16,24},{24,0},{1,9},{9,17},{17,25},{25,1},{2,10},{10... | collective-permute-start | bytes 1228808 | tf_op jit(solution)/shard_map/ppermute | solution.py:38
  164.2 17.8 %collective-permute-start.12 = (bf16[8,40,640]{2,1,0:T(8,128)(2,1)}, bf16[8,40,640]{2,1,0:T(8,128)(2,1)S(1)}, u32[]{:S(2)}, u32[]{:S(2)}) collective-permute-start(bf16[8,40,640]{2,1,0:T(8,128)(2,1)} %get-tuple-element.51), channel_id=1, source_target_pairs={{0,24},{8,0},{16,8},{24,16},{1,25},{9,1},{17,9},{25,17},{2,26},{10... | collective-permute-start | bytes 1228808 | tf_op jit(solution)/shard_map/ppermute | solution.py:38
  184.0 19.6 %all-to-all-start.7 = ((bf16[8,40,640]{2,1,0:T(8,128)(2,1)}), bf16[8,40,640]{2,1,0:T(8,128)(2,1)}, u32[]{:S(2)}, u32[]{:S(2)}) async-start(bf16[8,40,640]{2,1,0:T(8,128)(2,1)} %add_convert_fusion.2), calls=%async_computation.7 | async-start | bytes 819200 | tf_op jit(solution)/shard_map/all_to_all | solution.py:33
  192.6 12.1 %collective-permute-start.13 = (bf16[1,320]{1,0:T(2,128)(2,1)S(1)}, bf16[1,320]{1,0:T(2,128)(2,1)S(1)}, u32[]{:S(2)}, u32[]{:S(2)}) collective-permute-start(bf16[1,320]{1,0:T(2,128)(2,1)S(1)} %get-tuple-element.73), channel_id=1, source_target_pairs={{0,16},{8,24},{16,0},{24,8},{1,17},{9,25},{17,1},{25,9},{2,18},{10... | collective-permute-start | bytes 1928 | tf_op jit(solution)/shard_map/ppermute | solution.py:38
  194.7 10.0 %collective-permute-start.14 = (bf16[1,320]{1,0:T(2,128)(2,1)S(1)}, bf16[1,320]{1,0:T(2,128)(2,1)S(1)}, u32[]{:S(2)}, u32[]{:S(2)}) collective-permute-start(bf16[1,320]{1,0:T(2,128)(2,1)S(1)} %get-tuple-element.75), channel_id=1, source_target_pairs={{0,8},{8,16},{16,24},{24,0},{1,9},{9,17},{17,25},{25,1},{2,10},{10... | collective-permute-start | bytes 1928 | tf_op jit(solution)/shard_map/ppermute | solution.py:38
  196.1 8.6 %collective-permute-start.15 = (bf16[1,320]{1,0:T(2,128)(2,1)S(1)}, bf16[1,320]{1,0:T(2,128)(2,1)S(1)}, u32[]{:S(2)}, u32[]{:S(2)}) collective-permute-start(bf16[1,320]{1,0:T(2,128)(2,1)S(1)} %get-tuple-element.74), channel_id=1, source_target_pairs={{0,24},{8,0},{16,8},{24,16},{1,25},{9,1},{17,9},{25,17},{2,26},{10... | collective-permute-start | bytes 1928 | tf_op jit(solution)/shard_map/ppermute | solution.py:38
  204.9 7.5 %collective-permute-start.16 = (bf16[4,40]{1,0:T(4,128)(2,1)S(1)}, bf16[4,40]{1,0:T(4,128)(2,1)S(1)}, u32[]{:S(2)}, u32[]{:S(2)}) collective-permute-start(bf16[4,40]{1,0:T(4,128)(2,1)S(1)} %convert_element_type.140), channel_id=1, source_target_pairs={{0,128},{32,160},{64,192},{96,224},{128,0},{160,32},{192,64},{224,... | collective-permute-start | bytes 968 | tf_op jit(solution)/shard_map/ppermute | solution.py:534
  217.6 11.6 %all-to-all-start.6 = ((bf16[8,80,160]{2,1,0:T(8,128)(2,1)}), bf16[8,80,160]{2,1,0:T(8,128)(2,1)S(1)}, u32[]{:S(2)}, u32[]{:S(2)}) async-start(bf16[8,80,160]{2,1,0:T(8,128)(2,1)} %get-tuple-element.42), calls=%async_computation.6 | async-start | bytes 655360 | tf_op jit(solution)/shard_map/all_to_all | solution.py:33
  (13 other events, 103.0 us)

commit v3 on v2

--- a/solution.py
+++ b/solution.py
@@ -69,6 +69,46 @@
             wide = pltpu.roll(wide, HEAD * at, 1)
         total = wide if total is None else total + wide
     return total
+
+
+def half_rows(rows_ref):
+    return jnp.concatenate(
+        [rows_ref[image, 0, near] for near in range(4) for image in range(IMG)], axis=0
+    )
+
+
+def part_kernel(half_ref, rows_ref, w_ref, out_ref):
+    out_ref[...] = dot(half_rows(rows_ref), w_ref[...], 1, 1).astype(BF)
+
+
+def pair_kernel(half_ref, rows_ref, w_ref, got_ref, out_ref):
+    own = dot(half_rows(rows_ref), w_ref[...], 1, 1)
+    out_ref[...] = (own + got_ref[...].astype(F32)).astype(BF)
+
+
+def projected(half, grad_rows, w_proj, got=None):
+    depth = grad_rows.shape[1]
+    rows = grad_rows.reshape(IMG, 2, 4, 16, depth)
+    block = pl.BlockSpec((ROWS // 2, 256), lambda i, half: (0, i))
+    kernel, extra = (part_kernel, ()) if got is None else (pair_kernel, (got,))
+    return pl.pallas_call(
+        kernel,
+        grid_spec=pltpu.PrefetchScalarGridSpec(
+            num_scalar_prefetch=1,
+            grid=(WIDTH // 256,),
+            in_specs=[
+                pl.BlockSpec((IMG, 1, 4, 16, depth), lambda i, half: (0, half[0], 0, 0, 0)),
+                pl.BlockSpec((256, depth), lambda i, half: (i, 0)),
+                *(block for _ in extra),
+            ],
+            out_specs=block,
+        ),
+        out_shape=jax.ShapeDtypeStruct((ROWS // 2, WIDTH), BF),
+        cost_estimate=pl.CostEstimate(
+            flops=1_000_000_000, bytes_accessed=4_000_000, transcendentals=0
+        ),
+        name="projected",
+    )(half, rows, w_proj, *extra)
 
 
 def spread_kernel(place_ref, counts_ref, arrived_ref, out_ref):
@@ -382,9 +422,10 @@
     gain = gain_ref[...]
     results = []
     for image in range(IMG + 1):
-        incoming = arrived_ref[0, image].astype(F32)
+        rows = slice(image * 16, image * 16 + 16)
+        incoming = arrived_ref[0, rows].astype(F32)
         for peer in range(1, 4):
-            incoming = incoming + arrived_ref[peer, image].astype(F32)
+            incoming = incoming + arrived_ref[peer, rows].astype(F32)
         if image == IMG:
             term_ref[...] = incoming[:8]
             continue
@@ -462,14 +503,9 @@
     all_counts = jnp.sum(jnp.where(hits, patch_counts.reshape(1, -1), 0), axis=1)
     arrived_counts = lax.dynamic_slice_in_dim(all_counts, device * IMG, IMG, 0)
 
-    by_place = grad_rows.reshape(IMG, 2, 4, 16, -1).transpose(1, 2, 0, 3, 4)
-    by_place = by_place.reshape(2, ROWS // 2, -1)
-    for_other = lax.dynamic_index_in_dim(by_place, 1 - core, 0, keepdims=False)
-    for_own = lax.dynamic_index_in_dim(by_place, core, 0, keepdims=False)
-    part_other = dot(for_other, w_proj, 1, 1).astype(BF)
-    from_other = swapped(part_other)
-    part_own = dot(for_own, w_proj, 1, 1)
-    pair = (part_own + from_other.astype(F32)).astype(BF)
+    own_half = core.reshape(1).astype(jnp.int32)
+    part_other = projected(1 - own_half, grad_rows, w_proj)
+    pair = projected(own_half, grad_rows, w_proj, swapped(part_other))
     features = after(features, pair)
     arrived = exchanged(pair.reshape(4, 80, WIDTH), "y").reshape(4, IMG, 16, WIDTH)
 
@@ -506,36 +542,28 @@
     in_got = swapped(in_other)
     terms = weight_terms(words, normed_in, upstream, packed_grad, mixed)
     in_pair = (in_own.astype(F32) + in_got.astype(F32)).astype(BF)
+    in_pair = in_pair.reshape(4, 96, WIDTH)
     in_pair, proj_far = lax.optimization_barrier((in_pair, proj_far))
     grad_proj = summed(proj_far)
-    in_arrived = exchanged(in_pair.reshape(4, 96, WIDTH), "y").reshape(4, IMG + 1, 16, WIDTH)
+    in_arrived = exchanged(in_pair, "y")
     term_near = near_sum(terms)
     shares, gain_term = norm_back(in_arrived, block_rows, upstream_rows, gain)
     shares = exchanged(shares, TP)
     grad_input = shares.reshape(4, 2, IMG, 16, 160).transpose(2, 1, 0, 3, 4)
     grad_input = grad_input.reshape(ROWS, 160)
-    last = summed(exchanged(term_near, "z"))
     gain_rows = gain_term[0].astype(BF).reshape(8, 4, 40).transpose(1, 0, 2)
     gain_rows = gain_rows.reshape(4, 1, 320)
     here = lax.axis_index("x")
-
-    def gain_of(at):
-        return lax.dynamic_index_in_dim(gain_rows, lax.rem(here + at, 4), 0, keepdims=False)
-
-    gain_sum = gain_of(0).astype(F32)
-    for at in (2, 1, 3):
-        gain_sum = gain_sum + shifted(gain_of(at), "x", at).astype(F32)
-    gain_sum = gain_sum.reshape(8, 40)
-    far = lax.axis_index("z")
-    for reach in (4, 2, 1):
-        upper = (far // reach) % 2 == 1
-        low, high = gain_sum[:reach], gain_sum[reach:]
-        sent = jnp.where(upper, low, high).astype(BF)
-        got = lax.ppermute(sent, "z", tuple((i, i ^ reach) for i in range(8)))
-        gain_sum = jnp.where(upper, high, low) + got.astype(F32)
+    gain_parts = [
+        lax.dynamic_index_in_dim(gain_rows, lax.rem(here + at, 4), 0, keepdims=False)
+        for at in range(4)
+    ]
+    gain_near = near_sum(gain_parts).reshape(8, 40, 1)
+    last = jnp.concatenate([term_near, jnp.pad(gain_near, ((0, 0), (0, 0), (0, 127)))], axis=2)
+    last = summed(exchanged(last, "z"))
     grad_qkv = last[:, :480].reshape(40, 2, 240)
-    grad_out = last[:, 480:].T
-    grad_ln1 = gain_sum.reshape(40)
+    grad_out = last[:, 480:640].T
+    grad_ln1 = last[:, 640]
     return (grad_input, grad_proj, grad_qkv, grad_out, grad_ln1)
 
 

time: 233 us -> 221 us (0.948)
  Pallas kernels: 37 us -> 47.8 us
  waiting for transfers between devices: 85.8 us -> 77.5 us
  matrix products: 11.7 us -> 5.27 us
  other arithmetic: 12.9 us -> 9.8 us
  starting transfers between devices: 68.6 us -> 65.9 us
    all_to_all x8, waiting for transfers between devices: 49.4 us -> 63.7 us  [exchanged(): return lax.all_to_all(blocks, axis, split_axis=0, concat_axis=0, tiled=True)]
    ppermute x12, waiting for transfers between devices: 24.5 us -> 11.4 us  [shifted(): return lax.ppermute(values, axis, pairs)]
    pallas_call x0 -> x2, Pallas kernels: none -> 10.8 us  [projected(): pl.pallas_call(kernel, grid_spec=pltpu.PrefetchScalarGridSpec(num_scalar_...]
    ppermute x3 -> x0, waiting for transfers between devices: 9.53 us -> none  [shards(): got = lax.ppermute(sent, 'z', tuple(((i, i ^ reach) for i in range(8))))]
    dot_general x3 -> x1, matrix products: 11.7 us -> 5.27 us  [dot(): lax.dot_general(left, right, (((dim_left,), (dim_right,)), ((), ())), pre...]
    transpose x2 -> x1, local copies, waits for them, and re-layouts: 3.4 us -> 0.7 us  [shards(): grad_out = last[:, 480:640].T]
    convert_element_type x2 -> x3, other arithmetic: 4.97 us -> 3.05 us  [near_sum(): return total.astype(BF)]
    unnamed x23 -> x33, local copies, waits for them, and re-layouts: 3.42 us -> 5.29 us
  transfers between devices with their start and end apart: 27 -> 24, of which waited for: 17 -> 13; matrix products, arithmetic and copies ran while one was open for 11% -> 9% of each run, Pallas kernels for 14% -> 15%
where the time goes in v3:
time: 221 us; the launch traced here: 219 us
  waiting for transfers between devices  77.5 us (35%)
  starting transfers between devices  65.9 us (30%)
  Pallas kernels  47.8 us (22%)
  local copies, waits for them, and re-layouts  11.7 us (5%)
  other arithmetic  9.8 us (4%)
  matrix products  5.27 us (2%)
    all_to_all x8, waiting for transfers between devices, exchanged(): return lax.all_to_all(blocks, axis, split_axis=0, concat_axis=0, tiled=True)  63.7 us
    all_to_all x8, starting transfers between devices, exchanged(): return lax.all_to_all(blocks, axis, split_axis=0, concat_axis=0, tiled=True)  45.1 us
    ppermute x12, starting transfers between devices, shifted(): return lax.ppermute(values, axis, pairs)  20.5 us
    pallas_call x1, Pallas kernels, backward(): pl.pallas_call(backward_kernel, grid=(IMG + 1,), out_shape=(jax.ShapeDtyp...  11.7 us
    pallas_call x1, Pallas kernels, attention(): pl.pallas_call(attention_kernel, grid=(IMG,), out_shape=(jax.ShapeDtypeSt...  11.7 us
    ppermute x12, waiting for transfers between devices, shifted(): return lax.ppermute(values, axis, pairs)  11.4 us
    pallas_call x2, Pallas kernels, projected(): pl.pallas_call(kernel, grid_spec=pltpu.PrefetchScalarGridSpec(num_scalar_...  10.8 us
    unnamed x33, local copies, waits for them, and re-layouts  5.29 us
  transfers between devices with their start and end apart: 24, of which 13 were waited for; matrix products, arithmetic and copies ran while one was open for 9% of the time, Pallas kernels for 15%

profile of v3, /device:TPU:8, one launch (start us, length us, event | category | flops | bytes accessed | tf_op | source)
XLA Modules:
  0.0 218.7 jit_solution(4283458103287255182)
XLA Ops:
  0.6 5.3 %projected.2 = bf16[320,1280]{1,0:T(8,128)(2,1)} custom-call(s32[1]{0:T(128)S(6)} %sub.10.half_ref, bf16[5,2,4,16,1024]{4,3,2,1,0:T(8,128)(2,1)} %bitcast.61, bf16[1280,1024]{1,0:T(8,128)(2,1)} %w_ref.3), custom_call_target="tpu_custom_call" | custom-call | flops 1000000000 | bytes 4000000 | tf_op jit(solution)/shard_map/projected/pallas_call | solution.py:94
  9.5 5.5 %projected.3 = bf16[320,1280]{1,0:T(8,128)(2,1)} custom-call(s32[1]{0:T(128)} %bitcast.half_ref, bf16[5,2,4,16,1024]{4,3,2,1,0:T(8,128)(2,1)} %bitcast.62, bf16[1280,1024]{1,0:T(8,128)(2,1)} %w_ref.3, bf16[320,1280]{1,0:T(8,128)(2,1)} %copy-done.8), custom_call_target="tpu_custom_call" | custom-call | flops 1000000000 | bytes 4000000 | tf_op jit(solution)/shard_map/projected/pallas_call | solution.py:94
  14.9 5.7 %all-to-all-start = ((bf16[4,80,1280]{2,1,0:T(8,128)(2,1)}), bf16[4,80,1280]{2,1,0:T(8,128)(2,1)S(1)}, u32[]{:S(2)}, u32[]{:S(2)}) async-start(bf16[4,80,1280]{2,1,0:T(8,128)(2,1)} %bitcast.64), calls=%async_computation | async-start | bytes 1638400 | tf_op jit(solution)/shard_map/all_to_all | solution.py:33
  20.7 5.3 %convolution_convert_fusion = bf16[1280,1024]{1,0:T(8,128)(2,1)} fusion(bf16[640,1024]{1,0:T(8,128)(2,1)S(1)} %copy-done, bf16[640,1280]{1,0:T(8,128)(2,1)} %param.10, pred[640]{0:T(1024)(128)(4,1)S(1)} %fusion.9), kind=kOutput, calls=%fused_computation | convolution fusion | flops 1679851520 | bytes 5571200 | tf_op jit(solution)/shard_map/dot_general | solution.py:46
  26.0 6.4 %all-to-all-done = bf16[4,80,1280]{2,1,0:T(8,128)(2,1)S(1)} async-done(((bf16[4,80,1280]{2,1,0:T(8,128)(2,1)}), bf16[4,80,1280]{2,1,0:T(8,128)(2,1)S(1)}, u32[]{:S(2)}, u32[]{:S(2)}) %all-to-all-start) | async-done | bytes 819232 | tf_op jit(solution)/shard_map/all_to_all | solution.py:33
  35.4 10.3 %all-to-all-start.1 = ((bf16[32,5,8,128]{3,2,1,0:T(8,128)(2,1)}), bf16[32,5,8,128]{3,2,1,0:T(8,128)(2,1)S(1)}, u32[]{:S(2)}, u32[]{:S(2)}) async-start(bf16[32,5,8,128]{3,2,1,0:T(8,128)(2,1)} %spread.1), calls=%async_computation.1 | async-start | bytes 655360 | tf_op jit(solution)/shard_map/all_to_all | solution.py:33
  47.1 12.1 %all-to-all-done.1 = bf16[32,5,8,128]{3,2,1,0:T(8,128)(2,1)S(1)} async-done(((bf16[32,5,8,128]{3,2,1,0:T(8,128)(2,1)}), bf16[32,5,8,128]{3,2,1,0:T(8,128)(2,1)S(1)}, u32[]{:S(2)}, u32[]{:S(2)}) %all-to-all-start.1) | async-done | bytes 327712 | tf_op jit(solution)/shard_map/all_to_all | solution.py:33
  61.9 3.9 %all-to-all-start.2 = ((bf16[32,5,8,128]{3,2,1,0:T(8,128)(2,1)}), bf16[32,5,8,128]{3,2,1,0:T(8,128)(2,1)S(1)}, u32[]{:S(2)}, u32[]{:S(2)}) async-start(bf16[32,5,8,128]{3,2,1,0:T(8,128)(2,1)} %bitcast.68), calls=%async_computation.2 | async-start | bytes 655360 | tf_op jit(solution)/shard_map/all_to_all | solution.py:33
  70.0 6.1 %collective-permute-done.4 = bf16[160,640]{1,0:T(8,128)(2,1)S(1)} collective-permute-done((bf16[160,640]{1,0:T(8,128)(2,1)S(1)}, bf16[160,640]{1,0:T(8,128)(2,1)S(1)}, u32[]{:S(2)}, u32[]{:S(2)}) %collective-permute-start.4) | collective-permute-done | bytes 204832 | tf_op jit(solution)/shard_map/ppermute | solution.py:38
  81.9 5.1 %all-to-all-start.3 = ((bf16[4,80,1280]{2,1,0:T(8,128)(2,1)}), bf16[4,80,1280]{2,1,0:T(8,128)(2,1)S(1)}, u32[]{:S(2)}, u32[]{:S(2)}) async-start(bf16[4,80,1280]{2,1,0:T(8,128)(2,1)} %bitcast.73), calls=%async_computation.3 | async-start | bytes 1638400 | tf_op jit(solution)/shard_map/all_to_all | solution.py:33
  95.2 3.8 %all-to-all-done.3 = bf16[4,80,1280]{2,1,0:T(8,128)(2,1)S(1)} async-done(((bf16[4,80,1280]{2,1,0:T(8,128)(2,1)}), bf16[4,80,1280]{2,1,0:T(8,128)(2,1)S(1)}, u32[]{:S(2)}, u32[]{:S(2)}) %all-to-all-start.3) | async-done | bytes 819232 | tf_op jit(solution)/shard_map/all_to_all | solution.py:33
  99.1 11.7 %attention.1 = (bf16[640,1280]{1,0:T(8,128)(2,1)}, bf16[640,1280]{1,0:T(8,128)(2,1)}, bf16[5,16,1280]{2,1,0:T(8,128)(2,1)}, bf16[640,768]{1,0:T(8,128)(2,1)}, f3...) custom-call(s32[4]{0:T(128)} %pad_add_fusion.words_ref, s32[5]{0:T(128)} %dynamic_slice.34.counts_ref, ...), custom_call_target="tpu_custom_call" | custom-call | flops 10000000000 | bytes 10000000 | tf_op jit(solution)/shard_map/attention/pallas_call | solution.py:238
  110.8 11.7 %backward.1 = (bf16[640,1280]{1,0:T(8,128)(2,1)}, bf16[640,480]{1,0:T(8,128)(2,1)}, bf16[4,6,16,1280]{3,2,1,0:T(8,128)(2,1)}, bf16[4,6,16,1280]{3,2,1,0:T(8,128)(2,1)}) custom-call(s32[4]{0:T(128)} %pad_add_fusion.words_ref, bf16[4,5,16,1280]{3,2,1,0:T(8,128)(2,1)} %bitcast.72, bf16[4,5,16,1280]{3,2,1,0:T(8,128)(2,1)} %collective-permute-done.1.other_ref, ...), custom_call_target="tpu_custom_call" | custom-call | flops 10000000000 | bytes 10000000 | tf_op jit(solution)/shard_map/backward/pallas_call | solution.py:348
  125.8 6.8 %all-to-all-start.4 = ((bf16[8,40,1024]{2,1,0:T(8,128)(2,1)}), bf16[8,40,1024]{2,1,0:T(8,128)(2,1)S(1)}, u32[]{:S(2)}, u32[]{:S(2)}) async-start(bf16[8,40,1024]{2,1,0:T(8,128)(2,1)} %fusion.4), calls=%async_computation.4 | async-start | bytes 1310720 | tf_op jit(solution)/shard_map/all_to_all | solution.py:33
  135.1 18.2 %all-to-all-done.4 = bf16[8,40,1024]{2,1,0:T(8,128)(2,1)S(1)} async-done(((bf16[8,40,1024]{2,1,0:T(8,128)(2,1)}), bf16[8,40,1024]{2,1,0:T(8,128)(2,1)S(1)}, u32[]{:S(2)}, u32[]{:S(2)}) %all-to-all-start.4) | async-done | bytes 655392 | tf_op jit(solution)/shard_map/all_to_all | solution.py:33
  153.2 4.9 %all-to-all-start.5 = ((bf16[4,96,1280]{2,1,0:T(8,128)(2,1)}), bf16[4,96,1280]{2,1,0:T(8,128)(2,1)S(1)}, u32[]{:S(2)}, u32[]{:S(2)}) async-start(bf16[4,96,1280]{2,1,0:T(8,128)(2,1)} %bitcast.20), calls=%async_computation.5 | async-start | bytes 1966080 | tf_op jit(solution)/shard_map/all_to_all | solution.py:33
  158.1 4.9 %weight_terms.1 = (bf16[8,40,640]{2,1,0:T(8,128)(2,1)}, bf16[8,40,640]{2,1,0:T(8,128)(2,1)}, bf16[8,40,640]{2,1,0:T(8,128)(2,1)}, bf16[8,40,640]{2,1,0:T(8,128)(2,1)}) custom-call(s32[4]{0:T(128)} %pad_add_fusion.words_ref, bf16[640,1280]{1,0:T(8,128)(2,1)} %get-tuple-element.44.normed_ref, bf16[640,1280]{1,0:T(8,128)(2,1)} %get-tuple-element.45.upstream_ref, ...), custom_call_target="tpu_custom_call" | custom-call | flops 4000000000 | bytes 6000000 | tf_op jit(solution)/shard_map/weight_terms/pallas_call | solution.py:401
  163.0 3.0 %collective-permute-start.10 = (bf16[8,40,640]{2,1,0:T(8,128)(2,1)}, bf16[8,40,640]{2,1,0:T(8,128)(2,1)S(1)}, u32[]{:S(2)}, u32[]{:S(2)}) collective-permute-start(bf16[8,40,640]{2,1,0:T(8,128)(2,1)} %get-tuple-element.49), channel_id=1, source_target_pairs={{0,16},{8,24},{16,0},{24,8},{1,17},{9,25},{17,1},{25,9},{2,18},{10... | collective-permute-start | bytes 1228808 | tf_op jit(solution)/shard_map/ppermute | solution.py:38
  176.1 3.0 %collective-permute-start.13 = (bf16[1,320]{1,0:T(2,128)(2,1)S(1)}, bf16[1,320]{1,0:T(2,128)(2,1)S(1)}, u32[]{:S(2)}, u32[]{:S(2)}) collective-permute-start(bf16[1,320]{1,0:T(2,128)(2,1)S(1)} %get-tuple-element.68), channel_id=1, source_target_pairs={{0,16},{8,24},{16,0},{24,8},{1,17},{9,25},{17,1},{25,9},{2,18},{10... | collective-permute-start | bytes 1928 | tf_op jit(solution)/shard_map/ppermute | solution.py:38
  181.2 3.5 %collective-permute-done.11 = bf16[8,40,640]{2,1,0:T(8,128)(2,1)S(1)} collective-permute-done((bf16[8,40,640]{2,1,0:T(8,128)(2,1)}, bf16[8,40,640]{2,1,0:T(8,128)(2,1)S(1)}, u32[]{:S(2)}, u32[]{:S(2)}) %collective-permute-start.11) | collective-permute-done | bytes 409632 | tf_op jit(solution)/shard_map/ppermute | solution.py:38
  185.0 4.8 %all-to-all-start.6 = ((bf16[8,80,160]{2,1,0:T(8,128)(2,1)}), bf16[8,80,160]{2,1,0:T(8,128)(2,1)S(1)}, u32[]{:S(2)}, u32[]{:S(2)}) async-start(bf16[8,80,160]{2,1,0:T(8,128)(2,1)} %get-tuple-element.42), calls=%async_computation.6 | async-start | bytes 655360 | tf_op jit(solution)/shard_map/all_to_all | solution.py:33
  190.9 5.6 %all-to-all-done.6 = bf16[8,80,160]{2,1,0:T(8,128)(2,1)S(1)} async-done(((bf16[8,80,160]{2,1,0:T(8,128)(2,1)}), bf16[8,80,160]{2,1,0:T(8,128)(2,1)S(1)}, u32[]{:S(2)}, u32[]{:S(2)}) %all-to-all-start.6) | async-done | bytes 204832 | tf_op jit(solution)/shard_map/all_to_all | solution.py:33
  196.6 3.5 %all-to-all-start.7 = ((bf16[8,40,768]{2,1,0:T(8,128)(2,1)}), bf16[8,40,768]{2,1,0:T(8,128)(2,1)S(1)}, u32[]{:S(2)}, u32[]{:S(2)}) async-start(bf16[8,40,768]{2,1,0:T(8,128)(2,1)} %fusion.7), calls=%async_computation.7 | async-start | bytes 983040 | tf_op jit(solution)/shard_map/all_to_all | solution.py:33
  201.7 14.9 %all-to-all-done.7 = bf16[8,40,768]{2,1,0:T(8,128)(2,1)S(1)} async-done(((bf16[8,40,768]{2,1,0:T(8,128)(2,1)}), bf16[8,40,768]{2,1,0:T(8,128)(2,1)S(1)}, u32[]{:S(2)}, u32[]{:S(2)}) %all-to-all-start.7) | async-done | bytes 491552 | tf_op jit(solution)/shard_map/all_to_all | solution.py:33
  (98 shorter events, 51.8 us)
Async XLA Ops:
  6.0 2.5 %collective-permute-start = (bf16[320,1280]{1,0:T(8,128)(2,1)}, bf16[320,1280]{1,0:T(8,128)(2,1)S(1)}, u32[]{:S(2)}, u32[]{:S(2)}) collective-permute-start(bf16[320,1280]{1,0:T(8,128)(2,1)} %projected.2), channel_id=1, source_target_pairs={{0,1},{1,0},{2,3},{3,2},{4,5},{5,4},{6,7},{7,6},{8,9},{9,8},{10,11... | collective-permute-start | bytes 2457608 | tf_op jit(solution)/shard_map/ppermute | solution.py:42
  14.9 17.5 %all-to-all-start = ((bf16[4,80,1280]{2,1,0:T(8,128)(2,1)}), bf16[4,80,1280]{2,1,0:T(8,128)(2,1)S(1)}, u32[]{:S(2)}, u32[]{:S(2)}) async-start(bf16[4,80,1280]{2,1,0:T(8,128)(2,1)} %bitcast.64), calls=%async_computation | async-start | bytes 1638400 | tf_op jit(solution)/shard_map/all_to_all | solution.py:33
  35.4 23.8 %all-to-all-start.1 = ((bf16[32,5,8,128]{3,2,1,0:T(8,128)(2,1)}), bf16[32,5,8,128]{3,2,1,0:T(8,128)(2,1)S(1)}, u32[]{:S(2)}, u32[]{:S(2)}) async-start(bf16[32,5,8,128]{3,2,1,0:T(8,128)(2,1)} %spread.1), calls=%async_computation.1 | async-start | bytes 655360 | tf_op jit(solution)/shard_map/all_to_all | solution.py:33
  61.9 17.2 %all-to-all-start.2 = ((bf16[32,5,8,128]{3,2,1,0:T(8,128)(2,1)}), bf16[32,5,8,128]{3,2,1,0:T(8,128)(2,1)S(1)}, u32[]{:S(2)}, u32[]{:S(2)}) async-start(bf16[32,5,8,128]{3,2,1,0:T(8,128)(2,1)} %bitcast.68), calls=%async_computation.2 | async-start | bytes 655360 | tf_op jit(solution)/shard_map/all_to_all | solution.py:33
  65.8 10.2 %collective-permute-start.4 = (bf16[160,640]{1,0:T(8,128)(2,1)S(1)}, bf16[160,640]{1,0:T(8,128)(2,1)S(1)}, u32[]{:S(2)}, u32[]{:S(2)}) collective-permute-start(bf16[160,640]{1,0:T(8,128)(2,1)S(1)} %bitcast.74), channel_id=1, source_target_pairs={{0,6},{2,0},{4,2},{6,4},{1,7},{3,1},{5,3},{7,5},{8,14},{10,8},{12,... | collective-permute-start | bytes 614408 | tf_op jit(solution)/shard_map/ppermute | solution.py:38
  67.3 8.7 %collective-permute-start.3 = (bf16[160,640]{1,0:T(8,128)(2,1)S(1)}, bf16[160,640]{1,0:T(8,128)(2,1)S(1)}, u32[]{:S(2)}, u32[]{:S(2)}) collective-permute-start(bf16[160,640]{1,0:T(8,128)(2,1)S(1)} %bitcast.75), channel_id=1, source_target_pairs={{0,4},{2,6},{4,0},{6,2},{1,5},{3,7},{5,1},{7,3},{8,12},{10,14},{12... | collective-permute-start | bytes 614408 | tf_op jit(solution)/shard_map/ppermute | solution.py:38
  67.4 10.1 %collective-permute-start.2 = (bf16[160,640]{1,0:T(8,128)(2,1)S(1)}, bf16[160,640]{1,0:T(8,128)(2,1)S(1)}, u32[]{:S(2)}, u32[]{:S(2)}) collective-permute-start(bf16[160,640]{1,0:T(8,128)(2,1)S(1)} %bitcast.76), channel_id=1, source_target_pairs={{0,2},{2,4},{4,6},{6,0},{1,3},{3,5},{5,7},{7,1},{8,10},{10,12},{12... | collective-permute-start | bytes 614408 | tf_op jit(solution)/shard_map/ppermute | solution.py:38
  78.6 20.4 %collective-permute-start.5 = (bf16[4,160,640]{2,1,0:T(8,128)(2,1)}, bf16[4,160,640]{2,1,0:T(8,128)(2,1)}, u32[]{:S(2)}, u32[]{:S(2)}) collective-permute-start(bf16[4,160,640]{2,1,0:T(8,128)(2,1)} %pad_maximum_fusion.own_ref), channel_id=1, source_target_pairs={{0,1},{1,0},{2,3},{3,2},{4,5},{5,4},{6,7},{7,6},{8,9},{9,8},{10,11... | collective-permute-start | bytes 2457608 | tf_op jit(solution)/shard_map/ppermute | solution.py:42
  81.9 17.2 %all-to-all-start.3 = ((bf16[4,80,1280]{2,1,0:T(8,128)(2,1)}), bf16[4,80,1280]{2,1,0:T(8,128)(2,1)S(1)}, u32[]{:S(2)}, u32[]{:S(2)}) async-start(bf16[4,80,1280]{2,1,0:T(8,128)(2,1)} %bitcast.73), calls=%async_computation.3 | async-start | bytes 1638400 | tf_op jit(solution)/shard_map/all_to_all | solution.py:33
  90.2 32.6 %collective-permute-start.7 = (bf16[8,40,1024]{2,1,0:T(8,128)(2,1)}, bf16[8,40,1024]{2,1,0:T(8,128)(2,1)}, u32[]{:S(2)}, u32[]{:S(2)}) collective-permute-start(bf16[8,40,1024]{2,1,0:T(8,128)(2,1)} %get-tuple-element.65), channel_id=1, source_target_pairs={{0,16},{8,24},{16,0},{24,8},{1,17},{9,25},{17,1},{25,9},{2,18},{10... | collective-permute-start | bytes 1966088 | tf_op jit(solution)/shard_map/ppermute | solution.py:38
  93.2 29.8 %collective-permute-start.9 = (bf16[8,40,1024]{2,1,0:T(8,128)(2,1)}, bf16[8,40,1024]{2,1,0:T(8,128)(2,1)}, u32[]{:S(2)}, u32[]{:S(2)}) collective-permute-start(bf16[8,40,1024]{2,1,0:T(8,128)(2,1)} %get-tuple-element.66), channel_id=1, source_target_pairs={{0,24},{8,0},{16,8},{24,16},{1,25},{9,1},{17,9},{25,17},{2,26},{10... | collective-permute-start | bytes 1966088 | tf_op jit(solution)/shard_map/ppermute | solution.py:38
  94.4 28.6 %collective-permute-start.8 = (bf16[8,40,1024]{2,1,0:T(8,128)(2,1)}, bf16[8,40,1024]{2,1,0:T(8,128)(2,1)}, u32[]{:S(2)}, u32[]{:S(2)}) collective-permute-start(bf16[8,40,1024]{2,1,0:T(8,128)(2,1)} %get-tuple-element.67), channel_id=1, source_target_pairs={{0,8},{8,16},{16,24},{24,0},{1,9},{9,17},{17,25},{25,1},{2,10},{10... | collective-permute-start | bytes 1966088 | tf_op jit(solution)/shard_map/ppermute | solution.py:38
  99.1 11.7 %collective-permute-start.1 = (bf16[4,5,16,1280]{3,2,1,0:T(8,128)(2,1)S(1)}, bf16[4,5,16,1280]{3,2,1,0:T(8,128)(2,1)}, u32[]{:S(2)}, u32[]{:S(2)}) collective-permute-start(bf16[4,5,16,1280]{3,2,1,0:T(8,128)(2,1)S(1)} %bitcast.71), channel_id=1, source_target_pairs={{0,1},{1,0},{2,3},{3,2},{4,5},{5,4},{6,7},{7,6},{8,9},{9,8},{10,11... | collective-permute-start | bytes 2457608 | tf_op jit(solution)/shard_map/ppermute | solution.py:42
  122.5 10.1 %collective-permute-start.6 = (bf16[4,6,16,1280]{3,2,1,0:T(8,128)(2,1)}, bf16[4,6,16,1280]{3,2,1,0:T(8,128)(2,1)}, u32[]{:S(2)}, u32[]{:S(2)}) collective-permute-start(bf16[4,6,16,1280]{3,2,1,0:T(8,128)(2,1)} %get-tuple-element.37), channel_id=1, source_target_pairs={{0,1},{1,0},{2,3},{3,2},{4,5},{5,4},{6,7},{7,6},{8,9},{9,8},{10,11... | collective-permute-start | bytes 2949128 | tf_op jit(solution)/shard_map/ppermute | solution.py:42
  125.8 27.4 %all-to-all-start.4 = ((bf16[8,40,1024]{2,1,0:T(8,128)(2,1)}), bf16[8,40,1024]{2,1,0:T(8,128)(2,1)S(1)}, u32[]{:S(2)}, u32[]{:S(2)}) async-start(bf16[8,40,1024]{2,1,0:T(8,128)(2,1)} %fusion.4), calls=%async_computation.4 | async-start | bytes 1310720 | tf_op jit(solution)/shard_map/all_to_all | solution.py:33
  153.2 18.3 %all-to-all-start.5 = ((bf16[4,96,1280]{2,1,0:T(8,128)(2,1)}), bf16[4,96,1280]{2,1,0:T(8,128)(2,1)S(1)}, u32[]{:S(2)}, u32[]{:S(2)}) async-start(bf16[4,96,1280]{2,1,0:T(8,128)(2,1)} %bitcast.20), calls=%async_computation.5 | async-start | bytes 1966080 | tf_op jit(solution)/shard_map/all_to_all | solution.py:33
  163.0 17.3 %collective-permute-start.10 = (bf16[8,40,640]{2,1,0:T(8,128)(2,1)}, bf16[8,40,640]{2,1,0:T(8,128)(2,1)S(1)}, u32[]{:S(2)}, u32[]{:S(2)}) collective-permute-start(bf16[8,40,640]{2,1,0:T(8,128)(2,1)} %get-tuple-element.49), channel_id=1, source_target_pairs={{0,16},{8,24},{16,0},{24,8},{1,17},{9,25},{17,1},{25,9},{2,18},{10... | collective-permute-start | bytes 1228808 | tf_op jit(solution)/shard_map/ppermute | solution.py:38
  166.1 18.7 %collective-permute-start.11 = (bf16[8,40,640]{2,1,0:T(8,128)(2,1)}, bf16[8,40,640]{2,1,0:T(8,128)(2,1)S(1)}, u32[]{:S(2)}, u32[]{:S(2)}) collective-permute-start(bf16[8,40,640]{2,1,0:T(8,128)(2,1)} %get-tuple-element.50), channel_id=1, source_target_pairs={{0,8},{8,16},{16,24},{24,0},{1,9},{9,17},{17,25},{25,1},{2,10},{10... | collective-permute-start | bytes 1228808 | tf_op jit(solution)/shard_map/ppermute | solution.py:38
  166.6 18.1 %collective-permute-start.12 = (bf16[8,40,640]{2,1,0:T(8,128)(2,1)}, bf16[8,40,640]{2,1,0:T(8,128)(2,1)S(1)}, u32[]{:S(2)}, u32[]{:S(2)}) collective-permute-start(bf16[8,40,640]{2,1,0:T(8,128)(2,1)} %get-tuple-element.51), channel_id=1, source_target_pairs={{0,24},{8,0},{16,8},{24,16},{1,25},{9,1},{17,9},{25,17},{2,26},{10... | collective-permute-start | bytes 1228808 | tf_op jit(solution)/shard_map/ppermute | solution.py:38
  176.1 13.7 %collective-permute-start.13 = (bf16[1,320]{1,0:T(2,128)(2,1)S(1)}, bf16[1,320]{1,0:T(2,128)(2,1)S(1)}, u32[]{:S(2)}, u32[]{:S(2)}) collective-permute-start(bf16[1,320]{1,0:T(2,128)(2,1)S(1)} %get-tuple-element.68), channel_id=1, source_target_pairs={{0,16},{8,24},{16,0},{24,8},{1,17},{9,25},{17,1},{25,9},{2,18},{10... | collective-permute-start | bytes 1928 | tf_op jit(solution)/shard_map/ppermute | solution.py:38
  179.2 10.7 %collective-permute-start.15 = (bf16[1,320]{1,0:T(2,128)(2,1)S(1)}, bf16[1,320]{1,0:T(2,128)(2,1)S(1)}, u32[]{:S(2)}, u32[]{:S(2)}) collective-permute-start(bf16[1,320]{1,0:T(2,128)(2,1)S(1)} %get-tuple-element.69), channel_id=1, source_target_pairs={{0,24},{8,0},{16,8},{24,16},{1,25},{9,1},{17,9},{25,17},{2,26},{10... | collective-permute-start | bytes 1928 | tf_op jit(solution)/shard_map/ppermute | solution.py:38
  180.4 9.5 %collective-permute-start.14 = (bf16[1,320]{1,0:T(2,128)(2,1)S(1)}, bf16[1,320]{1,0:T(2,128)(2,1)S(1)}, u32[]{:S(2)}, u32[]{:S(2)}) collective-permute-start(bf16[1,320]{1,0:T(2,128)(2,1)S(1)} %get-tuple-element.70), channel_id=1, source_target_pairs={{0,8},{8,16},{16,24},{24,0},{1,9},{9,17},{17,25},{25,1},{2,10},{10... | collective-permute-start | bytes 1928 | tf_op jit(solution)/shard_map/ppermute | solution.py:38
  185.0 11.6 %all-to-all-start.6 = ((bf16[8,80,160]{2,1,0:T(8,128)(2,1)}), bf16[8,80,160]{2,1,0:T(8,128)(2,1)S(1)}, u32[]{:S(2)}, u32[]{:S(2)}) async-start(bf16[8,80,160]{2,1,0:T(8,128)(2,1)} %get-tuple-element.42), calls=%async_computation.6 | async-start | bytes 655360 | tf_op jit(solution)/shard_map/all_to_all | solution.py:33
  196.6 20.0 %all-to-all-start.7 = ((bf16[8,40,768]{2,1,0:T(8,128)(2,1)}), bf16[8,40,768]{2,1,0:T(8,128)(2,1)S(1)}, u32[]{:S(2)}, u32[]{:S(2)}) async-start(bf16[8,40,768]{2,1,0:T(8,128)(2,1)} %fusion.7), calls=%async_computation.7 | async-start | bytes 983040 | tf_op jit(solution)/shard_map/all_to_all | solution.py:33
  (15 other events, 155.6 us)

commit v4 on v3

--- a/solution.py
+++ b/solution.py
@@ -69,46 +69,6 @@
             wide = pltpu.roll(wide, HEAD * at, 1)
         total = wide if total is None else total + wide
     return total
-
-
-def half_rows(rows_ref):
-    return jnp.concatenate(
-        [rows_ref[image, 0, near] for near in range(4) for image in range(IMG)], axis=0
-    )
-
-
-def part_kernel(half_ref, rows_ref, w_ref, out_ref):
-    out_ref[...] = dot(half_rows(rows_ref), w_ref[...], 1, 1).astype(BF)
-
-
-def pair_kernel(half_ref, rows_ref, w_ref, got_ref, out_ref):
-    own = dot(half_rows(rows_ref), w_ref[...], 1, 1)
-    out_ref[...] = (own + got_ref[...].astype(F32)).astype(BF)
-
-
-def projected(half, grad_rows, w_proj, got=None):
-    depth = grad_rows.shape[1]
-    rows = grad_rows.reshape(IMG, 2, 4, 16, depth)
-    block = pl.BlockSpec((ROWS // 2, 256), lambda i, half: (0, i))
-    kernel, extra = (part_kernel, ()) if got is None else (pair_kernel, (got,))
-    return pl.pallas_call(
-        kernel,
-        grid_spec=pltpu.PrefetchScalarGridSpec(
-            num_scalar_prefetch=1,
-            grid=(WIDTH // 256,),
-            in_specs=[
-                pl.BlockSpec((IMG, 1, 4, 16, depth), lambda i, half: (0, half[0], 0, 0, 0)),
-                pl.BlockSpec((256, depth), lambda i, half: (i, 0)),
-                *(block for _ in extra),
-            ],
-            out_specs=block,
-        ),
-        out_shape=jax.ShapeDtypeStruct((ROWS // 2, WIDTH), BF),
-        cost_estimate=pl.CostEstimate(
-            flops=1_000_000_000, bytes_accessed=4_000_000, transcendentals=0
-        ),
-        name="projected",
-    )(half, rows, w_proj, *extra)
 
 
 def spread_kernel(place_ref, counts_ref, arrived_ref, out_ref):
@@ -284,7 +244,6 @@
     in_own_ref,
     in_other_ref,
     gain_term,
-    w_pad,
     wout_pad,
 ):
     step = pl.program_id(0)
@@ -293,7 +252,6 @@
     def _():
         gain_term[...] = jnp.zeros_like(gain_term)
         padded_heads(wout_pad, wout_ref)
-        padded_heads(w_pad, w_ref)
 
     @pl.when(step < IMG)
     def _():
@@ -319,9 +277,9 @@
             pieces.append(dot(score_grad, key, 1, 0))
             pieces.append(dot(score_grad, query, 0, 0))
             pieces.append(dot(probability.astype(BF), mixed_grad, 0, 0))
-        packed_grad_ref[...] = shifted_sum(pieces, 512)[:, :480].astype(BF)
-        wide = jnp.concatenate([piece.astype(BF) for piece in pieces], axis=1)
-        in_part = dot(wide, w_pad[...], 1, 0).astype(BF)
+        packed_grad = shifted_sum(pieces, 512)[:, :480].astype(BF)
+        packed_grad_ref[...] = packed_grad
+        in_part = dot(packed_grad, w_ref[...], 1, 0).astype(BF)
         gain_term[...] += jnp.sum(
             in_part.astype(F32) * normed_ref[...].astype(F32), axis=0, keepdims=True
         )
@@ -372,7 +330,6 @@
         ),
         scratch_shapes=[
             pltpu.VMEM((1, WIDTH), F32),
-            pltpu.VMEM((6 * LANE, WIDTH), BF),
             pltpu.VMEM((2 * LANE, WIDTH), BF),
         ],
         cost_estimate=pl.CostEstimate(
@@ -503,9 +460,14 @@
     all_counts = jnp.sum(jnp.where(hits, patch_counts.reshape(1, -1), 0), axis=1)
     arrived_counts = lax.dynamic_slice_in_dim(all_counts, device * IMG, IMG, 0)
 
-    own_half = core.reshape(1).astype(jnp.int32)
-    part_other = projected(1 - own_half, grad_rows, w_proj)
-    pair = projected(own_half, grad_rows, w_proj, swapped(part_other))
+    halves = grad_rows.reshape(IMG, 2, 64, columns)
+    for_other = lax.dynamic_index_in_dim(halves, 1 - core, 1, keepdims=False)
+    for_own = lax.dynamic_index_in_dim(halves, core, 1, keepdims=False)
+    part_other = dot(for_other.reshape(ROWS // 2, columns), w_proj, 1, 1).astype(BF)
+    from_other = swapped(part_other)
+    part_own = dot(for_own.reshape(ROWS // 2, columns), w_proj, 1, 1)
+    pair = (part_own + from_other.astype(F32)).astype(BF)
+    pair = pair.reshape(IMG, 4, 16, WIDTH).transpose(1, 0, 2, 3)
     features = after(features, pair)
     arrived = exchanged(pair.reshape(4, 80, WIDTH), "y").reshape(4, IMG, 16, WIDTH)
 

time: 221 us -> 222 us (level)
  Pallas kernels: 47.8 us -> 37 us
  other arithmetic: 9.8 us -> 14.4 us
  matrix products: 5.27 us -> 9.8 us
  local copies, waits for them, and re-layouts: 11.7 us -> 15.2 us
    pallas_call x2 -> x0, Pallas kernels: 10.8 us -> none  [projected(): pl.pallas_call(kernel, grid_spec=pltpu.PrefetchScalarGridSpec(num_scalar_...]
    dot_general x1 -> x3, matrix products: 5.27 us -> 9.8 us  [dot(): lax.dot_general(left, right, (((dim_left,), (dim_right,)), ((), ())), pre...]
    all_to_all x8, waiting for transfers between devices: 63.7 us -> 59.6 us  [exchanged(): return lax.all_to_all(blocks, axis, split_axis=0, concat_axis=0, tiled=True)]
    convert_element_type x3, other arithmetic: 3.05 us -> 5.35 us  [near_sum(): return total.astype(BF)]
    unnamed x33 -> x23, local copies, waits for them, and re-layouts: 5.29 us -> 3.99 us
  transfers between devices with their start and end apart: 24 -> 24, of which waited for: 13 -> 14; matrix products, arithmetic and copies ran while one was open for 9% -> 12% of each run, Pallas kernels for 15% -> 15%
where the time goes in v4:
time: 222 us; the launch traced here: 219 us
  waiting for transfers between devices  75.7 us (34%)
  starting transfers between devices  66.3 us (30%)
  Pallas kernels  37 us (17%)
  local copies, waits for them, and re-layouts  15.2 us (7%)
  other arithmetic  14.4 us (6%)
  matrix products  9.8 us (4%)
    all_to_all x8, waiting for transfers between devices, exchanged(): return lax.all_to_all(blocks, axis, split_axis=0, concat_axis=0, tiled=True)  59.6 us
    all_to_all x8, starting transfers between devices, exchanged(): return lax.all_to_all(blocks, axis, split_axis=0, concat_axis=0, tiled=True)  45.4 us
    ppermute x12, starting transfers between devices, shifted(): return lax.ppermute(values, axis, pairs)  20.5 us
    ppermute x12, waiting for transfers between devices, shifted(): return lax.ppermute(values, axis, pairs)  13.6 us
    pallas_call x1, Pallas kernels, backward(): pl.pallas_call(backward_kernel, grid=(IMG + 1,), out_shape=(jax.ShapeDtyp...  11.8 us
    pallas_call x1, Pallas kernels, attention(): pl.pallas_call(attention_kernel, grid=(IMG,), out_shape=(jax.ShapeDtypeSt...  11.6 us
    dot_general x3, matrix products, dot(): lax.dot_general(left, right, (((dim_left,), (dim_right,)), ((), ())), pre...  9.8 us
    convert_element_type x3, other arithmetic, near_sum(): return total.astype(BF)  5.35 us
  transfers between devices with their start and end apart: 24, of which 14 were waited for; matrix products, arithmetic and copies ran while one was open for 12% of the time, Pallas kernels for 15%

profile of v4, /device:TPU:8, one launch (start us, length us, event | category | flops | bytes accessed | tf_op | source)
XLA Modules:
  0.0 219.3 jit_solution(15235110173999337929)
XLA Ops:
  10.6 5.6 %all-to-all-start = ((bf16[4,80,1280]{2,1,0:T(8,128)(2,1)}), bf16[4,80,1280]{2,1,0:T(8,128)(2,1)S(1)}, u32[]{:S(2)}, u32[]{:S(2)}) async-start(bf16[4,80,1280]{2,1,0:T(8,128)(2,1)} %bitcast.9), calls=%async_computation | async-start | bytes 1638400 | tf_op jit(solution)/shard_map/all_to_all | solution.py:33
  16.3 5.7 %convolution_convert_fusion = bf16[1280,1024]{1,0:T(8,128)(2,1)} fusion(bf16[640,1024]{1,0:T(8,128)(2,1)} %param.9, bf16[640,1280]{1,0:T(8,128)(2,1)} %param.10, pred[640]{0:T(1024)(128)(4,1)S(1)} %fusion.9), kind=kOutput, calls=%fused_computation | convolution fusion | flops 1679851520 | bytes 5571200 | tf_op jit(solution)/shard_map/dot_general | solution.py:46
  21.9 6.0 %all-to-all-done = bf16[4,80,1280]{2,1,0:T(8,128)(2,1)S(1)} async-done(((bf16[4,80,1280]{2,1,0:T(8,128)(2,1)}), bf16[4,80,1280]{2,1,0:T(8,128)(2,1)S(1)}, u32[]{:S(2)}, u32[]{:S(2)}) %all-to-all-start) | async-done | bytes 819232 | tf_op jit(solution)/shard_map/all_to_all | solution.py:33
  30.9 10.5 %all-to-all-start.1 = ((bf16[32,5,8,128]{3,2,1,0:T(8,128)(2,1)}), bf16[32,5,8,128]{3,2,1,0:T(8,128)(2,1)S(1)}, u32[]{:S(2)}, u32[]{:S(2)}) async-start(bf16[32,5,8,128]{3,2,1,0:T(8,128)(2,1)} %spread.1), calls=%async_computation.1 | async-start | bytes 655360 | tf_op jit(solution)/shard_map/all_to_all | solution.py:33
  42.7 12.1 %all-to-all-done.1 = bf16[32,5,8,128]{3,2,1,0:T(8,128)(2,1)S(1)} async-done(((bf16[32,5,8,128]{3,2,1,0:T(8,128)(2,1)}), bf16[32,5,8,128]{3,2,1,0:T(8,128)(2,1)S(1)}, u32[]{:S(2)}, u32[]{:S(2)}) %all-to-all-start.1) | async-done | bytes 327712 | tf_op jit(solution)/shard_map/all_to_all | solution.py:33
  57.5 3.9 %all-to-all-start.2 = ((bf16[32,5,8,128]{3,2,1,0:T(8,128)(2,1)}), bf16[32,5,8,128]{3,2,1,0:T(8,128)(2,1)S(1)}, u32[]{:S(2)}, u32[]{:S(2)}) async-start(bf16[32,5,8,128]{3,2,1,0:T(8,128)(2,1)} %bitcast.75), calls=%async_computation.2 | async-start | bytes 655360 | tf_op jit(solution)/shard_map/all_to_all | solution.py:33
  65.6 6.1 %collective-permute-done.4 = bf16[160,640]{1,0:T(8,128)(2,1)S(1)} collective-permute-done((bf16[160,640]{1,0:T(8,128)(2,1)S(1)}, bf16[160,640]{1,0:T(8,128)(2,1)S(1)}, u32[]{:S(2)}, u32[]{:S(2)}) %collective-permute-start.4) | collective-permute-done | bytes 204832 | tf_op jit(solution)/shard_map/ppermute | solution.py:38
  77.5 5.1 %all-to-all-start.3 = ((bf16[4,80,1280]{2,1,0:T(8,128)(2,1)}), bf16[4,80,1280]{2,1,0:T(8,128)(2,1)S(1)}, u32[]{:S(2)}, u32[]{:S(2)}) async-start(bf16[4,80,1280]{2,1,0:T(8,128)(2,1)} %bitcast.80), calls=%async_computation.3 | async-start | bytes 1638400 | tf_op jit(solution)/shard_map/all_to_all | solution.py:33
  84.4 2.8 %dynamic-slice_bitcast_fusion.2 = (bf16[8,40,1024]{2,1,0:T(8,128)(2,1)}, bf16[8,40,1024]{2,1,0:T(8,128)(2,1)}, bf16[8,40,1024]{2,1,0:T(8,128)(2,1)}) fusion(bf16[8,4,40,1024]{3,2,1,0:T(8,128)(2,1)} %bitcast.72, s32[]{:T(128)S(6)} %select_n.65, s32[]{:T(128)S(6)} %select_n.67, s32[]{:T(128)S(6)} %select_n.66), kind=kLoop, calls=%fused_computation.19 | loop fusion | bytes 3932172 | tf_op jit(solution)/shard_map/jit(dynamic_index_in_dim)/squeeze | solution.py:430
  87.2 3.0 %collective-permute-start.7 = (bf16[8,40,1024]{2,1,0:T(8,128)(2,1)}, bf16[8,40,1024]{2,1,0:T(8,128)(2,1)}, u32[]{:S(2)}, u32[]{:S(2)}) collective-permute-start(bf16[8,40,1024]{2,1,0:T(8,128)(2,1)} %get-tuple-element.65), channel_id=1, source_target_pairs={{0,16},{8,24},{16,0},{24,8},{1,17},{9,25},{17,1},{25,9},{2,18},{10... | collective-permute-start | bytes 1966088 | tf_op jit(solution)/shard_map/ppermute | solution.py:38
  94.7 11.6 %attention.1 = (bf16[640,1280]{1,0:T(8,128)(2,1)}, bf16[640,1280]{1,0:T(8,128)(2,1)}, bf16[5,16,1280]{2,1,0:T(8,128)(2,1)}, bf16[640,768]{1,0:T(8,128)(2,1)}, f3...) custom-call(s32[4]{0:T(128)} %pad_add_fusion.words_ref, s32[5]{0:T(128)} %dynamic_slice.43.counts_ref, ...), custom_call_target="tpu_custom_call" | custom-call | flops 10000000000 | bytes 10000000 | tf_op jit(solution)/shard_map/attention/pallas_call | solution.py:198
  106.4 11.8 %backward.1 = (bf16[640,1280]{1,0:T(8,128)(2,1)}, bf16[640,480]{1,0:T(8,128)(2,1)}, bf16[4,6,16,1280]{3,2,1,0:T(8,128)(2,1)}, bf16[4,6,16,1280]{3,2,1,0:T(8,128)(2,1)}) custom-call(s32[4]{0:T(128)} %pad_add_fusion.words_ref, bf16[4,5,16,1280]{3,2,1,0:T(8,128)(2,1)} %bitcast.79, bf16[4,5,16,1280]{3,2,1,0:T(8,128)(2,1)} %collective-permute-done.1.other_ref, ...), custom_call_target="tpu_custom_call" | custom-call | flops 10000000000 | bytes 10000000 | tf_op jit(solution)/shard_map/backward/pallas_call | solution.py:306
  120.1 3.0 %fusion.4 = bf16[8,40,1024]{2,1,0:T(8,128)(2,1)} fusion(bf16[8,40,1024]{2,1,0:T(8,128)(2,1)} %collective-permute-done.9, bf16[8,40,1024]{2,1,0:T(8,128)(2,1)} %collective-permute-done.8, bf16[8,40,1024]{2,1,0:T(8,128)(2,1)} %collective-permute-done.7, bf16[8,4,40,1024]{3,2,1,0:T(8,128)(2,1)} %bitcast.73, s32[]{:T(128)S(6)} %select_n.64), kind=kLoop, calls=%fused_computation.9 | loop fusion | flops 2621440 | bytes 3276804 | tf_op jit(solution)/shard_map/convert_element_type | solution.py:440
  123.0 6.7 %all-to-all-start.4 = ((bf16[8,40,1024]{2,1,0:T(8,128)(2,1)}), bf16[8,40,1024]{2,1,0:T(8,128)(2,1)S(1)}, u32[]{:S(2)}, u32[]{:S(2)}) async-start(bf16[8,40,1024]{2,1,0:T(8,128)(2,1)} %fusion.4), calls=%async_computation.4 | async-start | bytes 1310720 | tf_op jit(solution)/shard_map/all_to_all | solution.py:33
  132.4 17.7 %all-to-all-done.4 = bf16[8,40,1024]{2,1,0:T(8,128)(2,1)S(1)} async-done(((bf16[8,40,1024]{2,1,0:T(8,128)(2,1)}), bf16[8,40,1024]{2,1,0:T(8,128)(2,1)S(1)}, u32[]{:S(2)}, u32[]{:S(2)}) %all-to-all-start.4) | async-done | bytes 655392 | tf_op jit(solution)/shard_map/all_to_all | solution.py:33
  150.1 4.8 %all-to-all-start.5 = ((bf16[4,96,1280]{2,1,0:T(8,128)(2,1)}), bf16[4,96,1280]{2,1,0:T(8,128)(2,1)}, u32[]{:S(2)}, u32[]{:S(2)}) async-start(bf16[4,96,1280]{2,1,0:T(8,128)(2,1)} %bitcast.70), calls=%async_computation.5 | async-start | bytes 1966080 | tf_op jit(solution)/shard_map/all_to_all | solution.py:33
  154.9 4.8 %weight_terms.1 = (bf16[8,40,640]{2,1,0:T(8,128)(2,1)}, bf16[8,40,640]{2,1,0:T(8,128)(2,1)}, bf16[8,40,640]{2,1,0:T(8,128)(2,1)}, bf16[8,40,640]{2,1,0:T(8,128)(2,1)}) custom-call(s32[4]{0:T(128)} %pad_add_fusion.words_ref, bf16[640,1280]{1,0:T(8,128)(2,1)} %get-tuple-element.44.normed_ref, bf16[640,1280]{1,0:T(8,128)(2,1)} %get-tuple-element.45.upstream_ref, ...), custom_call_target="tpu_custom_call" | custom-call | flops 4000000000 | bytes 6000000 | tf_op jit(solution)/shard_map/weight_terms/pallas_call | solution.py:358
  159.8 3.0 %collective-permute-start.10 = (bf16[8,40,640]{2,1,0:T(8,128)(2,1)}, bf16[8,40,640]{2,1,0:T(8,128)(2,1)}, u32[]{:S(2)}, u32[]{:S(2)}) collective-permute-start(bf16[8,40,640]{2,1,0:T(8,128)(2,1)} %get-tuple-element.49), channel_id=1, source_target_pairs={{0,16},{8,24},{16,0},{24,8},{1,17},{9,25},{17,1},{25,9},{2,18},{10... | collective-permute-start | bytes 1228808 | tf_op jit(solution)/shard_map/ppermute | solution.py:38
  171.8 3.1 %collective-permute-start.13 = (bf16[1,320]{1,0:T(2,128)(2,1)S(1)}, bf16[1,320]{1,0:T(2,128)(2,1)S(1)}, u32[]{:S(2)}, u32[]{:S(2)}) collective-permute-start(bf16[1,320]{1,0:T(2,128)(2,1)S(1)} %get-tuple-element.70), channel_id=1, source_target_pairs={{0,16},{8,24},{16,0},{24,8},{1,17},{9,25},{17,1},{25,9},{2,18},{10... | collective-permute-start | bytes 1928 | tf_op jit(solution)/shard_map/ppermute | solution.py:38
  176.8 4.4 %collective-permute-done.11 = bf16[8,40,640]{2,1,0:T(8,128)(2,1)} collective-permute-done((bf16[8,40,640]{2,1,0:T(8,128)(2,1)}, bf16[8,40,640]{2,1,0:T(8,128)(2,1)}, u32[]{:S(2)}, u32[]{:S(2)}) %collective-permute-start.11) | collective-permute-done | bytes 409632 | tf_op jit(solution)/shard_map/ppermute | solution.py:38
  183.7 4.8 %all-to-all-start.6 = ((bf16[8,80,160]{2,1,0:T(8,128)(2,1)}), bf16[8,80,160]{2,1,0:T(8,128)(2,1)}, u32[]{:S(2)}, u32[]{:S(2)}) async-start(bf16[8,80,160]{2,1,0:T(8,128)(2,1)} %get-tuple-element.42), calls=%async_computation.6 | async-start | bytes 655360 | tf_op jit(solution)/shard_map/all_to_all | solution.py:33
  190.6 4.7 %all-to-all-done.6 = bf16[8,80,160]{2,1,0:T(8,128)(2,1)} async-done(((bf16[8,80,160]{2,1,0:T(8,128)(2,1)}), bf16[8,80,160]{2,1,0:T(8,128)(2,1)}, u32[]{:S(2)}, u32[]{:S(2)}) %all-to-all-start.6) | async-done | bytes 204832 | tf_op jit(solution)/shard_map/all_to_all | solution.py:33
  195.3 4.1 %all-to-all-start.7 = ((bf16[8,40,768]{2,1,0:T(8,128)(2,1)}), bf16[8,40,768]{2,1,0:T(8,128)(2,1)}, u32[]{:S(2)}, u32[]{:S(2)}) async-start(bf16[8,40,768]{2,1,0:T(8,128)(2,1)} %fusion.7), calls=%async_computation.7 | async-start | bytes 983040 | tf_op jit(solution)/shard_map/all_to_all | solution.py:33
  202.1 14.0 %all-to-all-done.7 = bf16[8,40,768]{2,1,0:T(8,128)(2,1)} async-done(((bf16[8,40,768]{2,1,0:T(8,128)(2,1)}), bf16[8,40,768]{2,1,0:T(8,128)(2,1)}, u32[]{:S(2)}, u32[]{:S(2)}) %all-to-all-start.7) | async-done | bytes 491552 | tf_op jit(solution)/shard_map/all_to_all | solution.py:33
  (90 shorter events, 59.2 us)
Async XLA Ops:
  4.7 2.7 %collective-permute-start = (bf16[320,1280]{1,0:T(8,128)(2,1)}, bf16[320,1280]{1,0:T(8,128)(2,1)}, u32[]{:S(2)}, u32[]{:S(2)}) collective-permute-start(bf16[320,1280]{1,0:T(8,128)(2,1)} %convolution_convert_fusion.1), channel_id=1, source_target_pairs={{0,1},{1,0},{2,3},{3,2},{4,5},{5,4},{6,7},{7,6},{8,9},{9,8},{10,11... | collective-permute-start | bytes 2457608 | tf_op jit(solution)/shard_map/ppermute | solution.py:42
  10.6 17.4 %all-to-all-start = ((bf16[4,80,1280]{2,1,0:T(8,128)(2,1)}), bf16[4,80,1280]{2,1,0:T(8,128)(2,1)S(1)}, u32[]{:S(2)}, u32[]{:S(2)}) async-start(bf16[4,80,1280]{2,1,0:T(8,128)(2,1)} %bitcast.9), calls=%async_computation | async-start | bytes 1638400 | tf_op jit(solution)/shard_map/all_to_all | solution.py:33
  30.9 23.9 %all-to-all-start.1 = ((bf16[32,5,8,128]{3,2,1,0:T(8,128)(2,1)}), bf16[32,5,8,128]{3,2,1,0:T(8,128)(2,1)S(1)}, u32[]{:S(2)}, u32[]{:S(2)}) async-start(bf16[32,5,8,128]{3,2,1,0:T(8,128)(2,1)} %spread.1), calls=%async_computation.1 | async-start | bytes 655360 | tf_op jit(solution)/shard_map/all_to_all | solution.py:33
  57.5 17.2 %all-to-all-start.2 = ((bf16[32,5,8,128]{3,2,1,0:T(8,128)(2,1)}), bf16[32,5,8,128]{3,2,1,0:T(8,128)(2,1)S(1)}, u32[]{:S(2)}, u32[]{:S(2)}) async-start(bf16[32,5,8,128]{3,2,1,0:T(8,128)(2,1)} %bitcast.75), calls=%async_computation.2 | async-start | bytes 655360 | tf_op jit(solution)/shard_map/all_to_all | solution.py:33
  61.5 10.2 %collective-permute-start.4 = (bf16[160,640]{1,0:T(8,128)(2,1)S(1)}, bf16[160,640]{1,0:T(8,128)(2,1)S(1)}, u32[]{:S(2)}, u32[]{:S(2)}) collective-permute-start(bf16[160,640]{1,0:T(8,128)(2,1)S(1)} %bitcast.84), channel_id=1, source_target_pairs={{0,6},{2,0},{4,2},{6,4},{1,7},{3,1},{5,3},{7,5},{8,14},{10,8},{12,... | collective-permute-start | bytes 614408 | tf_op jit(solution)/shard_map/ppermute | solution.py:38
  63.0 8.7 %collective-permute-start.3 = (bf16[160,640]{1,0:T(8,128)(2,1)S(1)}, bf16[160,640]{1,0:T(8,128)(2,1)S(1)}, u32[]{:S(2)}, u32[]{:S(2)}) collective-permute-start(bf16[160,640]{1,0:T(8,128)(2,1)S(1)} %bitcast.85), channel_id=1, source_target_pairs={{0,4},{2,6},{4,0},{6,2},{1,5},{3,7},{5,1},{7,3},{8,12},{10,14},{12... | collective-permute-start | bytes 614408 | tf_op jit(solution)/shard_map/ppermute | solution.py:38
  63.1 10.1 %collective-permute-start.2 = (bf16[160,640]{1,0:T(8,128)(2,1)S(1)}, bf16[160,640]{1,0:T(8,128)(2,1)S(1)}, u32[]{:S(2)}, u32[]{:S(2)}) collective-permute-start(bf16[160,640]{1,0:T(8,128)(2,1)S(1)} %bitcast.86), channel_id=1, source_target_pairs={{0,2},{2,4},{4,6},{6,0},{1,3},{3,5},{5,7},{7,1},{8,10},{10,12},{12... | collective-permute-start | bytes 614408 | tf_op jit(solution)/shard_map/ppermute | solution.py:38
  74.3 20.5 %collective-permute-start.5 = (bf16[4,160,640]{2,1,0:T(8,128)(2,1)}, bf16[4,160,640]{2,1,0:T(8,128)(2,1)}, u32[]{:S(2)}, u32[]{:S(2)}) collective-permute-start(bf16[4,160,640]{2,1,0:T(8,128)(2,1)} %pad_maximum_fusion.own_ref), channel_id=1, source_target_pairs={{0,1},{1,0},{2,3},{3,2},{4,5},{5,4},{6,7},{7,6},{8,9},{9,8},{10,11... | collective-permute-start | bytes 2457608 | tf_op jit(solution)/shard_map/ppermute | solution.py:42
  77.5 17.2 %all-to-all-start.3 = ((bf16[4,80,1280]{2,1,0:T(8,128)(2,1)}), bf16[4,80,1280]{2,1,0:T(8,128)(2,1)S(1)}, u32[]{:S(2)}, u32[]{:S(2)}) async-start(bf16[4,80,1280]{2,1,0:T(8,128)(2,1)} %bitcast.80), calls=%async_computation.3 | async-start | bytes 1638400 | tf_op jit(solution)/shard_map/all_to_all | solution.py:33
  87.2 31.3 %collective-permute-start.7 = (bf16[8,40,1024]{2,1,0:T(8,128)(2,1)}, bf16[8,40,1024]{2,1,0:T(8,128)(2,1)}, u32[]{:S(2)}, u32[]{:S(2)}) collective-permute-start(bf16[8,40,1024]{2,1,0:T(8,128)(2,1)} %get-tuple-element.65), channel_id=1, source_target_pairs={{0,16},{8,24},{16,0},{24,8},{1,17},{9,25},{17,1},{25,9},{2,18},{10... | collective-permute-start | bytes 1966088 | tf_op jit(solution)/shard_map/ppermute | solution.py:38
  90.2 29.8 %collective-permute-start.9 = (bf16[8,40,1024]{2,1,0:T(8,128)(2,1)}, bf16[8,40,1024]{2,1,0:T(8,128)(2,1)}, u32[]{:S(2)}, u32[]{:S(2)}) collective-permute-start(bf16[8,40,1024]{2,1,0:T(8,128)(2,1)} %get-tuple-element.66), channel_id=1, source_target_pairs={{0,24},{8,0},{16,8},{24,16},{1,25},{9,1},{17,9},{25,17},{2,26},{10... | collective-permute-start | bytes 1966088 | tf_op jit(solution)/shard_map/ppermute | solution.py:38
  91.4 28.6 %collective-permute-start.8 = (bf16[8,40,1024]{2,1,0:T(8,128)(2,1)}, bf16[8,40,1024]{2,1,0:T(8,128)(2,1)}, u32[]{:S(2)}, u32[]{:S(2)}) collective-permute-start(bf16[8,40,1024]{2,1,0:T(8,128)(2,1)} %get-tuple-element.67), channel_id=1, source_target_pairs={{0,8},{8,16},{16,24},{24,0},{1,9},{9,17},{17,25},{25,1},{2,10},{10... | collective-permute-start | bytes 1966088 | tf_op jit(solution)/shard_map/ppermute | solution.py:38
  94.7 11.7 %collective-permute-start.1 = (bf16[4,5,16,1280]{3,2,1,0:T(8,128)(2,1)S(1)}, bf16[4,5,16,1280]{3,2,1,0:T(8,128)(2,1)}, u32[]{:S(2)}, u32[]{:S(2)}) collective-permute-start(bf16[4,5,16,1280]{3,2,1,0:T(8,128)(2,1)S(1)} %bitcast.78), channel_id=1, source_target_pairs={{0,1},{1,0},{2,3},{3,2},{4,5},{5,4},{6,7},{7,6},{8,9},{9,8},{10,11... | collective-permute-start | bytes 2457608 | tf_op jit(solution)/shard_map/ppermute | solution.py:42
  118.2 11.5 %collective-permute-start.6 = (bf16[4,6,16,1280]{3,2,1,0:T(8,128)(2,1)}, bf16[4,6,16,1280]{3,2,1,0:T(8,128)(2,1)}, u32[]{:S(2)}, u32[]{:S(2)}) collective-permute-start(bf16[4,6,16,1280]{3,2,1,0:T(8,128)(2,1)} %get-tuple-element.37), channel_id=1, source_target_pairs={{0,1},{1,0},{2,3},{3,2},{4,5},{5,4},{6,7},{7,6},{8,9},{9,8},{10,11... | collective-permute-start | bytes 2949128 | tf_op jit(solution)/shard_map/ppermute | solution.py:42
  123.0 27.1 %all-to-all-start.4 = ((bf16[8,40,1024]{2,1,0:T(8,128)(2,1)}), bf16[8,40,1024]{2,1,0:T(8,128)(2,1)S(1)}, u32[]{:S(2)}, u32[]{:S(2)}) async-start(bf16[8,40,1024]{2,1,0:T(8,128)(2,1)} %fusion.4), calls=%async_computation.4 | async-start | bytes 1310720 | tf_op jit(solution)/shard_map/all_to_all | solution.py:33
  150.1 18.0 %all-to-all-start.5 = ((bf16[4,96,1280]{2,1,0:T(8,128)(2,1)}), bf16[4,96,1280]{2,1,0:T(8,128)(2,1)}, u32[]{:S(2)}, u32[]{:S(2)}) async-start(bf16[4,96,1280]{2,1,0:T(8,128)(2,1)} %bitcast.70), calls=%async_computation.5 | async-start | bytes 1966080 | tf_op jit(solution)/shard_map/all_to_all | solution.py:33
  159.8 16.2 %collective-permute-start.10 = (bf16[8,40,640]{2,1,0:T(8,128)(2,1)}, bf16[8,40,640]{2,1,0:T(8,128)(2,1)}, u32[]{:S(2)}, u32[]{:S(2)}) collective-permute-start(bf16[8,40,640]{2,1,0:T(8,128)(2,1)} %get-tuple-element.49), channel_id=1, source_target_pairs={{0,16},{8,24},{16,0},{24,8},{1,17},{9,25},{17,1},{25,9},{2,18},{10... | collective-permute-start | bytes 1228808 | tf_op jit(solution)/shard_map/ppermute | solution.py:38
  162.8 18.5 %collective-permute-start.11 = (bf16[8,40,640]{2,1,0:T(8,128)(2,1)}, bf16[8,40,640]{2,1,0:T(8,128)(2,1)}, u32[]{:S(2)}, u32[]{:S(2)}) collective-permute-start(bf16[8,40,640]{2,1,0:T(8,128)(2,1)} %get-tuple-element.50), channel_id=1, source_target_pairs={{0,8},{8,16},{16,24},{24,0},{1,9},{9,17},{17,25},{25,1},{2,10},{10... | collective-permute-start | bytes 1228808 | tf_op jit(solution)/shard_map/ppermute | solution.py:38
  163.3 18.0 %collective-permute-start.12 = (bf16[8,40,640]{2,1,0:T(8,128)(2,1)}, bf16[8,40,640]{2,1,0:T(8,128)(2,1)}, u32[]{:S(2)}, u32[]{:S(2)}) collective-permute-start(bf16[8,40,640]{2,1,0:T(8,128)(2,1)} %get-tuple-element.51), channel_id=1, source_target_pairs={{0,24},{8,0},{16,8},{24,16},{1,25},{9,1},{17,9},{25,17},{2,26},{10... | collective-permute-start | bytes 1228808 | tf_op jit(solution)/shard_map/ppermute | solution.py:38
  171.8 16.7 %collective-permute-start.13 = (bf16[1,320]{1,0:T(2,128)(2,1)S(1)}, bf16[1,320]{1,0:T(2,128)(2,1)S(1)}, u32[]{:S(2)}, u32[]{:S(2)}) collective-permute-start(bf16[1,320]{1,0:T(2,128)(2,1)S(1)} %get-tuple-element.70), channel_id=1, source_target_pairs={{0,16},{8,24},{16,0},{24,8},{1,17},{9,25},{17,1},{25,9},{2,18},{10... | collective-permute-start | bytes 1928 | tf_op jit(solution)/shard_map/ppermute | solution.py:38
  174.8 13.7 %collective-permute-start.15 = (bf16[1,320]{1,0:T(2,128)(2,1)S(1)}, bf16[1,320]{1,0:T(2,128)(2,1)S(1)}, u32[]{:S(2)}, u32[]{:S(2)}) collective-permute-start(bf16[1,320]{1,0:T(2,128)(2,1)S(1)} %get-tuple-element.71), channel_id=1, source_target_pairs={{0,24},{8,0},{16,8},{24,16},{1,25},{9,1},{17,9},{25,17},{2,26},{10... | collective-permute-start | bytes 1928 | tf_op jit(solution)/shard_map/ppermute | solution.py:38
  176.0 12.5 %collective-permute-start.14 = (bf16[1,320]{1,0:T(2,128)(2,1)S(1)}, bf16[1,320]{1,0:T(2,128)(2,1)S(1)}, u32[]{:S(2)}, u32[]{:S(2)}) collective-permute-start(bf16[1,320]{1,0:T(2,128)(2,1)S(1)} %get-tuple-element.72), channel_id=1, source_target_pairs={{0,8},{8,16},{16,24},{24,0},{1,9},{9,17},{17,25},{25,1},{2,10},{10... | collective-permute-start | bytes 1928 | tf_op jit(solution)/shard_map/ppermute | solution.py:38
  183.7 11.7 %all-to-all-start.6 = ((bf16[8,80,160]{2,1,0:T(8,128)(2,1)}), bf16[8,80,160]{2,1,0:T(8,128)(2,1)}, u32[]{:S(2)}, u32[]{:S(2)}) async-start(bf16[8,80,160]{2,1,0:T(8,128)(2,1)} %get-tuple-element.42), calls=%async_computation.6 | async-start | bytes 655360 | tf_op jit(solution)/shard_map/all_to_all | solution.py:33
  195.3 20.8 %all-to-all-start.7 = ((bf16[8,40,768]{2,1,0:T(8,128)(2,1)}), bf16[8,40,768]{2,1,0:T(8,128)(2,1)}, u32[]{:S(2)}, u32[]{:S(2)}) async-start(bf16[8,40,768]{2,1,0:T(8,128)(2,1)} %fusion.7), calls=%async_computation.7 | async-start | bytes 983040 | tf_op jit(solution)/shard_map/all_to_all | solution.py:33
  (10 other events, 88.9 us)

commit v5 on v4

--- a/solution.py
+++ b/solution.py
@@ -243,95 +243,75 @@
     packed_grad_ref,
     in_own_ref,
     in_other_ref,
-    gain_term,
     wout_pad,
 ):
-    step = pl.program_id(0)
-
-    @pl.when(step == 0)
-    def _():
-        gain_term[...] = jnp.zeros_like(gain_term)
-        padded_heads(wout_pad, wout_ref)
-
-    @pl.when(step < IMG)
-    def _():
-        first = words_ref[0] == 0
-        own = own_ref[...].reshape(64, WIDTH)
-        other = other_ref[...].reshape(64, WIDTH)
-        upstream = jnp.concatenate(
-            [jnp.where(first, own, other), jnp.where(first, other, own)], axis=0
-        )
-        upstream_ref[...] = upstream
-        mixed_grads = dot(upstream, wout_pad[...], 1, 1).astype(BF)
+    padded_heads(wout_pad, wout_ref)
+    first = words_ref[0] == 0
+    for image in range(IMG):
+        own = own_ref[:, image].reshape(64, WIDTH)
+        other = other_ref[:, image].reshape(64, WIDTH)
+        at = image * TILE
+        upstream_ref[at : at + 64] = jnp.where(first, own, other)
+        upstream_ref[at + 64 : at + TILE] = jnp.where(first, other, own)
+    mixed_grads = dot(upstream_ref[...], wout_pad[...], 1, 1).astype(BF)
+
+    units = [(image, head) for image in range(IMG) for head in range(2)]
+
+    def part(image, head, which):
+        lane = (head * 3 + which) * LANE
+        return packed_ref[image * TILE : (image + 1) * TILE, lane : lane + LANE]
+
+    grads = [
+        mixed_grads[image * TILE : (image + 1) * TILE, head * LANE : (head + 1) * LANE]
+        for image, head in units
+    ]
+    prob_grads = [dot(grad, part(*unit, 2), 1, 1) for grad, unit in zip(grads, units)]
+    score_grads = []
+    for (image, head), prob_grad in zip(units, prob_grads):
+        probability = prob_ref[image, head]
+        inner = jnp.sum(probability * prob_grad, axis=-1, keepdims=True)
+        score_grads.append((probability * (prob_grad - inner) * SCALING).astype(BF))
+    query_grads = [dot(grad, part(*unit, 1), 1, 0) for grad, unit in zip(score_grads, units)]
+    key_grads = [dot(grad, part(*unit, 0), 0, 0) for grad, unit in zip(score_grads, units)]
+    value_grads = [
+        dot(prob_ref[image, head].astype(BF), grad, 0, 0)
+        for grad, (image, head) in zip(grads, units)
+    ]
+    for image in range(IMG):
         pieces = []
         for head in range(2):
-            query, key, value = (
-                packed_ref[:, (head * 3 + i) * LANE : (head * 3 + i + 1) * LANE]
-                for i in range(3)
-            )
-            probability = prob_ref[0, head]
-            mixed_grad = mixed_grads[:, head * LANE : (head + 1) * LANE]
-            prob_grad = dot(mixed_grad, value, 1, 1)
-            inner = jnp.sum(probability * prob_grad, axis=-1, keepdims=True)
-            score_grad = (probability * (prob_grad - inner) * SCALING).astype(BF)
-            pieces.append(dot(score_grad, key, 1, 0))
-            pieces.append(dot(score_grad, query, 0, 0))
-            pieces.append(dot(probability.astype(BF), mixed_grad, 0, 0))
-        packed_grad = shifted_sum(pieces, 512)[:, :480].astype(BF)
-        packed_grad_ref[...] = packed_grad
-        in_part = dot(packed_grad, w_ref[...], 1, 0).astype(BF)
-        gain_term[...] += jnp.sum(
-            in_part.astype(F32) * normed_ref[...].astype(F32), axis=0, keepdims=True
-        )
-        low, high = in_part[:64], in_part[64:]
-        in_own_ref[...] = jnp.where(first, low, high).reshape(4, 1, 16, WIDTH)
-        in_other_ref[...] = jnp.where(first, high, low).reshape(4, 1, 16, WIDTH)
-
-    @pl.when(step == IMG)
-    def _():
-        row = lax.broadcasted_iota(jnp.int32, (16, WIDTH), 0)
-        plane = jnp.where(row == 0, gain_term[...], 0.0).astype(BF)
-        for peer in range(4):
-            in_own_ref[peer, 0] = plane
-            in_other_ref[peer, 0] = plane
+            at = image * 2 + head
+            pieces += [query_grads[at], key_grads[at], value_grads[at]]
+        packed_grad_ref[image * TILE : (image + 1) * TILE] = shifted_sum(pieces, 512)[
+            :, :480
+        ].astype(BF)
+    in_parts = dot(packed_grad_ref[...], w_ref[...], 1, 0).astype(BF)
+    gain_term = jnp.sum(in_parts.astype(F32) * normed_ref[...].astype(F32), axis=0, keepdims=True)
+    row = lax.broadcasted_iota(jnp.int32, (16, WIDTH), 0)
+    plane = jnp.where(row == 0, gain_term, 0.0).astype(BF)
+    for near in range(4):
+        to = lax.rem(near + 4 - words_ref[2], 4)
+        for image in range(IMG):
+            at = image * TILE + near * 16
+            low, high = in_parts[at : at + 16], in_parts[at + 64 : at + 80]
+            in_own_ref[to, image] = jnp.where(first, low, high)
+            in_other_ref[to, image] = jnp.where(first, high, low)
+        in_own_ref[near, IMG] = plane
+        in_other_ref[near, IMG] = plane
 
 
 def backward(words, own, other, w_out, w_heads, packed, prob, normed):
-    def image(i):
-        return jnp.minimum(i, IMG - 1)
-
-    quarter = pl.BlockSpec((4, 1, 16, WIDTH), lambda i: (0, image(i), 0, 0))
-    plane = pl.BlockSpec((4, 1, 16, WIDTH), lambda i: (0, i, 0, 0))
-    rows = pl.BlockSpec((TILE, WIDTH), lambda i: (image(i), 0))
     return pl.pallas_call(
         backward_kernel,
-        grid=(IMG + 1,),
         out_shape=(
             jax.ShapeDtypeStruct((ROWS, WIDTH), BF),
             jax.ShapeDtypeStruct((ROWS, 6 * HEAD), BF),
             jax.ShapeDtypeStruct((4, IMG + 1, 16, WIDTH), BF),
             jax.ShapeDtypeStruct((4, IMG + 1, 16, WIDTH), BF),
         ),
-        in_specs=[
-            smem(),
-            quarter,
-            quarter,
-            pl.BlockSpec((2 * HEAD, WIDTH), lambda i: (0, 0)),
-            pl.BlockSpec((6 * HEAD, WIDTH), lambda i: (0, 0)),
-            pl.BlockSpec((TILE, 6 * LANE), lambda i: (image(i), 0)),
-            pl.BlockSpec((1, 2, TILE, TILE), lambda i: (image(i), 0, 0, 0)),
-            rows,
-        ],
-        out_specs=(
-            rows,
-            pl.BlockSpec((TILE, 6 * HEAD), lambda i: (image(i), 0)),
-            plane,
-            plane,
-        ),
-        scratch_shapes=[
-            pltpu.VMEM((1, WIDTH), F32),
-            pltpu.VMEM((2 * LANE, WIDTH), BF),
-        ],
+        in_specs=[smem()] + [pl.BlockSpec(memory_space=pltpu.VMEM)] * 7,
+        out_specs=(pl.BlockSpec(memory_space=pltpu.VMEM),) * 4,
+        scratch_shapes=[pltpu.VMEM((2 * LANE, WIDTH), BF)],
         cost_estimate=pl.CostEstimate(
             flops=10_000_000_000, bytes_accessed=10_000_000, transcendentals=0
         ),
@@ -375,14 +355,15 @@
     )(words, normed, upstream, packed_grad, mixed)
 
 
-def norm_back_kernel(arrived_ref, block_ref, upstream_ref, gain_ref, out_ref, term_ref):
+def norm_back_kernel(
+    own_ref, got_ref, got2_ref, got3_ref, block_ref, upstream_ref, gain_ref, out_ref, term_ref
+):
     gain = gain_ref[...]
     results = []
     for image in range(IMG + 1):
-        rows = slice(image * 16, image * 16 + 16)
-        incoming = arrived_ref[0, rows].astype(F32)
-        for peer in range(1, 4):
-            incoming = incoming + arrived_ref[peer, rows].astype(F32)
+        incoming = own_ref[image].astype(F32)
+        for more_ref in (got_ref, got2_ref, got3_ref):
+            incoming = incoming + more_ref[image].astype(F32)
         if image == IMG:
             term_ref[...] = incoming[:8]
             continue
@@ -402,17 +383,17 @@
         out_ref[share] = window[:, :160].astype(BF)
 
 
-def norm_back(arrived, block_rows, upstream_rows, gain):
+def norm_back(parts, block_rows, upstream_rows, gain):
     return pl.pallas_call(
         norm_back_kernel,
         out_shape=(
             jax.ShapeDtypeStruct((8, 80, 160), BF),
             jax.ShapeDtypeStruct((8, WIDTH), F32),
         ),
-        in_specs=[pl.BlockSpec(memory_space=pltpu.VMEM)] * 4,
+        in_specs=[pl.BlockSpec(memory_space=pltpu.VMEM)] * 7,
         out_specs=(pl.BlockSpec(memory_space=pltpu.VMEM),) * 2,
         name="norm_back",
-    )(arrived, block_rows, upstream_rows, gain)
+    )(*parts, block_rows, upstream_rows, gain)
 
 
 def summed(blocks):
@@ -503,13 +484,13 @@
     )
     in_got = swapped(in_other)
     terms = weight_terms(words, normed_in, upstream, packed_grad, mixed)
-    in_pair = (in_own.astype(F32) + in_got.astype(F32)).astype(BF)
-    in_pair = in_pair.reshape(4, 96, WIDTH)
-    in_pair, proj_far = lax.optimization_barrier((in_pair, proj_far))
     grad_proj = summed(proj_far)
-    in_arrived = exchanged(in_pair, "y")
+    in_pair = [
+        (own.astype(F32) + got.astype(F32)).astype(BF) for own, got in zip(in_own, in_got)
+    ]
+    in_parts = [in_pair[0]] + [shifted(in_pair[at], "y", at) for at in (2, 1, 3)]
     term_near = near_sum(terms)
-    shares, gain_term = norm_back(in_arrived, block_rows, upstream_rows, gain)
+    shares, gain_term = norm_back(in_parts, block_rows, upstream_rows, gain)
     shares = exchanged(shares, TP)
     grad_input = shares.reshape(4, 2, IMG, 16, 160).transpose(2, 1, 0, 3, 4)
     grad_input = grad_input.reshape(ROWS, 160)

time: 222 us -> 234 us (1.054)
  waiting for transfers between devices: 75.7 us -> 92.5 us
  Pallas kernels: 37 us -> 32.4 us
    ppermute x12 -> x15, waiting for transfers between devices: 13.6 us -> 42.8 us  [shifted(): return lax.ppermute(values, axis, pairs)]
    all_to_all x8 -> x7, waiting for transfers between devices: 59.6 us -> 47.2 us  [exchanged(): return lax.all_to_all(blocks, axis, split_axis=0, concat_axis=0, tiled=True)]
    pallas_call x1, Pallas kernels: 11.8 us -> 7.2 us  [backward(): pl.pallas_call(backward_kernel, out_shape=(jax.ShapeDtypeStruct((ROWS, WI...]
    ppermute x12 -> x15, starting transfers between devices: 20.5 us -> 23.7 us  [shifted(): return lax.ppermute(values, axis, pairs)]
    all_to_all x8 -> x7, starting transfers between devices: 45.4 us -> 42.6 us  [exchanged(): return lax.all_to_all(blocks, axis, split_axis=0, concat_axis=0, tiled=True)]
  transfers between devices with their start and end apart: 24 -> 26, of which waited for: 14 -> 13; matrix products, arithmetic and copies ran while one was open for 12% -> 11% of each run, Pallas kernels for 15% -> 9%
where the time goes in v5:
time: 234 us; the launch traced here: 232 us
  waiting for transfers between devices  92.5 us (40%)
  starting transfers between devices  66.6 us (28%)
  Pallas kernels  32.4 us (14%)
  local copies, waits for them, and re-layouts  15.2 us (6%)
  other arithmetic  14.2 us (6%)
  matrix products  9.81 us (4%)
    all_to_all x7, waiting for transfers between devices, exchanged(): return lax.all_to_all(blocks, axis, split_axis=0, concat_axis=0, tiled=True)  47.2 us
    ppermute x15, waiting for transfers between devices, shifted(): return lax.ppermute(values, axis, pairs)  42.8 us
    all_to_all x7, starting transfers between devices, exchanged(): return lax.all_to_all(blocks, axis, split_axis=0, concat_axis=0, tiled=True)  42.6 us
    ppermute x15, starting transfers between devices, shifted(): return lax.ppermute(values, axis, pairs)  23.7 us
    pallas_call x1, Pallas kernels, attention(): pl.pallas_call(attention_kernel, grid=(IMG,), out_shape=(jax.ShapeDtypeSt...  11.7 us
    dot_general x3, matrix products, dot(): lax.dot_general(left, right, (((dim_left,), (dim_right,)), ((), ())), pre...  9.81 us
    pallas_call x1, Pallas kernels, backward(): pl.pallas_call(backward_kernel, out_shape=(jax.ShapeDtypeStruct((ROWS, WI...  7.2 us
    convert_element_type x3, other arithmetic, near_sum(): return total.astype(BF)  5.13 us
  transfers between devices with their start and end apart: 26, of which 13 were waited for; matrix products, arithmetic and copies ran while one was open for 11% of the time, Pallas kernels for 9%

profile of v5, /device:TPU:8, one launch (start us, length us, event | category | flops | bytes accessed | tf_op | source)
XLA Modules:
  0.0 231.6 jit_solution(9845704234253055577)
XLA Ops:
  10.6 5.6 %all-to-all-start = ((bf16[4,80,1280]{2,1,0:T(8,128)(2,1)}), bf16[4,80,1280]{2,1,0:T(8,128)(2,1)S(1)}, u32[]{:S(2)}, u32[]{:S(2)}) async-start(bf16[4,80,1280]{2,1,0:T(8,128)(2,1)} %bitcast.9), calls=%async_computation | async-start | bytes 1638400 | tf_op jit(solution)/shard_map/all_to_all | solution.py:33
  16.3 5.7 %convolution_convert_fusion = bf16[1280,1024]{1,0:T(8,128)(2,1)} fusion(bf16[640,1024]{1,0:T(8,128)(2,1)} %param.9, bf16[640,1280]{1,0:T(8,128)(2,1)} %param.10, pred[640]{0:T(1024)(128)(4,1)S(1)} %fusion.13), kind=kOutput, calls=%fused_computation | convolution fusion | flops 1679851520 | bytes 5571200 | tf_op jit(solution)/shard_map/dot_general | solution.py:46
  21.9 6.0 %all-to-all-done = bf16[4,80,1280]{2,1,0:T(8,128)(2,1)S(1)} async-done(((bf16[4,80,1280]{2,1,0:T(8,128)(2,1)}), bf16[4,80,1280]{2,1,0:T(8,128)(2,1)S(1)}, u32[]{:S(2)}, u32[]{:S(2)}) %all-to-all-start) | async-done | bytes 819232 | tf_op jit(solution)/shard_map/all_to_all | solution.py:33
  30.9 10.5 %all-to-all-start.1 = ((bf16[32,5,8,128]{3,2,1,0:T(8,128)(2,1)}), bf16[32,5,8,128]{3,2,1,0:T(8,128)(2,1)S(1)}, u32[]{:S(2)}, u32[]{:S(2)}) async-start(bf16[32,5,8,128]{3,2,1,0:T(8,128)(2,1)} %spread.1), calls=%async_computation.1 | async-start | bytes 655360 | tf_op jit(solution)/shard_map/all_to_all | solution.py:33
  42.7 12.1 %all-to-all-done.1 = bf16[32,5,8,128]{3,2,1,0:T(8,128)(2,1)S(1)} async-done(((bf16[32,5,8,128]{3,2,1,0:T(8,128)(2,1)}), bf16[32,5,8,128]{3,2,1,0:T(8,128)(2,1)S(1)}, u32[]{:S(2)}, u32[]{:S(2)}) %all-to-all-start.1) | async-done | bytes 327712 | tf_op jit(solution)/shard_map/all_to_all | solution.py:33
  57.5 3.9 %all-to-all-start.2 = ((bf16[32,5,8,128]{3,2,1,0:T(8,128)(2,1)}), bf16[32,5,8,128]{3,2,1,0:T(8,128)(2,1)S(1)}, u32[]{:S(2)}, u32[]{:S(2)}) async-start(bf16[32,5,8,128]{3,2,1,0:T(8,128)(2,1)} %bitcast.81), calls=%async_computation.2 | async-start | bytes 655360 | tf_op jit(solution)/shard_map/all_to_all | solution.py:33
  65.6 6.1 %collective-permute-done.4 = bf16[160,640]{1,0:T(8,128)(2,1)S(1)} collective-permute-done((bf16[160,640]{1,0:T(8,128)(2,1)S(1)}, bf16[160,640]{1,0:T(8,128)(2,1)S(1)}, u32[]{:S(2)}, u32[]{:S(2)}) %collective-permute-start.4) | collective-permute-done | bytes 204832 | tf_op jit(solution)/shard_map/ppermute | solution.py:38
  77.5 5.1 %all-to-all-start.3 = ((bf16[4,80,1280]{2,1,0:T(8,128)(2,1)}), bf16[4,80,1280]{2,1,0:T(8,128)(2,1)S(1)}, u32[]{:S(2)}, u32[]{:S(2)}) async-start(bf16[4,80,1280]{2,1,0:T(8,128)(2,1)} %bitcast.86), calls=%async_computation.3 | async-start | bytes 1638400 | tf_op jit(solution)/shard_map/all_to_all | solution.py:33
  84.4 10.3 %all-to-all-done.3 = bf16[4,80,1280]{2,1,0:T(8,128)(2,1)S(1)} async-done(((bf16[4,80,1280]{2,1,0:T(8,128)(2,1)}), bf16[4,80,1280]{2,1,0:T(8,128)(2,1)S(1)}, u32[]{:S(2)}, u32[]{:S(2)}) %all-to-all-start.3) | async-done | bytes 819232 | tf_op jit(solution)/shard_map/all_to_all | solution.py:33
  94.7 11.7 %attention.1 = (bf16[640,1280]{1,0:T(8,128)(2,1)}, bf16[640,1280]{1,0:T(8,128)(2,1)}, bf16[5,16,1280]{2,1,0:T(8,128)(2,1)}, bf16[640,768]{1,0:T(8,128)(2,1)}, f3...) custom-call(s32[4]{0:T(128)} %pad_add_fusion.words_ref, s32[5]{0:T(128)} %dynamic_slice.43.counts_ref, ...), custom_call_target="tpu_custom_call" | custom-call | flops 10000000000 | bytes 10000000 | tf_op jit(solution)/shard_map/attention/pallas_call | solution.py:198
  106.4 7.2 %backward.1 = (bf16[640,1280]{1,0:T(8,128)(2,1)}, bf16[640,480]{1,0:T(8,128)(2,1)}, bf16[4,6,16,1280]{3,2,1,0:T(8,128)(2,1)}, bf16[4,6,16,1280]{3,2,1,0:T(8,128)(2,1)}) custom-call(s32[4]{0:T(128)} %pad_add_fusion.words_ref, bf16[4,5,16,1280]{3,2,1,0:T(8,128)(2,1)} %bitcast.85, bf16[4,5,16,1280]{3,2,1,0:T(8,128)(2,1)} %collective-permute-done.1.other_ref, ...), custom_call_target="tpu_custom_call" | custom-call | flops 10000000000 | bytes 10000000 | tf_op jit(solution)/shard_map/backward/pallas_call | solution.py:304
  113.8 2.8 %dynamic-slice_bitcast_fusion.2 = (bf16[8,40,1024]{2,1,0:T(8,128)(2,1)}, bf16[8,40,1024]{2,1,0:T(8,128)(2,1)}, bf16[8,40,1024]{2,1,0:T(8,128)(2,1)}) fusion(bf16[8,4,40,1024]{3,2,1,0:T(8,128)(2,1)} %bitcast.78, s32[]{:T(128)S(6)} %select_n.65, s32[]{:T(128)S(6)} %select_n.67, s32[]{:T(128)S(6)} %select_n.66), kind=kLoop, calls=%fused_computation.18 | loop fusion | bytes 3932172 | tf_op jit(solution)/shard_map/jit(dynamic_index_in_dim)/squeeze | solution.py:411
  116.7 3.0 %collective-permute-start.10 = (bf16[8,40,1024]{2,1,0:T(8,128)(2,1)}, bf16[8,40,1024]{2,1,0:T(8,128)(2,1)S(1)}, u32[]{:S(2)}, u32[]{:S(2)}) collective-permute-start(bf16[8,40,1024]{2,1,0:T(8,128)(2,1)} %get-tuple-element.61), channel_id=1, source_target_pairs={{0,16},{8,24},{16,0},{24,8},{1,17},{9,25},{17,1},{25,9},{2,18},{10... | collective-permute-start | bytes 1966088 | tf_op jit(solution)/shard_map/ppermute | solution.py:38
  121.7 14.3 %collective-permute-done.10 = bf16[8,40,1024]{2,1,0:T(8,128)(2,1)S(1)} collective-permute-done((bf16[8,40,1024]{2,1,0:T(8,128)(2,1)}, bf16[8,40,1024]{2,1,0:T(8,128)(2,1)S(1)}, u32[]{:S(2)}, u32[]{:S(2)}) %collective-permute-start.10) | collective-permute-done | bytes 655392 | tf_op jit(solution)/shard_map/ppermute | solution.py:38
  136.0 13.5 %collective-permute-done.12 = bf16[8,40,1024]{2,1,0:T(8,128)(2,1)} collective-permute-done((bf16[8,40,1024]{2,1,0:T(8,128)(2,1)}, bf16[8,40,1024]{2,1,0:T(8,128)(2,1)}, u32[]{:S(2)}, u32[]{:S(2)}) %collective-permute-start.12) | collective-permute-done | bytes 655392 | tf_op jit(solution)/shard_map/ppermute | solution.py:38
  149.5 2.8 %fusion.4 = bf16[8,40,1024]{2,1,0:T(8,128)(2,1)} fusion(bf16[8,40,1024]{2,1,0:T(8,128)(2,1)} %collective-permute-done.12, bf16[8,40,1024]{2,1,0:T(8,128)(2,1)} %collective-permute-done.11, bf16[8,40,1024]{2,1,0:T(8,128)(2,1)S(1)} %collective-permute-done.10, bf16[8,4,40,1024]{3,2,1,0:T(8,128)(2,1)} %bitcast.79, s32[]{:T(128)S(6)} %select_n.64), kind=kLoop, calls=%fused_computation.8 | loop fusion | flops 2621440 | bytes 3276804 | tf_op jit(solution)/shard_map/convert_element_type | solution.py:421
  152.3 6.7 %all-to-all-start.5 = ((bf16[8,40,1024]{2,1,0:T(8,128)(2,1)}), bf16[8,40,1024]{2,1,0:T(8,128)(2,1)S(1)}, u32[]{:S(2)}, u32[]{:S(2)}) async-start(bf16[8,40,1024]{2,1,0:T(8,128)(2,1)} %fusion.4), calls=%async_computation.5 | async-start | bytes 1310720 | tf_op jit(solution)/shard_map/all_to_all | solution.py:33
  166.4 4.8 %weight_terms.1 = (bf16[8,40,640]{2,1,0:T(8,128)(2,1)}, bf16[8,40,640]{2,1,0:T(8,128)(2,1)}, bf16[8,40,640]{2,1,0:T(8,128)(2,1)}, bf16[8,40,640]{2,1,0:T(8,128)(2,1)}) custom-call(s32[4]{0:T(128)} %pad_add_fusion.words_ref, bf16[640,1280]{1,0:T(8,128)(2,1)} %get-tuple-element.40.normed_ref, bf16[640,1280]{1,0:T(8,128)(2,1)} %get-tuple-element.41.upstream_ref, ...), custom_call_target="tpu_custom_call" | custom-call | flops 4000000000 | bytes 6000000 | tf_op jit(solution)/shard_map/weight_terms/pallas_call | solution.py:338
  171.2 2.9 %collective-permute-start.13 = (bf16[8,40,640]{2,1,0:T(8,128)(2,1)}, bf16[8,40,640]{2,1,0:T(8,128)(2,1)}, u32[]{:S(2)}, u32[]{:S(2)}) collective-permute-start(bf16[8,40,640]{2,1,0:T(8,128)(2,1)} %get-tuple-element.45), channel_id=1, source_target_pairs={{0,16},{8,24},{16,0},{24,8},{1,17},{9,25},{17,1},{25,9},{2,18},{10... | collective-permute-start | bytes 1228808 | tf_op jit(solution)/shard_map/ppermute | solution.py:38
  186.9 5.2 %collective-permute-done.14 = bf16[8,40,640]{2,1,0:T(8,128)(2,1)} collective-permute-done((bf16[8,40,640]{2,1,0:T(8,128)(2,1)}, bf16[8,40,640]{2,1,0:T(8,128)(2,1)}, u32[]{:S(2)}, u32[]{:S(2)}) %collective-permute-start.14) | collective-permute-done | bytes 409632 | tf_op jit(solution)/shard_map/ppermute | solution.py:38
  194.5 4.0 %all-to-all-start.4 = ((bf16[8,80,160]{2,1,0:T(8,128)(2,1)}), bf16[8,80,160]{2,1,0:T(8,128)(2,1)}, u32[]{:S(2)}, u32[]{:S(2)}) async-start(bf16[8,80,160]{2,1,0:T(8,128)(2,1)} %get-tuple-element.38), calls=%async_computation.4 | async-start | bytes 655360 | tf_op jit(solution)/shard_map/all_to_all | solution.py:33
  200.6 4.4 %all-to-all-done.4 = bf16[8,80,160]{2,1,0:T(8,128)(2,1)} async-done(((bf16[8,80,160]{2,1,0:T(8,128)(2,1)}), bf16[8,80,160]{2,1,0:T(8,128)(2,1)}, u32[]{:S(2)}, u32[]{:S(2)}) %all-to-all-start.4) | async-done | bytes 204832 | tf_op jit(solution)/shard_map/all_to_all | solution.py:33
  205.1 6.9 %all-to-all-start.6 = ((bf16[8,40,768]{2,1,0:T(8,128)(2,1)}), bf16[8,40,768]{2,1,0:T(8,128)(2,1)}, u32[]{:S(2)}, u32[]{:S(2)}) async-start(bf16[8,40,768]{2,1,0:T(8,128)(2,1)} %fusion.7), calls=%async_computation.6 | async-start | bytes 983040 | tf_op jit(solution)/shard_map/all_to_all | solution.py:33
  214.6 13.9 %all-to-all-done.6 = bf16[8,40,768]{2,1,0:T(8,128)(2,1)} async-done(((bf16[8,40,768]{2,1,0:T(8,128)(2,1)}), bf16[8,40,768]{2,1,0:T(8,128)(2,1)}, u32[]{:S(2)}, u32[]{:S(2)}) %all-to-all-start.6) | async-done | bytes 491552 | tf_op jit(solution)/shard_map/all_to_all | solution.py:33
  (96 shorter events, 61.5 us)
Async XLA Ops:
  10.6 17.4 %all-to-all-start = ((bf16[4,80,1280]{2,1,0:T(8,128)(2,1)}), bf16[4,80,1280]{2,1,0:T(8,128)(2,1)S(1)}, u32[]{:S(2)}, u32[]{:S(2)}) async-start(bf16[4,80,1280]{2,1,0:T(8,128)(2,1)} %bitcast.9), calls=%async_computation | async-start | bytes 1638400 | tf_op jit(solution)/shard_map/all_to_all | solution.py:33
  30.9 23.9 %all-to-all-start.1 = ((bf16[32,5,8,128]{3,2,1,0:T(8,128)(2,1)}), bf16[32,5,8,128]{3,2,1,0:T(8,128)(2,1)S(1)}, u32[]{:S(2)}, u32[]{:S(2)}) async-start(bf16[32,5,8,128]{3,2,1,0:T(8,128)(2,1)} %spread.1), calls=%async_computation.1 | async-start | bytes 655360 | tf_op jit(solution)/shard_map/all_to_all | solution.py:33
  57.5 17.2 %all-to-all-start.2 = ((bf16[32,5,8,128]{3,2,1,0:T(8,128)(2,1)}), bf16[32,5,8,128]{3,2,1,0:T(8,128)(2,1)S(1)}, u32[]{:S(2)}, u32[]{:S(2)}) async-start(bf16[32,5,8,128]{3,2,1,0:T(8,128)(2,1)} %bitcast.81), calls=%async_computation.2 | async-start | bytes 655360 | tf_op jit(solution)/shard_map/all_to_all | solution.py:33
  61.4 10.2 %collective-permute-start.4 = (bf16[160,640]{1,0:T(8,128)(2,1)S(1)}, bf16[160,640]{1,0:T(8,128)(2,1)S(1)}, u32[]{:S(2)}, u32[]{:S(2)}) collective-permute-start(bf16[160,640]{1,0:T(8,128)(2,1)S(1)} %bitcast.90), channel_id=1, source_target_pairs={{0,6},{2,0},{4,2},{6,4},{1,7},{3,1},{5,3},{7,5},{8,14},{10,8},{12,... | collective-permute-start | bytes 614408 | tf_op jit(solution)/shard_map/ppermute | solution.py:38
  63.1 10.1 %collective-permute-start.2 = (bf16[160,640]{1,0:T(8,128)(2,1)S(1)}, bf16[160,640]{1,0:T(8,128)(2,1)S(1)}, u32[]{:S(2)}, u32[]{:S(2)}) collective-permute-start(bf16[160,640]{1,0:T(8,128)(2,1)S(1)} %bitcast.92), channel_id=1, source_target_pairs={{0,2},{2,4},{4,6},{6,0},{1,3},{3,5},{5,7},{7,1},{8,10},{10,12},{12... | collective-permute-start | bytes 614408 | tf_op jit(solution)/shard_map/ppermute | solution.py:38
  74.3 20.4 %collective-permute-start.5 = (bf16[4,160,640]{2,1,0:T(8,128)(2,1)}, bf16[4,160,640]{2,1,0:T(8,128)(2,1)}, u32[]{:S(2)}, u32[]{:S(2)}) collective-permute-start(bf16[4,160,640]{2,1,0:T(8,128)(2,1)} %pad_maximum_fusion.own_ref), channel_id=1, source_target_pairs={{0,1},{1,0},{2,3},{3,2},{4,5},{5,4},{6,7},{7,6},{8,9},{9,8},{10,11... | collective-permute-start | bytes 2457608 | tf_op jit(solution)/shard_map/ppermute | solution.py:42
  77.5 17.2 %all-to-all-start.3 = ((bf16[4,80,1280]{2,1,0:T(8,128)(2,1)}), bf16[4,80,1280]{2,1,0:T(8,128)(2,1)S(1)}, u32[]{:S(2)}, u32[]{:S(2)}) async-start(bf16[4,80,1280]{2,1,0:T(8,128)(2,1)} %bitcast.86), calls=%async_computation.3 | async-start | bytes 1638400 | tf_op jit(solution)/shard_map/all_to_all | solution.py:33
  94.7 11.7 %collective-permute-start.1 = (bf16[4,5,16,1280]{3,2,1,0:T(8,128)(2,1)S(1)}, bf16[4,5,16,1280]{3,2,1,0:T(8,128)(2,1)}, u32[]{:S(2)}, u32[]{:S(2)}) collective-permute-start(bf16[4,5,16,1280]{3,2,1,0:T(8,128)(2,1)S(1)} %bitcast.84), channel_id=1, source_target_pairs={{0,1},{1,0},{2,3},{3,2},{4,5},{5,4},{6,7},{7,6},{8,9},{9,8},{10,11... | collective-permute-start | bytes 2457608 | tf_op jit(solution)/shard_map/ppermute | solution.py:42
  113.6 45.4 %collective-permute-start.6 = (bf16[4,6,16,1280]{3,2,1,0:T(8,128)(2,1)}, bf16[4,6,16,1280]{3,2,1,0:T(8,128)(2,1)}, u32[]{:S(2)}, u32[]{:S(2)}) collective-permute-start(bf16[4,6,16,1280]{3,2,1,0:T(8,128)(2,1)} %get-tuple-element.35), channel_id=1, source_target_pairs={{0,1},{1,0},{2,3},{3,2},{4,5},{5,4},{6,7},{7,6},{8,9},{9,8},{10,11... | collective-permute-start | bytes 2949128 | tf_op jit(solution)/shard_map/ppermute | solution.py:42
  116.7 19.4 %collective-permute-start.10 = (bf16[8,40,1024]{2,1,0:T(8,128)(2,1)}, bf16[8,40,1024]{2,1,0:T(8,128)(2,1)S(1)}, u32[]{:S(2)}, u32[]{:S(2)}) collective-permute-start(bf16[8,40,1024]{2,1,0:T(8,128)(2,1)} %get-tuple-element.61), channel_id=1, source_target_pairs={{0,16},{8,24},{16,0},{24,8},{1,17},{9,25},{17,1},{25,9},{2,18},{10... | collective-permute-start | bytes 1966088 | tf_op jit(solution)/shard_map/ppermute | solution.py:38
  119.7 29.8 %collective-permute-start.12 = (bf16[8,40,1024]{2,1,0:T(8,128)(2,1)}, bf16[8,40,1024]{2,1,0:T(8,128)(2,1)}, u32[]{:S(2)}, u32[]{:S(2)}) collective-permute-start(bf16[8,40,1024]{2,1,0:T(8,128)(2,1)} %get-tuple-element.62), channel_id=1, source_target_pairs={{0,24},{8,0},{16,8},{24,16},{1,25},{9,1},{17,9},{25,17},{2,26},{10... | collective-permute-start | bytes 1966088 | tf_op jit(solution)/shard_map/ppermute | solution.py:38
  120.8 28.7 %collective-permute-start.11 = (bf16[8,40,1024]{2,1,0:T(8,128)(2,1)}, bf16[8,40,1024]{2,1,0:T(8,128)(2,1)}, u32[]{:S(2)}, u32[]{:S(2)}) collective-permute-start(bf16[8,40,1024]{2,1,0:T(8,128)(2,1)} %get-tuple-element.63), channel_id=1, source_target_pairs={{0,8},{8,16},{16,24},{24,0},{1,9},{9,17},{17,25},{25,1},{2,10},{10... | collective-permute-start | bytes 1966088 | tf_op jit(solution)/shard_map/ppermute | solution.py:38
  152.3 42.2 %all-to-all-start.5 = ((bf16[8,40,1024]{2,1,0:T(8,128)(2,1)}), bf16[8,40,1024]{2,1,0:T(8,128)(2,1)S(1)}, u32[]{:S(2)}, u32[]{:S(2)}) async-start(bf16[8,40,1024]{2,1,0:T(8,128)(2,1)} %fusion.4), calls=%async_computation.5 | async-start | bytes 1310720 | tf_op jit(solution)/shard_map/all_to_all | solution.py:33
  161.7 13.0 %collective-permute-start.9 = (bf16[6,16,1280]{2,1,0:T(8,128)(2,1)}, bf16[6,16,1280]{2,1,0:T(8,128)(2,1)S(1)}, u32[]{:S(2)}, u32[]{:S(2)}) collective-permute-start(bf16[6,16,1280]{2,1,0:T(8,128)(2,1)} %get-tuple-element.64), channel_id=1, source_target_pairs={{0,6},{2,0},{4,2},{6,4},{1,7},{3,1},{5,3},{7,5},{8,14},{10,8},{12,... | collective-permute-start | bytes 737288 | tf_op jit(solution)/shard_map/ppermute | solution.py:38
  163.1 14.3 %collective-permute-start.8 = (bf16[6,16,1280]{2,1,0:T(8,128)(2,1)}, bf16[6,16,1280]{2,1,0:T(8,128)(2,1)}, u32[]{:S(2)}, u32[]{:S(2)}) collective-permute-start(bf16[6,16,1280]{2,1,0:T(8,128)(2,1)} %get-tuple-element.65), channel_id=1, source_target_pairs={{0,2},{2,4},{4,6},{6,0},{1,3},{3,5},{5,7},{7,1},{8,10},{10,12},{12... | collective-permute-start | bytes 737288 | tf_op jit(solution)/shard_map/ppermute | solution.py:38
  163.7 13.7 %collective-permute-start.7 = (bf16[6,16,1280]{2,1,0:T(8,128)(2,1)}, bf16[6,16,1280]{2,1,0:T(8,128)(2,1)}, u32[]{:S(2)}, u32[]{:S(2)}) collective-permute-start(bf16[6,16,1280]{2,1,0:T(8,128)(2,1)} %get-tuple-element.66), channel_id=1, source_target_pairs={{0,4},{2,6},{4,0},{6,2},{1,5},{3,7},{5,1},{7,3},{8,12},{10,14},{12... | collective-permute-start | bytes 737288 | tf_op jit(solution)/shard_map/ppermute | solution.py:38
  171.2 14.2 %collective-permute-start.13 = (bf16[8,40,640]{2,1,0:T(8,128)(2,1)}, bf16[8,40,640]{2,1,0:T(8,128)(2,1)}, u32[]{:S(2)}, u32[]{:S(2)}) collective-permute-start(bf16[8,40,640]{2,1,0:T(8,128)(2,1)} %get-tuple-element.45), channel_id=1, source_target_pairs={{0,16},{8,24},{16,0},{24,8},{1,17},{9,25},{17,1},{25,9},{2,18},{10... | collective-permute-start | bytes 1228808 | tf_op jit(solution)/shard_map/ppermute | solution.py:38
  174.2 17.9 %collective-permute-start.14 = (bf16[8,40,640]{2,1,0:T(8,128)(2,1)}, bf16[8,40,640]{2,1,0:T(8,128)(2,1)}, u32[]{:S(2)}, u32[]{:S(2)}) collective-permute-start(bf16[8,40,640]{2,1,0:T(8,128)(2,1)} %get-tuple-element.46), channel_id=1, source_target_pairs={{0,8},{8,16},{16,24},{24,0},{1,9},{9,17},{17,25},{25,1},{2,10},{10... | collective-permute-start | bytes 1228808 | tf_op jit(solution)/shard_map/ppermute | solution.py:38
  174.7 17.4 %collective-permute-start.15 = (bf16[8,40,640]{2,1,0:T(8,128)(2,1)}, bf16[8,40,640]{2,1,0:T(8,128)(2,1)}, u32[]{:S(2)}, u32[]{:S(2)}) collective-permute-start(bf16[8,40,640]{2,1,0:T(8,128)(2,1)} %get-tuple-element.47), channel_id=1, source_target_pairs={{0,24},{8,0},{16,8},{24,16},{1,25},{9,1},{17,9},{25,17},{2,26},{10... | collective-permute-start | bytes 1228808 | tf_op jit(solution)/shard_map/ppermute | solution.py:38
  181.1 17.4 %collective-permute-start.16 = (bf16[1,320]{1,0:T(2,128)(2,1)S(1)}, bf16[1,320]{1,0:T(2,128)(2,1)S(1)}, u32[]{:S(2)}, u32[]{:S(2)}) collective-permute-start(bf16[1,320]{1,0:T(2,128)(2,1)S(1)} %get-tuple-element.70), channel_id=1, source_target_pairs={{0,16},{8,24},{16,0},{24,8},{1,17},{9,25},{17,1},{25,9},{2,18},{10... | collective-permute-start | bytes 1928 | tf_op jit(solution)/shard_map/ppermute | solution.py:38
  182.2 16.4 %collective-permute-start.18 = (bf16[1,320]{1,0:T(2,128)(2,1)S(1)}, bf16[1,320]{1,0:T(2,128)(2,1)S(1)}, u32[]{:S(2)}, u32[]{:S(2)}) collective-permute-start(bf16[1,320]{1,0:T(2,128)(2,1)S(1)} %get-tuple-element.71), channel_id=1, source_target_pairs={{0,24},{8,0},{16,8},{24,16},{1,25},{9,1},{17,9},{25,17},{2,26},{10... | collective-permute-start | bytes 1928 | tf_op jit(solution)/shard_map/ppermute | solution.py:38
  185.4 13.1 %collective-permute-start.17 = (bf16[1,320]{1,0:T(2,128)(2,1)S(1)}, bf16[1,320]{1,0:T(2,128)(2,1)S(1)}, u32[]{:S(2)}, u32[]{:S(2)}) collective-permute-start(bf16[1,320]{1,0:T(2,128)(2,1)S(1)} %get-tuple-element.72), channel_id=1, source_target_pairs={{0,8},{8,16},{16,24},{24,0},{1,9},{9,17},{17,25},{25,1},{2,10},{10... | collective-permute-start | bytes 1928 | tf_op jit(solution)/shard_map/ppermute | solution.py:38
  194.5 10.6 %all-to-all-start.4 = ((bf16[8,80,160]{2,1,0:T(8,128)(2,1)}), bf16[8,80,160]{2,1,0:T(8,128)(2,1)}, u32[]{:S(2)}, u32[]{:S(2)}) async-start(bf16[8,80,160]{2,1,0:T(8,128)(2,1)} %get-tuple-element.38), calls=%async_computation.4 | async-start | bytes 655360 | tf_op jit(solution)/shard_map/all_to_all | solution.py:33
  205.1 23.4 %all-to-all-start.6 = ((bf16[8,40,768]{2,1,0:T(8,128)(2,1)}), bf16[8,40,768]{2,1,0:T(8,128)(2,1)}, u32[]{:S(2)}, u32[]{:S(2)}) async-start(bf16[8,40,768]{2,1,0:T(8,128)(2,1)} %fusion.7), calls=%async_computation.6 | async-start | bytes 983040 | tf_op jit(solution)/shard_map/all_to_all | solution.py:33
  (13 other events, 102.9 us)
